TPU v7x, 32 devices: a whole 2x2x4 slice. The times are simulated.
32 devices in a mesh: gx: 4 (over z), gy: 8 (over y, x, core).
Axes of the slice: x: 2, y: 2, z: 4, core: 2. Of those that a mesh axis runs over, the one named last changes fastest.
Arguments:
- conductivity: float32 [128, 32768], P(('gx', 'gy')), may hold values from 0.5 to 2
- owner_rank: int32 [8192, 1], P(('gx', 'gy')), may hold values from 0 to 31; in each aligned block of 256 rows (0 to 255, 256 to 511, ...) at most 17 rows name the same one
- tile_slot: int32 [8192], P(('gx', 'gy')), may hold values from 0 to 3
- offsets: int32 [3, 8192], P(None, ('gx', 'gy')), may hold values from 0 to 30
- fractions: float32 [3, 8192], P(None, ('gx', 'gy')), may hold values from 0 to 1
- source: float32 [8192], P(('gx', 'gy')), may hold values from -1.5 to 1.5
- observed: float32 [8192], P(('gx', 'gy')), may hold values from -3 to 3
- live_count: int32 [32], P(('gx', 'gy')), may hold values from 1 to 256, 6144 in all
- fourier: float32 [128, 3], replicated, may hold values from -1.5 to 1.5
- weights: float32 [6, 256, 256], replicated, may hold values from -0.375 to 0.375
- biases: float32 [6, 256], replicated, may hold values from -3 to 3
- readout: float32 [256], replicated, may hold values from -0.375 to 0.375
Outputs:
- conductivity_grad: float32 [128, 32768], P(('gx', 'gy'))
- weight_grad: float32 [6, 256, 256], replicated
- bias_grad: float32 [6, 256], replicated
- readout_grad: float32 [256], replicated
- losses: float32 [3], replicated
Inputs may be any that keep to these rules, and one draw needn't show every extreme that they name: `owner_rank`: among the rows of one device at most 17 name the same owner, and that number is reached in some device's rows. `live_count`: they sum to 6144, and some device has all 256 points live.
All inputs are finite; a program needn't handle non-finite values.
Results may differ from a plain program's by a relative error of at most 0.0003.
Values sent between devices are 32-bit elements; how exact they have to be, the bound alone decides.
No kernel may reach another device: no remote copies, remote signals or barrier semaphores. Data moves between devices by JAX's collectives and lax.ppermute only.
A program may use at most 128 MiB of HBM per device.

v0:
```python
import jax
import jax.numpy as jnp
from jax import lax
from jax.sharding import PartitionSpec as P

TILE_SIDE = 32
LAYERS = 6


data_weight = 1.0
smooth_weight = 0.05
highest = lax.Precision.HIGHEST


def padded_2(value, sides, width):
    for axis, dim in sides:
        size, length = (lax.axis_size(axis), value.shape[dim])
        up = [(i, (i + 1) % size) for i in range(size - 1)]
        down = [(j, i) for i, j in up]
        last = lax.slice_in_dim(value, length - width, length, axis=dim)
        initial = lax.slice_in_dim(value, 0, width, axis=dim)
        before = lax.ppermute(last, axis, up)
        after = lax.ppermute(initial, axis, down)
        value = jnp.concatenate([before, value, after], axis=dim)
    return value


def encode(fourier, position):
    phases = (
        fourier[:, 0:1] * position[0][None, :]
        + fourier[:, 1:2] * position[1][None, :]
        + fourier[:, 2:3] * position[2][None, :]
    )
    sin_part = jnp.sin(phases)
    cos_part = jnp.cos(phases)
    squared = jnp.sum(fourier * fourier, axis=1, keepdims=True)
    streams = [jnp.concatenate([sin_part, cos_part], axis=0)]
    for column in range(3):
        column_rate = fourier[:, column : column + 1]
        streams.append(jnp.concatenate([cos_part * column_rate, -sin_part * column_rate], axis=0))
    streams.append(jnp.concatenate([-sin_part * squared, -cos_part * squared], axis=0))
    return jnp.stack(streams)


def hidden_layer(weight, bias_row, streams):
    projected = jnp.einsum("oi,sip->sop", weight, streams, precision=highest)
    values = jnp.tanh(projected[0] + bias_row[:, None])
    slopes = 1.0 - values * values
    gradient_part = slopes[None] * projected[1:4]
    curvature = slopes * projected[4] - 2.0 * values * slopes * jnp.sum(
        projected[1:4] * projected[1:4], axis=0
    )
    return jnp.concatenate([values[None], gradient_part, curvature[None]], axis=0)


def readout_map(readout, streams):
    return jnp.einsum("i,sip->sp", readout, streams, precision=highest)


def interpolate(flat_field, cell_index, fractions):
    lower_weight = 1.0 - fractions
    value_sum = jnp.zeros_like(fractions[0])
    first_sum = jnp.zeros_like(fractions[0])
    second_sum = jnp.zeros_like(fractions[0])
    third_sum = jnp.zeros_like(fractions[0])
    for along_x in (0, 1):
        for along_y in (0, 1):
            for along_z in (0, 1):
                shift_cells = (along_x * TILE_SIDE + along_y) * TILE_SIDE + along_z
                corner = flat_field[cell_index + shift_cells]
                weight_first = fractions[0] if along_x else lower_weight[0]
                weight_second = fractions[1] if along_y else lower_weight[1]
                weight_third = fractions[2] if along_z else lower_weight[2]
                sign_first = 1.0 if along_x else -1.0
                sign_second = 1.0 if along_y else -1.0
                sign_third = 1.0 if along_z else -1.0
                value_sum = value_sum + weight_first * weight_second * weight_third * corner
                first_sum = first_sum + sign_first * weight_second * weight_third * corner
                second_sum = second_sum + weight_first * sign_second * weight_third * corner
                third_sum = third_sum + weight_first * weight_second * sign_third * corner
    return jnp.stack([value_sum, first_sum, second_sum, third_sum])


def spread(size, cell_index, fractions, gradient_rows):
    lower_weight = 1.0 - fractions
    accumulated = jnp.zeros((size,), gradient_rows.dtype)
    for along_x in (0, 1):
        for along_y in (0, 1):
            for along_z in (0, 1):
                shift_cells = (along_x * TILE_SIDE + along_y) * TILE_SIDE + along_z
                weight_first = fractions[0] if along_x else lower_weight[0]
                weight_second = fractions[1] if along_y else lower_weight[1]
                weight_third = fractions[2] if along_z else lower_weight[2]
                sign_first = 1.0 if along_x else -1.0
                sign_second = 1.0 if along_y else -1.0
                sign_third = 1.0 if along_z else -1.0
                contribution = (
                    gradient_rows[0] * weight_first * weight_second * weight_third
                    + gradient_rows[1] * sign_first * weight_second * weight_third
                    + gradient_rows[2] * weight_first * sign_second * weight_third
                    + gradient_rows[3] * weight_first * weight_second * sign_third
                )
                accumulated = accumulated.at[cell_index + shift_cells].add(contribution)
    return accumulated


def route_slots(owner_device, devices, capacity):
    point_count = owner_device.shape[0]
    targets = lax.broadcasted_iota(jnp.int32, (point_count, devices), 1)
    onehot = (owner_device[:, None] == targets).astype(jnp.bfloat16)
    row_order = lax.broadcasted_iota(jnp.int32, (point_count, point_count), 0)
    column_order = lax.broadcasted_iota(jnp.int32, (point_count, point_count), 1)
    earlier = (column_order < row_order).astype(jnp.bfloat16)
    before = jnp.dot(earlier, onehot, preferred_element_type=jnp.float32)
    slot_rank = jnp.sum(before * onehot.astype(jnp.float32), axis=1).astype(jnp.int32)
    return owner_device * capacity + slot_rank


def pack_rows(row_data, slot_index, devices, capacity):
    columns = row_data.shape[1]
    buffer = jnp.zeros((devices * capacity, columns), jnp.float32).at[slot_index].set(row_data)
    return buffer.reshape(devices, capacity, columns)


def unpack_rows(buffer, slot_index):
    return buffer.reshape(-1, buffer.shape[2])[slot_index]


def smooth_local(conductivity):
    tile_side = TILE_SIDE
    block_grid = conductivity.reshape(-1, tile_side, tile_side)
    padded = padded_2(block_grid, ((("gx", "gy"), 1),), 1)
    device_index = lax.axis_index(("gx", "gy"))
    devices = lax.axis_size(("gx", "gy"))
    lower_edge = (device_index > 0).astype(jnp.float32)
    upper_edge = (device_index < devices - 1).astype(jnp.float32)
    edge_mask = jnp.concatenate(
        [lower_edge[None], jnp.ones((tile_side - 1,), jnp.float32), upper_edge[None]]
    )
    across = (padded[:, 1:, :] - padded[:, :-1, :]) * edge_mask[None, :, None]
    energy = jnp.sum(across[:, :tile_side, :] * across[:, :tile_side, :])
    gradient = across[:, :tile_side, :] - across[:, 1:, :]
    for direction in (0, 2):
        difference = jnp.diff(block_grid, axis=direction)
        energy = energy + jnp.sum(difference * difference)
        pad_before = [(0, 0), (0, 0), (0, 0)]
        pad_after = [(0, 0), (0, 0), (0, 0)]
        pad_before[direction] = (1, 0)
        pad_after[direction] = (0, 1)
        gradient = gradient + jnp.pad(difference, pad_before) - jnp.pad(difference, pad_after)
    return (energy, 2.0 * smooth_weight * gradient)


def on_device(
    conductivity,
    owner_rank,
    tile_slot,
    offsets,
    fractions,
    source,
    observed,
    live_count,
    fourier,
    weights,
    biases,
    readout,
):
    devices = lax.axis_size(("gx", "gy"))
    point_count = tile_slot.shape[0]
    capacity = (2 * point_count + devices - 1) // devices + 1
    tile_cells = TILE_SIDE**3
    owner_device = owner_rank[:, 0]
    local_cell = (
        tile_slot * tile_cells + (offsets[0] * TILE_SIDE + offsets[1]) * TILE_SIDE + offsets[2]
    )
    position = (
        jnp.stack(
            [TILE_SIDE * tile_slot + offsets[0], TILE_SIDE * owner_device + offsets[1], offsets[2]]
        ).astype(jnp.float32)
        + fractions
    )
    live_mask = (lax.broadcasted_iota(jnp.int32, (point_count,), 0) < live_count[0]).astype(
        jnp.float32
    )
    slot_index = route_slots(owner_device, devices, capacity)
    flat_field = conductivity.reshape(-1)
    request_rows = jnp.concatenate([local_cell.astype(jnp.float32)[None], fractions], axis=0)
    streams = encode(fourier, position)
    pull_backs = []
    for layer_depth in range(LAYERS):
        streams, pull_back = jax.vjp(
            hidden_layer, weights[layer_depth], biases[layer_depth], streams
        )
        pull_backs.append(pull_back)
    outputs, readout_pull = jax.vjp(readout_map, readout, streams)
    misfit = outputs[0] - observed
    misfit_sum = jnp.sum(live_mask * misfit * misfit)
    misfit_grad = 2.0 * data_weight * live_mask * misfit
    received = lax.all_to_all(
        pack_rows(request_rows.T, slot_index, devices, capacity),
        ("gx", "gy"),
        split_axis=0,
        concat_axis=0,
        tiled=True,
    )
    arrived = received.reshape(-1, 4).T
    arrived_cells = arrived[0].astype(jnp.int32)
    looked = interpolate(flat_field, arrived_cells, arrived[1:4])
    returned = lax.all_to_all(
        looked.T.reshape(devices, capacity, 4),
        ("gx", "gy"),
        split_axis=0,
        concat_axis=0,
        tiled=True,
    )
    point_values = unpack_rows(returned, slot_index).T
    residual = (
        -(point_values[0] * outputs[4] + jnp.sum(point_values[1:4] * outputs[1:4], axis=0)) - source
    )
    residual_sum = jnp.sum(live_mask * residual * residual)
    scaled = 2.0 * live_mask * residual
    output_grad = jnp.stack(
        [
            misfit_grad,
            -scaled * point_values[1],
            -scaled * point_values[2],
            -scaled * point_values[3],
            -scaled * point_values[0],
        ]
    )
    value_grad = jnp.stack(
        [-scaled * outputs[4], -scaled * outputs[1], -scaled * outputs[2], -scaled * outputs[3]]
    )
    owed_grads = lax.all_to_all(
        pack_rows(value_grad.T, slot_index, devices, capacity),
        ("gx", "gy"),
        split_axis=0,
        concat_axis=0,
        tiled=True,
    )
    field_part = spread(
        flat_field.shape[0], arrived_cells, arrived[1:4], owed_grads.reshape(-1, 4).T
    )
    readout_part, stream_grad = readout_pull(output_grad)
    energy, smooth_grad = smooth_local(conductivity)
    local_sums = jnp.stack([residual_sum, misfit_sum, live_count[0].astype(jnp.float32), energy])
    totals, readout_total = lax.psum((local_sums, readout_part), ("gx", "gy"))
    live_total = totals[2]
    weight_parts = []
    bias_parts = []
    for layer_depth in reversed(range(LAYERS)):
        weight_part, bias_part, stream_grad = pull_backs[layer_depth](stream_grad)
        weight_parts.insert(0, weight_part)
        bias_parts.insert(0, bias_part)
    weight_total, bias_total = lax.psum(
        (jnp.stack(weight_parts), jnp.stack(bias_parts)), ("gx", "gy")
    )
    cells_total = devices * flat_field.shape[0]
    losses = jnp.stack([totals[0] / live_total, totals[1] / live_total, totals[3] / cells_total])
    conductivity_grad = (field_part + smooth_grad.reshape(-1)).reshape(conductivity.shape)
    return (
        conductivity_grad,
        weight_total / live_total,
        bias_total / live_total,
        readout_total / live_total,
        losses,
    )


def solution(mesh):
    in_specs = (
        P(("gx", "gy"), None),
        P(("gx", "gy"), None),
        P(("gx", "gy")),
        P(None, ("gx", "gy")),
        P(None, ("gx", "gy")),
        P(("gx", "gy")),
        P(("gx", "gy")),
        P(("gx", "gy")),
        P(),
        P(),
        P(),
        P(),
    )
    out_specs = (P(("gx", "gy"), None), P(), P(), P(), P())
    return jax.shard_map(
        on_device, mesh=mesh, in_specs=in_specs, out_specs=out_specs, check_vma=False
    )
```

profile of v0, /device:TPU:0, one launch (start us, length us, event | category | flops | bytes accessed | tf_op | source)
XLA Modules:
  0.0 329.3 jit_solution(10373270310764862623)
XLA Ops:
  11.2 1.2 scatter_custom_fusion
  13.3 7.5 %all-to-all-start = ((f32[32,17,4]{1,2,0:T(4,128)}), f32[32,17,4]{1,2,0:T(4,128)}, u32[]{:S(2)}, u32[]{:S(2)}) async-start(f32[32,17,4]{1,2,0:T(4,128)} %copy.78), calls=%async_computation | async-start | bytes 131072 | tf_op jit(solution)/shard_map/all_to_all | solution.py:199
  22.3 2.7 collective-permute-start.1
  25.0 1.5 collective-permute-start
  27.1 2.4 multiply_reduce_fusion.2
  29.5 2.6 multiply_reduce_fusion
  33.7 1.3 copy-done.15
  34.9 1.2 convolution_bitcast_fusion.10
  37.4 1.2 convolution_bitcast_fusion.9
  40.0 1.2 convolution_bitcast_fusion.8
  42.5 1.2 convolution_bitcast_fusion.7
  45.0 1.2 convolution_bitcast_fusion.6
  47.6 1.2 convolution_bitcast_fusion.5
  50.7 1.6 fusion.69
  52.4 1.0 slice_reduce_fusion.3
  53.4 1.2 fusion.194
  54.7 1.1 copy.113
  55.8 2.9 fusion
  60.4 5.2 %gather_fusion.7 = f32[544]{0:T(1024)} fusion(f32[131072]{0:T(1024)S(1)} %bitcast.530, s32[1024]{0:T(1024)S(1)} %get-tuple-element.168), kind=kCustom, calls=%fused_computation.7 | custom fusion | bytes 6528 | tf_op jit(solution)/shard_map/gather | solution.py:70
  65.6 5.2 %gather_fusion.6 = f32[544]{0:T(1024)} fusion(f32[131072]{0:T(1024)S(1)} %bitcast.531, s32[1024]{0:T(1024)S(1)} %get-tuple-element.169), kind=kCustom, calls=%fused_computation.6 | custom fusion | bytes 6528 | tf_op jit(solution)/shard_map/gather | solution.py:70
  70.9 5.2 %gather_fusion.5 = f32[544]{0:T(1024)} fusion(f32[131072]{0:T(1024)S(1)} %bitcast.532, s32[1024]{0:T(1024)S(1)} %get-tuple-element.170), kind=kCustom, calls=%fused_computation.5 | custom fusion | bytes 6528 | tf_op jit(solution)/shard_map/gather | solution.py:70
  76.1 5.2 %gather_fusion.4 = f32[544]{0:T(1024)} fusion(f32[131072]{0:T(1024)S(1)} %bitcast.533, s32[1024]{0:T(1024)S(1)} %get-tuple-element.171), kind=kCustom, calls=%fused_computation.4 | custom fusion | bytes 6528 | tf_op jit(solution)/shard_map/gather | solution.py:70
  81.3 5.2 %gather_fusion.3 = f32[544]{0:T(1024)} fusion(f32[131072]{0:T(1024)S(1)} %bitcast.534, s32[1024]{0:T(1024)S(1)} %get-tuple-element.172), kind=kCustom, calls=%fused_computation.3 | custom fusion | bytes 6528 | tf_op jit(solution)/shard_map/gather | solution.py:70
  86.5 5.2 %gather_fusion.2 = f32[544]{0:T(1024)} fusion(f32[131072]{0:T(1024)S(1)} %bitcast.535, s32[1024]{0:T(1024)S(1)} %get-tuple-element.173), kind=kCustom, calls=%fused_computation.2 | custom fusion | bytes 6528 | tf_op jit(solution)/shard_map/gather | solution.py:70
  92.3 5.2 %gather_fusion.1 = f32[544]{0:T(1024)} fusion(f32[131072]{0:T(1024)S(1)} %bitcast.536, s32[1024]{0:T(1024)S(1)} %get-tuple-element.174), kind=kCustom, calls=%fused_computation.1 | custom fusion | bytes 6528 | tf_op jit(solution)/shard_map/gather | solution.py:70
  97.5 5.5 %gather_fusion = f32[544]{0:T(1024)} fusion(f32[131072]{0:T(1024)S(1)} %bitcast.537, s32[1024]{0:T(1024)} %get-tuple-element.175), kind=kCustom, calls=%fused_computation | custom fusion | bytes 6528 | tf_op jit(solution)/shard_map/gather | solution.py:70
  105.6 7.5 %all-to-all-start.1 = ((f32[32,17,4]{1,2,0:T(4,128)}), f32[32,17,4]{1,2,0:T(4,128)}, u32[]{:S(2)}, u32[]{:S(2)}) async-start(f32[32,17,4]{1,2,0:T(4,128)} %copy.80), calls=%async_computation.1 | async-start | bytes 131072 | tf_op jit(solution)/shard_map/all_to_all | solution.py:209
  113.0 6.6 %multiply_reduce_fusion.1 = (f32[]{:T(128)}, f32[128,32,32]{2,1,0:T(8,128)}) fusion(f32[128,33,32]{2,1,0:T(8,128)S(1)} %copy-done.12, f32[128,32,31]{2,1,0:T(8,128)} %get-tuple-element.42, f32[127,32,32]{2,1,0:T(8,128)} %get-tuple-element.44), kind=kLoop, calls=%fused_computation.29 | loop fusion | flops 1048575 | bytes 2600964 | tf_op jit(solution)/shard_map/reduce_sum | solution.py:141
  119.7 2.0 reshape.512
  129.3 1.8 copy-done.16
  131.1 1.2 convolution_bitcast_fusion.4
  135.5 1.2 convolution_bitcast_fusion.3
  139.8 1.2 convolution_bitcast_fusion.2
  144.2 1.2 convolution_bitcast_fusion.1
  147.6 1.2 convolution_bitcast_fusion
  149.3 1.0 slice_multiply_fusion
  150.3 1.5 fusion.77
  151.8 1.0 fusion.156
  153.2 1.4 fusion.68
  154.7 2.1 scatter_custom_fusion.1
  156.8 1.1 copy.84
  158.7 5.8 %all-to-all-start.2 = ((f32[32,17,4]{1,2,0:T(4,128)}), f32[32,17,4]{1,2,0:T(4,128)S(1)}, u32[]{:S(2)}, u32[]{:S(2)}) async-start(f32[32,17,4]{1,2,0:T(4,128)} %copy.85), calls=%async_computation.2 | async-start | bytes 131072 | tf_op jit(solution)/shard_map/all_to_all | solution.py:234
  164.5 1.1 slice_multiply_fusion.16
  165.9 3.0 fusion.64
  169.0 3.0 fusion.58
  172.0 3.0 fusion.52
  175.1 3.0 fusion.46
  178.2 3.0 fusion.40
  181.3 3.2 fusion.34
  184.5 1.4 pad_maximum_fusion.19
  186.0 40.8 %all-reduce.28 = (f32[4]{0:T(128)S(1)}, f32[6,256]{1,0:T(8,128)S(1)}, f32[256]{0:T(256)S(1)}) all-reduce(f32[4]{0:T(128)S(1)} %pad_maximum_fusion.19, f32[6,256]{1,0:T(8,128)S(1)} %stack.170, f32[256]{0:T(256)S(1)} %bitcast.590), channel_id=1, replica_groups=mesh['gx'=4,'gy'=8] {'gx','gy'}, use_global_device_ids=true, to_apply=%region_31.32 | all-reduce | flops 1796 | bytes 14368 | tf_op jit(solution)/shard_map/psum | solution.py:247
  227.5 1.3 broadcast_divide_fusion.1
  228.7 1.2 broadcast_divide_fusion.2
  234.1 5.1 %scatter_fusion = f32[131072]{0:T(1024)S(1)} fusion(f32[131072]{0:T(1024)S(1)} %reshape.512, s32[544]{0:T(1024)S(1)} %copy-done.137, f32[544]{0:T(1024)S(1)} %get-tuple-element.121), kind=kCustom, calls=%fused_computation.11 | custom fusion | flops 544 | bytes 8704 | tf_op jit(solution)/shard_map/scatter-add | solution.py:103
  239.3 5.1 %scatter_fusion.1 = f32[131072]{0:T(1024)S(1)} fusion(f32[131072]{0:T(1024)S(1)} %scatter_fusion, s32[544]{0:T(1024)S(1)} %copy-done.135, f32[544]{0:T(1024)S(1)} %get-tuple-element.122), kind=kCustom, calls=%fused_computation.12 | custom fusion | flops 544 | bytes 8704 | tf_op jit(solution)/shard_map/scatter-add | solution.py:103
  244.4 5.1 %scatter_fusion.2 = f32[131072]{0:T(1024)S(1)} fusion(f32[131072]{0:T(1024)S(1)} %scatter_fusion.1, s32[544]{0:T(1024)S(1)} %copy-done.133, f32[544]{0:T(1024)S(1)} %get-tuple-element.120), kind=kCustom, calls=%fused_computation.13 | custom fusion | flops 544 | bytes 8704 | tf_op jit(solution)/shard_map/scatter-add | solution.py:103
  249.5 5.1 %scatter_fusion.3 = f32[131072]{0:T(1024)S(1)} fusion(f32[131072]{0:T(1024)S(1)} %scatter_fusion.2, s32[544]{0:T(1024)S(1)} %copy-done.131, f32[544]{0:T(1024)S(1)} %get-tuple-element.119), kind=kCustom, calls=%fused_computation.14 | custom fusion | flops 544 | bytes 8704 | tf_op jit(solution)/shard_map/scatter-add | solution.py:103
  254.7 5.1 %scatter_fusion.4 = f32[131072]{0:T(1024)S(1)} fusion(f32[131072]{0:T(1024)S(1)} %scatter_fusion.3, s32[544]{0:T(1024)S(1)} %copy-done.129, f32[544]{0:T(1024)S(1)} %get-tuple-element.123), kind=kCustom, calls=%fused_computation.15 | custom fusion | flops 544 | bytes 8704 | tf_op jit(solution)/shard_map/scatter-add | solution.py:103
  259.8 5.1 %scatter_fusion.5 = f32[131072]{0:T(1024)S(1)} fusion(f32[131072]{0:T(1024)S(1)} %scatter_fusion.4, s32[544]{0:T(1024)S(1)} %copy-done.127, f32[544]{0:T(1024)S(1)} %get-tuple-element.124), kind=kCustom, calls=%fused_computation.16 | custom fusion | flops 544 | bytes 8704 | tf_op jit(solution)/shard_map/scatter-add | solution.py:103
  264.9 5.4 %scatter_fusion.6 = f32[131072]{0:T(1024)S(1)} fusion(f32[131072]{0:T(1024)S(1)} %scatter_fusion.5, s32[544]{0:T(1024)S(1)} %copy-done.125, f32[544]{0:T(1024)S(1)} %multiply_add_fusion.6), kind=kCustom, calls=%fused_computation.17 | custom fusion | flops 544 | bytes 8704 | tf_op jit(solution)/shard_map/scatter-add | solution.py:103
  270.3 5.1 %scatter_fusion.7 = f32[131072]{0:T(1024)S(1)} fusion(f32[131072]{0:T(1024)S(1)} %scatter_fusion.6, s32[544]{0:T(1024)S(1)} %get-tuple-element.35, f32[544]{0:T(1024)S(1)} %get-tuple-element.125), kind=kCustom, calls=%fused_computation.18 | custom fusion | flops 544 | bytes 8704 | tf_op jit(solution)/shard_map/scatter-add | solution.py:103
  275.4 1.0 reshape.520
  276.4 42.4 %all-reduce.31.cloned.1.call-done = f32[6,256,256]{2,1,0:T(8,128)} async-done(((f32[6,256,256]{2,1,0:T(8,128)}), f32[6,256,256]{2,1,0:T(8,128)}) %all-reduce.31.cloned.1.call-update) | async-done | bytes 1572880 | tf_op jit(solution)/shard_map/psum | solution.py:255
  318.8 3.4 %broadcast_divide_fusion = f32[6,256,256]{2,1,0:T(8,128)} fusion(f32[6,256,256]{2,1,0:T(8,128)} %all-reduce.31.cloned.1.call-done, f32[]{:T(128)} %bitcast.123), kind=kLoop, calls=%fused_computation.96 | loop fusion | flops 393216 | bytes 3145732 | tf_op jit(solution)/shard_map/div | solution.py:263
  (446 shorter events, 41.2 us)
Async XLA Ops:
  7.2 13.6 %copy-start.86 = (f32[4,32768]{1,0:T(4,128)S(1)}, f32[4,32768]{1,0:T(4,128)}, u32[]{:S(2)}) copy-start(f32[4,32768]{1,0:T(4,128)} %param.12) | copy-start | bytes 1572868
  8.8 17.6 %copy-start.163 = (s32[256,1]{0,1:T(1,128)}, s32[256,1]{0,1:T(1,128)S(1)}, u32[]{:S(2)}) copy-start(s32[256,1]{0,1:T(1,128)S(1)} %compare_select_fusion.8) | copy-start | bytes 3076
  13.3 45.4 %all-to-all-start = ((f32[32,17,4]{1,2,0:T(4,128)}), f32[32,17,4]{1,2,0:T(4,128)}, u32[]{:S(2)}, u32[]{:S(2)}) async-start(f32[32,17,4]{1,2,0:T(4,128)} %copy.78), calls=%async_computation | async-start | bytes 131072 | tf_op jit(solution)/shard_map/all_to_all | solution.py:199
  20.8 5.6 %copy-start.152 = (f32[128,3]{0,1:T(4,128)S(1)}, f32[128,3]{0,1:T(4,128)}, u32[]{:S(2)}) copy-start(f32[128,3]{0,1:T(4,128)} %param.20) | copy-start | bytes 4612
  22.3 33.5 %collective-permute-start.1 = (f32[128,1,32]{2,1,0:T(1,128)}, f32[128,1,32]{2,1,0:T(1,128)}, u32[]{:S(2)}, u32[]{:S(2)}) collective-permute-start(f32[128,1,32]{2,1,0:T(1,128)} %get-tuple-element.75), channel_id=1, source_target_pairs={{0,1},{1,2},{2,3},{3,4},{4,5},{5,6},{6,7},{7,8},{8,9},{9,10},{10,1... | collective-permute-start | bytes 49160 | tf_op jit(solution)/shard_map/ppermute | solution.py:22
  25.0 30.8 %collective-permute-start = (f32[128,1,32]{2,1,0:T(1,128)}, f32[128,1,32]{2,1,0:T(1,128)}, u32[]{:S(2)}, u32[]{:S(2)}) collective-permute-start(f32[128,1,32]{2,1,0:T(1,128)} %get-tuple-element.76), channel_id=1, source_target_pairs={{1,0},{2,1},{3,2},{4,3},{5,4},{6,5},{7,6},{8,7},{9,8},{10,9},{11,1... | collective-permute-start | bytes 49160 | tf_op jit(solution)/shard_map/ppermute | solution.py:23
  29.5 3.3 copy-start.138
  29.5 3.3 %copy-start.153 = (f32[6,256]{1,0:T(8,128)S(1)}, f32[6,256]{1,0:T(8,128)}, u32[]{:S(2)}) copy-start(f32[6,256]{1,0:T(8,128)} %param.22) | copy-start | bytes 18436
  32.8 3.4 %copy-start.139 = (f32[1,256]{1,0:T(1,128)}, f32[1,256]{1,0:T(1,128)S(1)}, u32[]{:S(2)}) copy-start(f32[1,256]{1,0:T(1,128)S(1)} %get-tuple-element.131) | copy-start | bytes 3076
  32.8 5.9 %copy-start.141 = (f32[1,256]{1,0:T(1,128)}, f32[1,256]{1,0:T(1,128)S(1)}, u32[]{:S(2)}) copy-start(f32[1,256]{1,0:T(1,128)S(1)} %get-tuple-element.130) | copy-start | bytes 3076
  32.9 8.5 %copy-start.143 = (f32[1,256]{1,0:T(1,128)}, f32[1,256]{1,0:T(1,128)S(1)}, u32[]{:S(2)}) copy-start(f32[1,256]{1,0:T(1,128)S(1)} %get-tuple-element.129) | copy-start | bytes 3076
  32.9 10.9 %copy-start.145 = (f32[1,256]{1,0:T(1,128)}, f32[1,256]{1,0:T(1,128)S(1)}, u32[]{:S(2)}) copy-start(f32[1,256]{1,0:T(1,128)S(1)} %get-tuple-element.128) | copy-start | bytes 3076
  32.9 13.4 %copy-start.147 = (f32[1,256]{1,0:T(1,128)}, f32[1,256]{1,0:T(1,128)S(1)}, u32[]{:S(2)}) copy-start(f32[1,256]{1,0:T(1,128)S(1)} %get-tuple-element.132) | copy-start | bytes 3076
  32.9 15.9 %copy-start.149 = (f32[1,256]{1,0:T(1,128)}, f32[1,256]{1,0:T(1,128)S(1)}, u32[]{:S(2)}) copy-start(f32[1,256]{1,0:T(1,128)S(1)} %get-tuple-element.127) | copy-start | bytes 3076
  49.0 3.4 %copy-start.39 = (f32[256,256]{0,1:T(8,128)}, f32[256,256]{0,1:T(8,128)S(1)}, u32[]{:S(2)}) copy-start(f32[256,256]{0,1:T(8,128)S(1)} %get-tuple-element.102) | copy-start | bytes 786436
  50.0 3.4 %copy-start.166 = (f32[256]{0:T(256)S(1)}, f32[256]{0:T(256)}, u32[]{:S(2)}) copy-start(f32[256]{0:T(256)} %param.18) | copy-start | bytes 3076
  60.3 5.3 %copy-start.124 = (s32[544]{0:T(1024)}, s32[544]{0:T(1024)S(1)}, u32[]{:S(2)}) copy-start(s32[544]{0:T(1024)S(1)} %get-tuple-element.29) | copy-start | bytes 6532
  60.3 10.5 %copy-start.126 = (s32[544]{0:T(1024)}, s32[544]{0:T(1024)S(1)}, u32[]{:S(2)}) copy-start(s32[544]{0:T(1024)S(1)} %get-tuple-element.32) | copy-start | bytes 6532
  60.3 10.5 %copy-start.128 = (s32[544]{0:T(1024)}, s32[544]{0:T(1024)S(1)}, u32[]{:S(2)}) copy-start(s32[544]{0:T(1024)S(1)} %get-tuple-element.34) | copy-start | bytes 6532
  60.4 21.0 %copy-start.130 = (s32[544]{0:T(1024)}, s32[544]{0:T(1024)S(1)}, u32[]{:S(2)}) copy-start(s32[544]{0:T(1024)S(1)} %get-tuple-element.31) | copy-start | bytes 6532
  60.4 20.9 %copy-start.132 = (s32[544]{0:T(1024)}, s32[544]{0:T(1024)S(1)}, u32[]{:S(2)}) copy-start(s32[544]{0:T(1024)S(1)} %get-tuple-element.33) | copy-start | bytes 6532
  60.4 31.3 %copy-start.134 = (s32[544]{0:T(1024)}, s32[544]{0:T(1024)S(1)}, u32[]{:S(2)}) copy-start(s32[544]{0:T(1024)S(1)} %get-tuple-element.28) | copy-start | bytes 6532
  60.4 31.3 %copy-start.136 = (s32[544]{0:T(1024)}, s32[544]{0:T(1024)S(1)}, u32[]{:S(2)}) copy-start(s32[544]{0:T(1024)S(1)} %get-tuple-element.30) | copy-start | bytes 6532
  97.5 15.5 %copy-start.12 = (f32[128,33,32]{2,1,0:T(8,128)S(1)}, f32[128,33,32]{2,1,0:T(8,128)}, u32[]{:S(2)}) copy-start(f32[128,33,32]{2,1,0:T(8,128)} %fusion) | copy-start | bytes 1622020
  105.6 18.1 %all-to-all-start.1 = ((f32[32,17,4]{1,2,0:T(4,128)}), f32[32,17,4]{1,2,0:T(4,128)}, u32[]{:S(2)}, u32[]{:S(2)}) async-start(f32[32,17,4]{1,2,0:T(4,128)} %copy.80), calls=%async_computation.1 | async-start | bytes 131072 | tf_op jit(solution)/shard_map/all_to_all | solution.py:209
  121.7 4.6 %copy-start.151 = (f32[256]{0:T(256)S(1)}, f32[256]{0:T(256)}, u32[]{:S(2)}) copy-start(f32[256]{0:T(256)} %get-tuple-element.13) | copy-start | bytes 3076
  121.7 4.6 %copy-start.167 = (f32[256]{0:T(256)S(1)}, f32[256]{0:T(256)}, u32[]{:S(2)}) copy-start(f32[256]{0:T(256)} %param.17) | copy-start | bytes 3076
  121.7 5.2 %copy-start.160 = (f32[256]{0:T(256)S(1)}, f32[256]{0:T(256)}, u32[]{:S(2)}) copy-start(f32[256]{0:T(256)} %get-tuple-element.10) | copy-start | bytes 3076
  121.7 5.2 %copy-start.161 = (f32[256]{0:T(256)S(1)}, f32[256]{0:T(256)}, u32[]{:S(2)}) copy-start(f32[256]{0:T(256)} %get-tuple-element.11) | copy-start | bytes 3076
  121.7 5.2 %copy-start.162 = (f32[256]{0:T(256)S(1)}, f32[256]{0:T(256)}, u32[]{:S(2)}) copy-start(f32[256]{0:T(256)} %get-tuple-element.12) | copy-start | bytes 3076
  121.8 5.2 %copy-start.164 = (f32[256]{0:T(256)S(1)}, f32[256]{0:T(256)}, u32[]{:S(2)}) copy-start(f32[256]{0:T(256)} %get-tuple-element.151) | copy-start | bytes 3076
  121.8 5.2 %copy-start.169 = (f32[256]{0:T(256)S(1)}, f32[256]{0:T(256)}, u32[]{:S(2)}) copy-start(f32[256]{0:T(256)} %param.23) | copy-start | bytes 3076
  129.2 3.1 copy-start.87
  129.2 3.1 copy-start.89
  154.7 11.0 %copy-start.14 = (f32[5,256,256]{1,2,0:T(8,128)S(1)}, f32[5,256,256]{1,2,0:T(8,128)}, u32[]{:S(2)}) copy-start(f32[5,256,256]{1,2,0:T(8,128)} %copy-done.13) | copy-start | bytes 3932164
  158.7 75.2 %all-to-all-start.2 = ((f32[32,17,4]{1,2,0:T(4,128)}), f32[32,17,4]{1,2,0:T(4,128)S(1)}, u32[]{:S(2)}, u32[]{:S(2)}) async-start(f32[32,17,4]{1,2,0:T(4,128)} %copy.85), calls=%async_computation.2 | async-start | bytes 131072 | tf_op jit(solution)/shard_map/all_to_all | solution.py:234
  164.4 154.4 %all-reduce.31.cloned.1.call-start = ((), (), s32[]{:S(2)}) async-start(), calls=%async_computation.3 | async-start | bytes 3145728 | tf_op jit(solution)/shard_map/psum | solution.py:255
  168.9 3.0 copy-start.19
  168.9 3.0 copy-start.48
  168.9 3.0 copy-start.58
  172.0 3.1 copy-start.22
  172.0 3.1 copy-start.46
  172.0 3.1 copy-start.56
  172.0 3.0 copy-start.67
  172.0 3.0 copy-start.96
  172.0 3.0 copy-start.98
  172.0 3.0 copy-start.114
  175.1 3.0 copy-start.25
  175.1 3.0 copy-start.44
  175.1 3.0 copy-start.54
  175.1 3.0 copy-start.69
  175.1 3.0 copy-start.92
  178.2 3.0 copy-start.28
  178.2 3.0 copy-start.42
  178.2 3.0 copy-start.52
  178.2 3.0 copy-start.71
  184.5 49.5 %copy-start.123 = (f32[3,544]{1,0:T(4,128)S(1)}, f32[3,544]{1,0:T(4,128)}, u32[]{:S(2)}) copy-start(f32[3,544]{1,0:T(4,128)} %slice_subtract_fusion.3) | copy-start | bytes 19588
  184.5 49.6 %copy-start.137 = (s32[544]{0:T(1024)S(1)}, s32[544]{0:T(1024)}, u32[]{:S(2)}) copy-start(s32[544]{0:T(1024)} %copy-done.136) | copy-start | bytes 6532
  234.1 5.1 %copy-start.135 = (s32[544]{0:T(1024)S(1)}, s32[544]{0:T(1024)}, u32[]{:S(2)}) copy-start(s32[544]{0:T(1024)} %copy-done.134) | copy-start | bytes 6532
  239.3 5.1 %copy-start.133 = (s32[544]{0:T(1024)S(1)}, s32[544]{0:T(1024)}, u32[]{:S(2)}) copy-start(s32[544]{0:T(1024)} %copy-done.132) | copy-start | bytes 6532
  244.4 5.1 %copy-start.131 = (s32[544]{0:T(1024)S(1)}, s32[544]{0:T(1024)}, u32[]{:S(2)}) copy-start(s32[544]{0:T(1024)} %copy-done.130) | copy-start | bytes 6532
  249.5 5.1 %copy-start.129 = (s32[544]{0:T(1024)S(1)}, s32[544]{0:T(1024)}, u32[]{:S(2)}) copy-start(s32[544]{0:T(1024)} %copy-done.128) | copy-start | bytes 6532
  254.7 5.1 %copy-start.127 = (s32[544]{0:T(1024)S(1)}, s32[544]{0:T(1024)}, u32[]{:S(2)}) copy-start(s32[544]{0:T(1024)} %copy-done.126) | copy-start | bytes 6532
  259.8 5.1 %copy-start.125 = (s32[544]{0:T(1024)S(1)}, s32[544]{0:T(1024)}, u32[]{:S(2)}) copy-start(s32[544]{0:T(1024)} %copy-done.124) | copy-start | bytes 6532
  (112 other events, 182.9 us)
Sparse Core Ops, SparseCore 0:
  184.6 134.1 all-reduce.30
where the time goes:
time: 333 us; the launch traced here: 329 us
  other arithmetic  85.1 us (26%)
  local copies, waits for them, and re-layouts  78.4 us (24%)
  waiting for transfers between devices  42.4 us (13%)
  blocking collectives  40.8 us (12%)
  matrix products  35.2 us (11%)
  starting transfers between devices  24.9 us (7%)
  between operations  22.6 us (7%)
    psum x1, waiting for transfers between devices, on_device(): lax.psum((jnp.stack(weight_parts), jnp.stack(bias_parts)), ('gx', 'gy'))  42.4 us
    gather x8, local copies, waits for them, and re-layouts, interpolate(): corner = flat_field[cell_index + shift_cells]  42 us
    scatter-add x8, other arithmetic, spread(): accumulated = accumulated.at[cell_index + shift_cells].add(contribution)  41.1 us
    psum x1, blocking collectives, on_device(): totals, readout_total = lax.psum((local_sums, readout_part), ('gx', 'gy'))  40.8 us
    dot_general x17, matrix products, hidden_layer(): projected = jnp.einsum('oi,sip->sop', weight, streams, precision=highest)  31.3 us
    unnamed x341, local copies, waits for them, and re-layouts  19.5 us
    all_to_all x1, starting transfers between devices, on_device(): lax.all_to_all(looked.T.reshape(devices, capacity, 4), ('gx', 'gy'), spli...  7.47 us
    all_to_all x1, starting transfers between devices, on_device(): lax.all_to_all(pack_rows(request_rows.T, slot_index, devices, capacity),...  7.45 us
  transfers between devices with their start and end apart: 6, of which 1 were waited for; matrix products, arithmetic and copies ran while one was open for 30% of the time, Pallas kernels for 0%

commit v1 on v0

v1 whole, which is shorter than its diff:
```python
import functools

import jax
import jax.numpy as jnp
from jax import lax
from jax.experimental import pallas as pl
from jax.experimental.pallas import tpu as pltpu
from jax.sharding import PartitionSpec as P

TILE_SIDE = 32
LANES = 128
data_weight = 1.0
smooth_weight = 0.05
AXES = ("gx", "gy")
f32 = jnp.float32
bf16 = jnp.bfloat16
NN = (((1,), (0,)), ((), ()))
NT = (((1,), (1,)), ((), ()))


def dot(a, b, dims=NN):
    return lax.dot_general(a, b, dims, preferred_element_type=f32)


def split2(x):
    hi = x.astype(bf16)
    return hi, (x - hi.astype(f32)).astype(bf16)


def split3(x):
    hi = x.astype(bf16)
    rest = x - hi.astype(f32)
    mid = rest.astype(bf16)
    return hi, mid, (rest - mid.astype(f32)).astype(bf16)


def iota(shape, dim):
    return lax.broadcasted_iota(jnp.int32, shape, dim)


def sin_cos(phase):
    turns = jnp.floor(phase * 0.6366197723675814 + 0.5)
    y = phase - turns * 1.5703125
    y = y - turns * 4.837512969970703125e-4
    y = y - turns * 7.549789954891882e-8
    quarter = turns.astype(jnp.int32)
    y2 = y * y
    s = y + y * y2 * (-1.6666654611e-1 + y2 * (8.3321608736e-3 - y2 * 1.9515295891e-4))
    c = (
        1.0
        - 0.5 * y2
        + y2
        * y2
        * (4.166664568298827e-2 + y2 * (-1.388731625493765e-3 + y2 * 2.443315711809948e-5))
    )
    odd = (quarter & 1) == 1
    sin_part = jnp.where(odd, c, s)
    cos_part = jnp.where(odd, s, c)
    sin_part = jnp.where((quarter & 2) == 2, -sin_part, sin_part)
    cos_part = jnp.where(((quarter + 1) & 2) == 2, -cos_part, cos_part)
    return sin_part, cos_part


def activations(v, z1, z2, z3, z4):
    s = 1.0 - v * v
    q = z1 * z1 + z2 * z2 + z3 * z3
    return s, q, s * z4 - 2.0 * v * s * q


def slot_ranks_row(owner_col, owner_row):
    n = owner_row.shape[1]
    same = (owner_col == owner_row) & (iota((n, n), 0) < iota((n, n), 1))
    return jnp.sum(jnp.where(same, 1.0, 0.0), axis=0, keepdims=True).astype(jnp.int32)


def slot_ranks_col(owner_col, owner_row):
    n = owner_row.shape[1]
    same = (owner_col == owner_row) & (iota((n, n), 1) < iota((n, n), 0))
    return jnp.sum(jnp.where(same, 1.0, 0.0), axis=1, keepdims=True).astype(jnp.int32)


ROWS = 32


def forward_kernel(
    devices, layers, tiles,
    live_ref, owner_col_ref, owner_row_ref, slot_ref, offsets_ref, fractions_ref, source_ref,
    fourier_ref, weights_ref, small_ref,
    request_ref, pre_ref, first_ref, outputs_ref,
    hi_ref, lo_ref, z_ref, col_ref,
):
    points = slot_ref.shape[1]
    width = weights_ref.shape[1]
    streams = 5
    off = offsets_ref[...]
    fractions = fractions_ref[...]
    owner_row = owner_row_ref[...]
    slot = slot_ref[...]
    cells = jnp.concatenate(
        [TILE_SIDE * slot + off[0:1], TILE_SIDE * owner_row + off[1:2], off[2:3]], axis=0
    )
    position = cells.astype(f32) + fractions
    f = fourier_ref[...]
    phases = f[:, 0:1] * position[0:1] + f[:, 1:2] * position[1:2] + f[:, 2:3] * position[2:3]
    sin_part, cos_part = sin_cos(phases)
    squared = f[:, 0:1] * f[:, 0:1] + f[:, 1:2] * f[:, 1:2] + f[:, 2:3] * f[:, 2:3]
    freqs = f.shape[0]

    def put(stream, top, bottom):
        for start, value in ((0, top), (freqs, bottom)):
            rows = pl.ds(start, freqs)
            lanes = pl.ds(stream * points, points)
            first_ref[rows, lanes] = value
            hi, lo = split2(value)
            hi_ref[rows, lanes] = hi
            lo_ref[rows, lanes] = lo

    put(0, sin_part, cos_part)
    for k in range(3):
        put(k + 1, cos_part * f[:, k : k + 1], -sin_part * f[:, k : k + 1])
    put(4, -sin_part * squared, -cos_part * squared)

    small_cols = jnp.transpose(small_ref[...])
    readout_col = small_cols[:, layers : layers + 1]

    def layer(depth, sums):
        w_hi, w_lo = split2(weights_ref[depth])
        for k in range(streams):
            lanes = pl.ds(k * points, points)
            h_hi = hi_ref[:, lanes]
            z_ref[:, lanes] = dot(w_hi, h_hi) + dot(w_hi, lo_ref[:, lanes]) + dot(w_lo, h_hi)
        bias = jnp.sum(
            jnp.where(iota(small_cols.shape, 1) == depth, small_cols, 0.0), axis=1, keepdims=True
        )
        col_ref[:, 0:1] = bias
        col_ref[:, 1:2] = readout_col

        def chunk(c, totals):
            rows = pl.ds(pl.multiple_of(c * ROWS, ROWS), ROWS)

            def z_of(k):
                return z_ref[rows, pl.ds(k * points, points)]

            v = jnp.tanh(z_of(0) + col_ref[rows, 0:1])
            z1, z2, z3, z4 = z_of(1), z_of(2), z_of(3), z_of(4)
            s, _, curve = activations(v, z1, z2, z3, z4)
            r = col_ref[rows, 1:2]
            new = []
            for k, (kept, h) in enumerate(
                ((v, v), (z1, s * z1), (z2, s * z2), (z3, s * z3), (z4, curve))
            ):
                lanes = pl.ds(k * points, points)
                pre_ref[depth, rows, lanes] = kept
                hi, lo = split2(h)
                hi_ref[rows, lanes] = hi
                lo_ref[rows, lanes] = lo
                new.append(totals[k] + jnp.sum(r * h, axis=0, keepdims=True))
            return tuple(new)

        zero = tuple(jnp.zeros((1, points), f32) for _ in range(streams))
        return lax.fori_loop(0, width // ROWS, chunk, zero)

    zero = tuple(jnp.zeros((1, points), f32) for _ in range(streams))
    out = lax.fori_loop(0, layers, layer, zero)
    outputs = jnp.concatenate(list(out) + [jnp.zeros((3, points), f32)], axis=0)
    outputs_ref[...] = outputs

    live = jnp.where(iota((1, points), 1) < live_ref[0, 0], 1.0, 0.0)
    row_index = ((off[0:1] * (TILE_SIDE // 4) + off[1:2] // 4) * tiles + slot).astype(f32)
    lane_index = ((off[1:2] % 4) * TILE_SIDE + off[2:3]).astype(f32)
    comps = [
        row_index, lane_index, fractions[0:1], fractions[1:2], fractions[2:3],
        outputs[1:2], outputs[2:3], outputs[3:4], outputs[4:5], source_ref[...], live,
    ]
    to_owner = owner_row == iota((devices, points), 0)
    ranks = slot_ranks_col(owner_col_ref[...], owner_row)
    place = jnp.where(ranks == iota((points, LANES), 1), 1.0, 0.0).astype(bf16)
    spread = jnp.concatenate([jnp.where(to_owner, c, 0.0) for c in comps], axis=0)
    a, b, c = split3(spread)
    packed = dot(a, place) + dot(b, place) + dot(c, place)
    for k in range(len(comps)):
        request_ref[:, k, :] = packed[k * devices : (k + 1) * devices]
    for k in range(len(comps), request_ref.shape[1]):
        request_ref[:, k, :] = jnp.zeros((devices, LANES), f32)


def owner_kernel(
    devices, tiles, lanes_each,
    received_ref, field_ref,
    response_ref, kept_ref,
    padded_ref, window_hi, window_lo, x_ref,
):
    cells = field_ref.shape[0]
    group = LANES // lanes_each
    blocks = devices // group
    slots = blocks * LANES
    plane = (TILE_SIDE // 4) * tiles
    padded_ref[0:cells, :] = field_ref[...]
    padded_ref[cells:, :] = jnp.zeros((padded_ref.shape[0] - cells, LANES), f32)
    for a in range(2):
        base = a * plane
        main = jnp.transpose(padded_ref[base : base + cells, :])
        hi, lo = split2(main)
        window_hi[a * 160 : a * 160 + 128, :] = hi
        window_lo[a * 160 : a * 160 + 128, :] = lo
        extra = jnp.transpose(padded_ref[base + tiles : base + tiles + cells, :])[0:TILE_SIDE]
        hi, lo = split2(extra)
        window_hi[a * 160 + 128 : a * 160 + 160, :] = hi
        window_lo[a * 160 + 128 : a * 160 + 160, :] = lo
    for j in range(blocks):
        total = received_ref[group * j]
        for m in range(1, group):
            total = total + pltpu.roll(received_ref[group * j + m], lanes_each * m, 1)
        x_ref[:, j * LANES : (j + 1) * LANES] = total

    step = 2 * LANES
    for start in range(0, slots, step):
        x = x_ref[:, start : start + step]
        rows = x[0:1].astype(jnp.int32)
        place = x[1:2].astype(jnp.int32)
        hot = jnp.where(iota((cells, step), 0) == rows, 1.0, 0.0).astype(bf16)
        found = dot(window_hi[...], hot) + dot(window_lo[...], hot)
        y_mod = place // TILE_SIDE
        z_cell = place % TILE_SIDE
        z_iota = iota((TILE_SIDE, step), 0)
        at_z = (z_iota == z_cell, z_iota == z_cell + 1)
        corner = {}
        for a in range(2):
            parts = [found[a * 160 + TILE_SIDE * j : a * 160 + TILE_SIDE * (j + 1)] for j in range(5)]
            for b in range(2):
                rows_y = jnp.where(y_mod == 0, parts[b], 0.0)
                for j in range(1, 4):
                    rows_y = jnp.where(y_mod == j, parts[j + b], rows_y)
                for c in range(2):
                    corner[a, b, c] = jnp.sum(
                        jnp.where(at_z[c], rows_y, 0.0), axis=0, keepdims=True
                    )
        fr = [x[2:3], x[3:4], x[4:5]]
        w = [(1.0 - t, t) for t in fr]
        sign = (-1.0, 1.0)
        values = [jnp.zeros((1, step), f32) for _ in range(4)]
        for (a, b, c), k in corner.items():
            values[0] = values[0] + w[0][a] * w[1][b] * w[2][c] * k
            values[1] = values[1] + sign[a] * w[1][b] * w[2][c] * k
            values[2] = values[2] + w[0][a] * sign[b] * w[2][c] * k
            values[3] = values[3] + w[0][a] * w[1][b] * sign[c] * k
        du = [x[5:6], x[6:7], x[7:8]]
        lap = x[8:9]
        residual = (
            -(values[0] * lap + (values[1] * du[0] + values[2] * du[1] + values[3] * du[2]))
            - x[9:10]
        )
        scaled = 2.0 * x[10:11] * residual
        zeros = jnp.zeros((4, step), f32)
        answer = jnp.concatenate(values + [zeros], axis=0)
        for j in range(step // LANES):
            block = start // LANES + j
            part = answer[:, j * LANES : (j + 1) * LANES]
            for m in range(group):
                shifted = pltpu.roll(part, (LANES - lanes_each * m) % LANES, 1) if m else part
                response_ref[group * block + m] = shifted
        kept_ref[:, start : start + step] = jnp.concatenate(
            [x[0:5], -scaled * lap, -scaled * du[0], -scaled * du[1], -scaled * du[2]]
            + [jnp.zeros((7, step), f32)],
            axis=0,
        )


def field_kernel(
    devices, tiles,
    index_ref, kept_ref, field_ref, before_ref, after_ref,
    grad_ref, energy_ref,
    hot_ref, c_hi, c_lo, sum_ref, part_ref,
):
    cells = field_ref.shape[0]
    slots = kept_ref.shape[1]
    plane = (TILE_SIDE // 4) * tiles
    step = 2 * LANES
    for start in range(0, slots, step):
        lanes = slice(start, start + step)
        x = kept_ref[:, lanes]
        rows = x[0:1].astype(jnp.int32)
        place = x[1:2].astype(jnp.int32)
        hot_ref[:, lanes] = jnp.where(iota((cells, step), 0) == rows, 1.0, 0.0).astype(bf16)
        y_mod = place // TILE_SIDE
        z_cell = place % TILE_SIDE
        z_iota = iota((TILE_SIDE, step), 0)
        at_z = (z_iota == z_cell, z_iota == z_cell + 1)
        w = [(1.0 - x[k : k + 1], x[k : k + 1]) for k in (2, 3, 4)]
        g = [x[k : k + 1] for k in (5, 6, 7, 8)]
        sign = (-1.0, 1.0)
        for a in range(2):
            along = []
            for b in range(2):
                pair = []
                for c in range(2):
                    pair.append(
                        g[0] * w[0][a] * w[1][b] * w[2][c]
                        + g[1] * sign[a] * w[1][b] * w[2][c]
                        + g[2] * w[0][a] * sign[b] * w[2][c]
                        + g[3] * w[0][a] * w[1][b] * sign[c]
                    )
                along.append(jnp.where(at_z[0], pair[0], 0.0) + jnp.where(at_z[1], pair[1], 0.0))
            for j in range(5):
                value = jnp.where(y_mod == j, along[0], 0.0) + jnp.where(
                    y_mod == j - 1, along[1], 0.0
                )
                hi, lo = split2(value)
                at = a * 128 + TILE_SIDE * j if j < 4 else 256 + a * TILE_SIDE
                c_hi[at : at + TILE_SIDE, lanes] = hi
                c_lo[at : at + TILE_SIDE, lanes] = lo
    sum_ref[...] = jnp.zeros(sum_ref.shape, f32)
    block = 2 * LANES
    for start in range(0, cells, block):
        hot = hot_ref[start : start + block, :]
        part = dot(hot, c_hi[...], NT) + dot(hot, c_lo[...], NT)
        part_ref[start : start + block, :] = part
    sum_ref[0:cells, :] = part_ref[:, 0:128]
    sum_ref[plane : plane + cells, :] += part_ref[:, 128:256]
    low = slice(0, TILE_SIDE)
    sum_ref[tiles : tiles + cells, low] += part_ref[:, 256 : 256 + TILE_SIDE]
    sum_ref[plane + tiles : plane + tiles + cells, low] += part_ref[
        :, 256 + TILE_SIDE : 256 + 2 * TILE_SIDE
    ]

    me = index_ref[0, 0]
    row = iota((plane, LANES), 0)
    lane = iota((plane, LANES), 1)
    z_inner = (lane % TILE_SIDE) < TILE_SIDE - 1
    first_row = row < tiles
    last_row = row >= plane - tiles
    low_lane = lane < TILE_SIDE
    high_lane = lane >= LANES - TILE_SIDE
    has_after = jnp.where(me < devices - 1, 1.0, 0.0)
    has_before = jnp.where(me > 0, 1.0, 0.0)
    after_mask = jnp.where(last_row & high_lane, has_after, 1.0)
    before_mask = jnp.where(first_row & low_lane, has_before, 1.0)
    energy_mask = before_mask
    next_tile = (row % tiles) < tiles - 1
    prev_tile = (row % tiles) > 0

    def load(x):
        return field_ref[pl.ds(pl.multiple_of(x * plane, plane), plane), :]

    def plane_step(x, energy):
        here = load(x)
        diff_z = jnp.where(z_inner, pltpu.roll(here, LANES - 1, 1) - here, 0.0)
        grad = pltpu.roll(diff_z, 1, 1) - diff_z
        energy = energy + diff_z * diff_z
        above = jnp.concatenate([here[tiles:], after_ref[x]], axis=0)
        up = pltpu.roll(jnp.where(low_lane, above, here), LANES - TILE_SIDE, 1)
        below = jnp.concatenate([before_ref[x], here[: plane - tiles]], axis=0)
        down = pltpu.roll(jnp.where(high_lane, below, here), TILE_SIDE, 1)
        diff_up = (up - here) * after_mask
        diff_down = (here - down) * before_mask
        grad = grad + diff_down - diff_up
        energy = energy + diff_down * diff_down
        first = x == 0
        last = x == TILE_SIDE - 1
        nxt = load(jnp.where(last, 0, x + 1))
        nxt = jnp.where(last, pltpu.roll(nxt, plane - 1, 0), nxt)
        prv = load(jnp.where(first, TILE_SIDE - 1, x - 1))
        prv = jnp.where(first, pltpu.roll(prv, 1, 0), prv)
        diff_next = jnp.where(jnp.logical_not(last) | next_tile, nxt - here, 0.0)
        diff_prev = jnp.where(jnp.logical_not(first) | prev_tile, here - prv, 0.0)
        grad = grad + diff_prev - diff_next
        energy = energy + diff_prev * diff_prev
        at = pl.ds(pl.multiple_of(x * plane, plane), plane)
        grad_ref[at, :] = sum_ref[at, :] + 2.0 * smooth_weight * grad
        return energy

    energy = lax.fori_loop(0, TILE_SIDE, plane_step, jnp.zeros((plane, LANES), f32))
    total = jnp.sum(energy, axis=0, keepdims=True)
    wide = jnp.concatenate([total, jnp.zeros((1, energy_ref.shape[1] - LANES), f32)], axis=1)
    energy_ref[...] = jnp.where(iota(energy_ref.shape, 0) == 0, wide, 0.0)


def backward_kernel(
    devices, layers, lanes_each,
    scalars_ref, owner_col_ref, owner_row_ref, source_ref, observed_ref, response_ref,
    outputs_ref, weights_ref, small_ref, pre_ref, first_ref,
    keep_ref, send_ref,
    bar_ref, zh_ref, zl_ref, hh_ref, hl_ref, col_ref, cols_ref,
):
    points = owner_row_ref.shape[1]
    width = weights_ref.shape[1]
    owner_row = owner_row_ref[...]
    ranks = slot_ranks_row(owner_col_ref[...], owner_row)
    picked = jnp.where(ranks == iota((lanes_each, points), 0), 1.0, 0.0)
    from_owner = jnp.where(owner_row == iota((devices, points), 0), 1.0, 0.0).astype(bf16)
    values = []
    for k in range(4):
        rows = jnp.transpose(response_ref[:, k, :])[0:lanes_each]
        a, b, c = split3(rows)
        wide = dot(a, from_owner) + dot(b, from_owner) + dot(c, from_owner)
        values.append(jnp.sum(picked * wide, axis=0, keepdims=True))
    outputs = outputs_ref[...]
    out = [outputs[k : k + 1] for k in range(5)]
    live = jnp.where(iota((1, points), 1) < scalars_ref[0, 0], 1.0, 0.0)
    misfit = out[0] - observed_ref[...]
    residual = (
        -(values[0] * out[4] + (values[1] * out[1] + values[2] * out[2] + values[3] * out[3]))
        - source_ref[...]
    )
    scaled = 2.0 * live * residual
    out_grad = [2.0 * data_weight * live * misfit] + [-scaled * values[k] for k in (1, 2, 3, 0)]
    residual_sum = jnp.sum(live * residual * residual, axis=1, keepdims=True)
    misfit_sum = jnp.sum(live * misfit * misfit, axis=1, keepdims=True)
    small_cols = jnp.transpose(small_ref[...])
    readout_col = small_cols[:, layers : layers + 1]
    col_ref[...] = readout_col
    cols_ref[...] = jnp.zeros(cols_ref.shape, f32)
    lane8 = iota((ROWS, cols_ref.shape[1]), 1)
    chunks = width // ROWS

    def rows_of(c):
        return pl.ds(pl.multiple_of(c * ROWS, ROWS), ROWS)

    def pre_of(depth, rows):
        return [pre_ref[depth, rows, pl.ds(k * points, points)] for k in range(5)]

    def readout_chunk(c, carry):
        rows = rows_of(c)
        v, z1, z2, z3, z4 = pre_of(layers - 1, rows)
        s, _, curve = activations(v, z1, z2, z3, z4)
        total = out_grad[0] * v + out_grad[1] * (s * z1) + out_grad[2] * (s * z2)
        total = total + out_grad[3] * (s * z3) + out_grad[4] * curve
        grad = jnp.sum(total, axis=1, keepdims=True)
        cols_ref[rows, :] += jnp.where(lane8 == layers, grad, 0.0)
        r = col_ref[rows, :]
        for k in range(5):
            bar_ref[rows, pl.ds(k * points, points)] = r * out_grad[k]
        return carry

    lax.fori_loop(0, chunks, readout_chunk, 0)
    mine = scalars_ref[0, 1]
    half = layers // 2

    def layer(step, carry):
        depth = layers - 1 - step

        def bars(c, inner):
            rows = rows_of(c)
            v, z1, z2, z3, z4 = pre_of(depth, rows)
            b = [bar_ref[rows, pl.ds(k * points, points)] for k in range(5)]
            s = 1.0 - v * v
            q = z1 * z1 + z2 * z2 + z3 * z3
            slope = b[1] * z1 + b[2] * z2 + b[3] * z3
            v4c = 4.0 * v * b[4]
            z_bar = [
                s
                * (
                    b[0]
                    - 2.0 * v * slope
                    + b[4] * (q * (4.0 * v * v - 2.0 * s) - 2.0 * v * z4)
                ),
                s * (b[1] - v4c * z1),
                s * (b[2] - v4c * z2),
                s * (b[3] - v4c * z3),
                s * b[4],
            ]
            grad = jnp.sum(z_bar[0], axis=1, keepdims=True)
            cols_ref[rows, :] += jnp.where(lane8 == depth, grad, 0.0)
            for k in range(5):
                lanes = pl.ds(k * points, points)
                hi, lo = split2(z_bar[k])
                zh_ref[rows, lanes] = hi
                zl_ref[rows, lanes] = lo
            return inner

        lax.fori_loop(0, chunks, bars, 0)

        def put_h(rows, hs):
            for k in range(5):
                lanes = pl.ds(k * points, points)
                hi, lo = split2(hs[k])
                hh_ref[rows, lanes] = hi
                hl_ref[rows, lanes] = lo

        @pl.when(depth > 0)
        def _():
            def body(c, inner):
                rows = rows_of(c)
                v, z1, z2, z3, z4 = pre_of(jnp.maximum(depth - 1, 0), rows)
                s, _, curve = activations(v, z1, z2, z3, z4)
                put_h(rows, [v, s * z1, s * z2, s * z3, curve])
                return inner

            lax.fori_loop(0, chunks, body, 0)

        @pl.when(depth == 0)
        def _():
            def body(c, inner):
                rows = rows_of(c)
                put_h(rows, [first_ref[rows, pl.ds(k * points, points)] for k in range(5)])
                return inner

            lax.fori_loop(0, chunks, body, 0)

        grad = (
            dot(zh_ref[...], hh_ref[...], NT)
            + dot(zh_ref[...], hl_ref[...], NT)
            + dot(zl_ref[...], hh_ref[...], NT)
        )
        upper = (depth >= half).astype(jnp.int32)
        at = pl.ds(pl.multiple_of((depth - upper * half) * width, width), width)

        @pl.when(upper == mine)
        def _():
            keep_ref[at, :] = grad

        @pl.when(upper != mine)
        def _():
            send_ref[at, :] = grad

        @pl.when(depth > 0)
        def _():
            w_hi, w_lo = split2(jnp.transpose(weights_ref[depth]))
            for k in range(5):
                lanes = pl.ds(k * points, points)
                z_hi = zh_ref[:, lanes]
                bar_ref[:, lanes] = dot(w_hi, z_hi) + dot(w_hi, zl_ref[:, lanes]) + dot(w_lo, z_hi)

        return carry

    lax.fori_loop(0, layers, layer, 0)
    small = jnp.transpose(cols_ref[...])
    lane = iota((1, width), 1)
    count = jnp.full((1, 1), scalars_ref[0, 0], jnp.int32).astype(f32)
    last = jnp.where(lane == 0, residual_sum, 0.0) + jnp.where(lane == 1, misfit_sum, 0.0)
    last = last + jnp.where(lane == 2, count, 0.0)
    small = jnp.where(iota(small.shape, 0) == small.shape[0] - 1, last, small)
    keep_ref[half * width :, :] = small
    send_ref[half * width :, :] = small


def vmem():
    return pl.BlockSpec(memory_space=pltpu.VMEM)


def smem():
    return pl.BlockSpec(memory_space=pltpu.SMEM)


def call(kernel, name, specs, out_shapes, scratch, flops, limit=40):
    return pl.pallas_call(
        kernel,
        name=name,
        out_shape=out_shapes,
        in_specs=specs,
        out_specs=jax.tree.map(lambda _: vmem(), out_shapes),
        scratch_shapes=scratch,
        compiler_params=pltpu.CompilerParams(vmem_limit_bytes=limit << 20),
        cost_estimate=pl.CostEstimate(flops=flops, bytes_accessed=1 << 20, transcendentals=0),
    )


def shape(*dims):
    return jax.ShapeDtypeStruct(dims, f32)


def on_device(
    conductivity, owner_rank, tile_slot, offsets, fractions, source, observed, live_count,
    fourier, weights, biases, readout,
):
    devices = lax.axis_size(AXES)
    index = lax.axis_index(AXES)
    points = tile_slot.shape[0]
    tiles = conductivity.shape[0]
    layers, width = biases.shape
    capacity = (2 * points + devices - 1) // devices + 1
    lanes_each = 1 << (capacity - 1).bit_length()
    lanes_each = max(lanes_each, 2 * LANES // devices)
    slots = devices * lanes_each
    cells = conductivity.size // LANES
    plane = (TILE_SIDE // 4) * tiles
    wide = 5 * points

    owner_row = owner_rank.reshape(1, points)
    slot = tile_slot.reshape(1, points)
    source_row = source.reshape(1, points)
    observed_row = observed.reshape(1, points)
    small = jnp.concatenate(
        [biases, readout[None], jnp.zeros((8 - layers - 1, width), f32)], axis=0
    )
    field = conductivity.reshape(tiles, cells // tiles, LANES).transpose(1, 0, 2)
    field = field.reshape(cells, LANES)
    planes = field.reshape(TILE_SIDE, plane, LANES)

    request, pre, first, outputs = call(
        functools.partial(forward_kernel, devices, layers, tiles),
        "forward",
        [smem()] + [vmem()] * 9,
        (shape(devices, 16, LANES), shape(layers, width, wide), shape(width, wide), shape(8, points)),
        [
            pltpu.VMEM((width, wide), bf16),
            pltpu.VMEM((width, wide), bf16),
            pltpu.VMEM((width, wide), f32),
            pltpu.VMEM((width, 2), f32),
        ],
        6 * 2 * layers * width * width * wide,
    )(
        live_count.reshape(1, 1), owner_rank, owner_row, slot, offsets, fractions, source_row,
        fourier, weights, small,
    )
    received = lax.all_to_all(request, AXES, split_axis=0, concat_axis=0, tiled=True)
    response, kept = call(
        functools.partial(owner_kernel, devices, tiles, lanes_each),
        "lookup",
        [vmem()] * 2,
        (shape(devices, 8, LANES), shape(16, slots)),
        [
            pltpu.VMEM((cells + 2 * plane, LANES), f32),
            pltpu.VMEM((320, cells), bf16),
            pltpu.VMEM((320, cells), bf16),
            pltpu.VMEM((16, slots), f32),
        ],
        2 * 640 * cells * slots,
    )(received, field)
    answered = lax.all_to_all(response, AXES, split_axis=0, concat_axis=0, tiled=True)

    up = [(i, i + 1) for i in range(devices - 1)]
    down = [(j, i) for i, j in up]
    before = lax.ppermute(planes[:, plane - tiles :, :], AXES, up)
    after = lax.ppermute(planes[:, :tiles, :], AXES, down)

    half_rows = layers * width // 2
    core = index % 2
    scalars = jnp.stack([live_count[0], core]).reshape(1, 2)
    keep, send = call(
        functools.partial(backward_kernel, devices, layers, lanes_each),
        "backward",
        [smem()] + [vmem()] * 10,
        (shape(half_rows + 8, width), shape(half_rows + 8, width)),
        [
            pltpu.VMEM((width, wide), f32),
            pltpu.VMEM((width, wide), bf16),
            pltpu.VMEM((width, wide), bf16),
            pltpu.VMEM((width, wide), bf16),
            pltpu.VMEM((width, wide), bf16),
            pltpu.VMEM((width, 1), f32),
            pltpu.VMEM((width, 8), f32),
        ],
        12 * 2 * layers * width * width * wide,
    )(
        scalars, owner_rank, owner_row, source_row, observed_row, answered, outputs, weights,
        small, pre, first,
    )
    grad, energy = call(
        functools.partial(field_kernel, devices, tiles),
        "field",
        [smem()] + [vmem()] * 4,
        (shape(cells, LANES), shape(8, width)),
        [
            pltpu.VMEM((cells, slots), bf16),
            pltpu.VMEM((320, slots), bf16),
            pltpu.VMEM((320, slots), bf16),
            pltpu.VMEM((cells + 2 * plane, LANES), f32),
            pltpu.VMEM((cells, 320), f32),
        ],
        2 * 640 * cells * slots,
    )(index.reshape(1, 1), kept, field, before, after)

    bits = [1 << k for k in range(devices.bit_length() - 1)]

    def exchange(value, bit):
        return lax.ppermute(value, AXES, [(i, i ^ bit) for i in range(devices)])

    arrived = exchange(send, bits[0])
    current = keep + arrived
    main, extra = current[:half_rows], current[half_rows:]
    for bit in bits[1:]:
        half = main.shape[0] // 2
        upper = (index // bit) % 2 == 1
        low, high = main[:half], main[half:]
        outgoing = jnp.concatenate([jnp.where(upper, low, high), extra], axis=0)
        arrived = exchange(outgoing, bit)
        main = jnp.where(upper, high, low) + arrived[:half]
        extra = extra + arrived[half:]
    live_total = extra[7, 2]
    main = main / live_total
    for bit in reversed(bits):
        upper = (index // bit) % 2 == 1
        arrived = exchange(jnp.concatenate([main, energy], axis=0), bit)
        other = arrived[: main.shape[0]]
        energy = energy + arrived[main.shape[0] :]
        main = jnp.concatenate(
            [jnp.where(upper, other, main), jnp.where(upper, main, other)], axis=0
        )
    cells_total = devices * conductivity.size
    losses = jnp.stack(
        [extra[7, 0] / live_total, extra[7, 1] / live_total, jnp.sum(energy) / cells_total]
    )
    conductivity_grad = grad.reshape(cells // tiles, tiles, LANES).transpose(1, 0, 2)
    return (
        conductivity_grad.reshape(conductivity.shape),
        main.reshape(weights.shape),
        extra[:layers] / live_total,
        extra[layers] / live_total,
        losses,
    )


def solution(mesh):
    in_specs = (
        P(AXES, None), P(AXES, None), P(AXES), P(None, AXES), P(None, AXES), P(AXES), P(AXES),
        P(AXES), P(), P(), P(), P(),
    )
    out_specs = (P(AXES, None), P(), P(), P(), P())
    return jax.shard_map(
        on_device, mesh=mesh, in_specs=in_specs, out_specs=out_specs, check_vma=False
    )
```

time: 333 us -> 154 us (0.46)
  other arithmetic: 85.1 us -> 7.17 us
  local copies, waits for them, and re-layouts: 78.4 us -> 14.7 us
  Pallas kernels: 0 us -> 41.1 us
  matrix products: 35.2 us -> 0 us
  blocking collectives: 40.8 us -> 17.7 us
  between operations: 22.6 us -> 4.97 us
  waiting for transfers between devices: 42.4 us -> 50.4 us
  starting transfers between devices: 24.9 us -> 17.2 us
    gather x9 -> x0, local copies, waits for them, and re-layouts: 42.8 us -> none  [the longest x8 42 us: interpolate(): corner = flat_field[cell_index + shift_cells]]
    psum x1 -> x0, waiting for transfers between devices: 42.4 us -> none  [on_device(): lax.psum((jnp.stack(weight_parts), jnp.stack(bias_parts)), ('gx', 'gy'))]
    ppermute x2 -> x12, waiting for transfers between devices: 0.01 us -> 42.3 us  [the longest x10 42.3 us: exchange(): return lax.ppermute(value, AXES, [(i, i ^ bit) for i in range(devices)])]
    pallas_call x0 -> x4, Pallas kernels: none -> 41.1 us  [the longest x1 18 us: on_device(): call(functools.partial(backward_kernel, devices, layers, lanes_each), 'ba...]
    scatter-add x8 -> x0, other arithmetic: 41.1 us -> none  [spread(): accumulated = accumulated.at[cell_index + shift_cells].add(contribution)]
    psum x1 -> x0, blocking collectives: 40.8 us -> none  [on_device(): totals, readout_total = lax.psum((local_sums, readout_part), ('gx', 'gy'))]
    dot_general x20 -> x0, matrix products: 35.2 us -> none  [the longest x17 31.3 us: hidden_layer(): projected = jnp.einsum('oi,sip->sop', weight, streams, precision=highest)]
    reduce_sum x13 -> x1, other arithmetic: 19.2 us -> 0.6 us  [on_device(): jnp.sum(energy) / cells_total]
  transfers between devices with their start and end apart: 6 -> 13, of which waited for: 1 -> 9; matrix products, arithmetic and copies ran while one was open for 30% -> 2% of each run, Pallas kernels for 0% -> 6%
where the time goes in v1:
time: 154 us; the launch traced here: 153 us
  waiting for transfers between devices  50.4 us (33%)
  Pallas kernels  41.1 us (27%)
  blocking collectives  17.7 us (11%)
  starting transfers between devices  17.2 us (11%)
  local copies, waits for them, and re-layouts  14.7 us (10%)
  other arithmetic  7.17 us (5%)
  between operations  4.97 us (3%)
    ppermute x10, waiting for transfers between devices, exchange(): return lax.ppermute(value, AXES, [(i, i ^ bit) for i in range(devices)])  42.3 us
    pallas_call x1, Pallas kernels, on_device(): call(functools.partial(backward_kernel, devices, layers, lanes_each), 'ba...  18 us
    all_to_all x1, blocking collectives, on_device(): lax.all_to_all(request, AXES, split_axis=0, concat_axis=0, tiled=True)  17.7 us
    unnamed x32, local copies, waits for them, and re-layouts  14 us
    ppermute x10, starting transfers between devices, exchange(): return lax.ppermute(value, AXES, [(i, i ^ bit) for i in range(devices)])  12 us
    pallas_call x1, Pallas kernels, on_device(): call(functools.partial(forward_kernel, devices, layers, tiles), 'forward'...  11.5 us
    pallas_call x1, Pallas kernels, on_device(): call(functools.partial(field_kernel, devices, tiles), 'field', [smem()] +...  8.52 us
    all_to_all x1, waiting for transfers between devices, on_device(): lax.all_to_all(response, AXES, split_axis=0, concat_axis=0, tiled=True)  8.11 us
  transfers between devices with their start and end apart: 13, of which 9 were waited for; matrix products, arithmetic and copies ran while one was open for 2% of the time, Pallas kernels for 6%

profile of v1, /device:TPU:0, one launch (start us, length us, event | category | flops | bytes accessed | tf_op | source)
XLA Modules:
  0.0 153.3 jit_solution(14532536409217013701)
XLA Ops:
  1.3 0.8 copy.17.owner_col_ref
  2.1 0.8 copy.18.fourier_ref
  2.9 0.1 pad.39.clone
  3.0 0.8 maximum_maximum_fusion.small_ref
  3.7 0.7 copy-done.1
  4.4 1.4 copy-done.3
  5.8 0.7 copy-done.5
  6.5 0.7 copy-done.6
  7.2 0.7 copy-done.7
  7.9 0.7 copy-done.8
  8.6 11.5 %forward.1 = (f32[32,16,128]{2,1,0:T(8,128)S(1)}, f32[6,256,1280]{2,1,0:T(8,128)S(1)}, f32[256,1280]{1,0:T(8,128)S(1)}, f32[8,256]{1,0:T(8,128)S(1)}) custom-call(s32[1,1]{1,0:T(1,128)} %bitcast.31.live_ref, s32[256,1]{1,0:T(8,128)S(1)} %copy.17.owner_col_ref, s32[1,256]{1,0:T(1,128)S(1)} %bitcast.35, s32[1,256]{1,0:T(1,128)S(1)} %bitcast.37, ...), custom_call_target="tpu_custom_call" | custom-call | flops 6039797760 | bytes 1048576 | tf_op jit(solution)/shard_map/forward/pallas_call | solution.py:590
  20.1 0.0 copy-start.11
  20.1 3.1 %copy-done.11 = f32[6,256,1280]{2,1,0:T(8,128)} copy-done((f32[6,256,1280]{2,1,0:T(8,128)}, f32[6,256,1280]{2,1,0:T(8,128)S(1)}, u32[]{:S(2)}) %copy-start.11) | copy-done | bytes 7864344
  23.2 17.7 %all_to_all.10.received_ref = f32[32,16,128]{2,1,0:T(8,128)S(1)} all-to-all(f32[32,16,128]{2,1,0:T(8,128)S(1)} %get-tuple-element.15), channel_id=1, replica_groups=mesh['gx'=4,'gy'=8] {'gx','gy'}, dimensions={0} | all-to-all | bytes 524288 | tf_op jit(solution)/shard_map/all_to_all | solution.py:606
  40.9 0.0 copy-done
  40.9 0.0 copy-start.10
  40.9 3.2 %lookup.1 = (f32[32,8,128]{2,1,0:T(8,128)}, f32[16,1024]{1,0:T(8,128)S(1)}) custom-call(f32[32,16,128]{2,1,0:T(8,128)S(1)} %all_to_all.10.received_ref, f32[1024,128]{1,0:T(8,128)S(1)} %bitcast.32), custom_call_target="tpu_custom_call" | custom-call | flops 1342177280 | bytes 1048576 | tf_op jit(solution)/shard_map/lookup/pallas_call | solution.py:607
  44.0 0.0 copy-done.13
  44.0 2.6 %all-to-all-start.1 = ((f32[32,8,128]{2,1,0:T(8,128)}), f32[32,8,128]{2,1,0:T(8,128)S(1)}, u32[]{:S(2)}, u32[]{:S(2)}) async-start(f32[32,8,128]{2,1,0:T(8,128)} %get-tuple-element.18), calls=%async_computation.1 | async-start | bytes 262144 | tf_op jit(solution)/shard_map/all_to_all | solution.py:620
  46.6 0.1 add_bitcast_fusion.scalars_ref
  46.7 8.1 %all-to-all-done.1.response_ref = f32[32,8,128]{2,1,0:T(8,128)S(1)} async-done(((f32[32,8,128]{2,1,0:T(8,128)}), f32[32,8,128]{2,1,0:T(8,128)S(1)}, u32[]{:S(2)}, u32[]{:S(2)}) %all-to-all-start.1) | async-done | bytes 131104 | tf_op jit(solution)/shard_map/all_to_all | solution.py:620
  54.8 0.0 copy-done.2
  54.8 0.0 copy-done.4
  54.9 3.2 %copy-done.12 = f32[6,256,1280]{2,1,0:T(8,128)S(1)} copy-done((f32[6,256,1280]{2,1,0:T(8,128)S(1)}, f32[6,256,1280]{2,1,0:T(8,128)}, u32[]{:S(2)}) %copy-start.12) | copy-done | bytes 7864344
  58.1 1.3 copy-done.14
  59.4 18.0 %backward.1 = (f32[776,256]{1,0:T(8,128)S(1)}, f32[776,256]{1,0:T(8,128)}) custom-call(s32[1,2]{1,0:T(1,128)S(1)} %add_bitcast_fusion.scalars_ref, s32[256,1]{1,0:T(8,128)S(1)} %copy.17.owner_col_ref, s32[1,256]{1,0:T(1,128)S(1)} %bitcast.36, f32[1,256]{1,0:T(1,128)S(1)} %bitcast.39, f32[1,256]{1,0:T(1,128)S(1)} %bitcast.40, ...), custom_call_target="tpu_custom_call" | custom-call | flops 12079595520 | bytes 1048576 | tf_op jit(solution)/shard_map/backward/pallas_call | solution.py:630
  77.4 0.2 collective-permute-start.2
  77.6 2.3 %collective-permute-done.2 = f32[776,256]{1,0:T(8,128)S(1)} collective-permute-done((f32[776,256]{1,0:T(8,128)}, f32[776,256]{1,0:T(8,128)S(1)}, u32[]{:S(2)}, u32[]{:S(2)}) %collective-permute-start.2) | collective-permute-done | bytes 794656 | tf_op jit(solution)/shard_map/ppermute | solution.py:667
  79.9 0.1 add.77
  80.0 0.1 slice_select_fusion.4
  80.1 0.4 collective-permute-start.3
  80.5 11.1 %collective-permute-done.3 = f32[392,256]{1,0:T(8,128)S(1)} collective-permute-done((f32[392,256]{1,0:T(8,128)S(1)}, f32[392,256]{1,0:T(8,128)S(1)}, u32[]{:S(2)}, u32[]{:S(2)}) %collective-permute-start.3) | collective-permute-done | bytes 401440 | tf_op jit(solution)/shard_map/ppermute | solution.py:667
  91.5 0.1 slice_add_fusion
  91.7 0.6 collective-permute-start.4
  92.3 5.8 %collective-permute-done.4 = f32[200,256]{1,0:T(8,128)S(1)} collective-permute-done((f32[200,256]{1,0:T(8,128)S(1)}, f32[200,256]{1,0:T(8,128)S(1)}, u32[]{:S(2)}, u32[]{:S(2)}) %collective-permute-start.4) | collective-permute-done | bytes 204832 | tf_op jit(solution)/shard_map/ppermute | solution.py:667
  98.2 0.6 collective-permute-start.5
  98.8 1.3 collective-permute-start
  100.1 1.3 collective-permute-start.1
  101.4 1.5 %collective-permute-done.5 = f32[104,256]{1,0:T(8,128)S(1)} collective-permute-done((f32[104,256]{1,0:T(8,128)S(1)}, f32[104,256]{1,0:T(8,128)S(1)}, u32[]{:S(2)}, u32[]{:S(2)}) %collective-permute-start.5) | collective-permute-done | bytes 106528 | tf_op jit(solution)/shard_map/ppermute | solution.py:667
  103.0 4.5 %collective-permute-start.6 = (f32[56,256]{1,0:T(8,128)S(1)}, f32[56,256]{1,0:T(8,128)S(1)}, u32[]{:S(2)}, u32[]{:S(2)}) collective-permute-start(f32[56,256]{1,0:T(8,128)S(1)} %pad_maximum_fusion.12), channel_id=1, source_target_pairs={{0,16},{1,17},{2,18},{3,19},{4,20},{5,21},{6,22},{7,23},{8,24},{9,... | collective-permute-start | bytes 172040 | tf_op jit(solution)/shard_map/ppermute | solution.py:667
  107.5 0.0 collective-permute-done.before_ref
  107.5 0.0 collective-permute-done.1.after_ref
  107.5 8.5 %field.1 = (f32[1024,128]{1,0:T(8,128)}, f32[8,256]{1,0:T(8,128)S(1)}) custom-call(s32[1,1]{1,0:T(1,128)} %bitcast.index_ref, f32[16,1024]{1,0:T(8,128)S(1)} %get-tuple-element.16.kept_ref, f32[1024,128]{1,0:T(8,128)S(1)} %bitcast.34, f32[32,4,128]{2,1,0:T(4,128)S(1)} %collective-permute-done.before_ref, f32[32,4,128]{2,1,0:T(4,128)S(1)} %collective-permute-done.1.after_ref), custom_call_target="tpu_custom_call" | custom-call | flops 1342177280 | bytes 1048576 | tf_op jit(solution)/shard_map/field/pallas_call | solution.py:649
  116.0 0.0 collective-permute-done.6
  116.0 0.6 fusion.3
  116.6 0.7 fusion
  117.3 1.8 %collective-permute-start.7 = (f32[56,256]{1,0:T(8,128)S(1)}, f32[56,256]{1,0:T(8,128)S(1)}, u32[]{:S(2)}, u32[]{:S(2)}) collective-permute-start(f32[56,256]{1,0:T(8,128)S(1)} %pad_maximum_fusion.13), channel_id=1, source_target_pairs={{0,16},{1,17},{2,18},{3,19},{4,20},{5,21},{6,22},{7,23},{8,24},{9,... | collective-permute-start | bytes 172040 | tf_op jit(solution)/shard_map/ppermute | solution.py:667
  119.1 3.4 %collective-permute-done.7 = f32[56,256]{1,0:T(8,128)S(1)} collective-permute-done((f32[56,256]{1,0:T(8,128)S(1)}, f32[56,256]{1,0:T(8,128)S(1)}, u32[]{:S(2)}, u32[]{:S(2)}) %collective-permute-start.7) | collective-permute-done | bytes 57376 | tf_op jit(solution)/shard_map/ppermute | solution.py:667
  122.5 3.1 %collective-permute-start.8 = (f32[104,256]{1,0:T(8,128)S(1)}, f32[104,256]{1,0:T(8,128)S(1)}, u32[]{:S(2)}, u32[]{:S(2)}) collective-permute-start(f32[104,256]{1,0:T(8,128)S(1)} %pad_maximum_fusion.10), channel_id=1, source_target_pairs={{0,8},{1,9},{2,10},{3,11},{4,12},{5,13},{6,14},{7,15},{8,0},{9,1},... | collective-permute-start | bytes 319496 | tf_op jit(solution)/shard_map/ppermute | solution.py:667
  125.6 2.7 %collective-permute-done.8 = f32[104,256]{1,0:T(8,128)S(1)} collective-permute-done((f32[104,256]{1,0:T(8,128)S(1)}, f32[104,256]{1,0:T(8,128)S(1)}, u32[]{:S(2)}, u32[]{:S(2)}) %collective-permute-start.8) | collective-permute-done | bytes 106528 | tf_op jit(solution)/shard_map/ppermute | solution.py:667
  128.4 0.4 collective-permute-start.9
  128.8 5.4 %collective-permute-done.9 = f32[200,256]{1,0:T(8,128)S(1)} collective-permute-done((f32[200,256]{1,0:T(8,128)S(1)}, f32[200,256]{1,0:T(8,128)S(1)}, u32[]{:S(2)}, u32[]{:S(2)}) %collective-permute-start.9) | collective-permute-done | bytes 204832 | tf_op jit(solution)/shard_map/ppermute | solution.py:667
  134.3 0.3 collective-permute-start.10
  134.6 10.1 %collective-permute-done.10 = f32[392,256]{1,0:T(8,128)S(1)} collective-permute-done((f32[392,256]{1,0:T(8,128)S(1)}, f32[392,256]{1,0:T(8,128)S(1)}, u32[]{:S(2)}, u32[]{:S(2)}) %collective-permute-start.10) | collective-permute-done | bytes 401440 | tf_op jit(solution)/shard_map/ppermute | solution.py:667
  144.7 0.1 slice_select_fusion.3
  144.8 0.1 pad_maximum_fusion.1
  144.9 0.1 collective-permute-start.11
  147.6 1.2 slice_divide_fusion.1
  148.8 1.2 slice_divide_fusion
  150.1 0.0 collective-permute-done.11
  150.1 0.6 fusion.1
  151.4 0.1 slice_select_fusion.1
  151.5 1.2 pad_maximum_fusion
  152.7 0.6 pad_maximum_fusion.14
  (41 shorter events, 0.4 us)
Async XLA Ops:
  3.7 0.7 copy-start.1
  4.4 1.4 copy-start.3
  5.8 0.7 copy-start.5
  6.5 0.7 copy-start.6
  7.2 0.7 copy-start.7
  7.9 0.7 copy-start.8
  8.6 32.3 %copy-start = (f32[4,32768]{1,0:T(4,128)S(1)}, f32[4,32768]{1,0:T(4,128)}, u32[]{:S(2)}) copy-start(f32[4,32768]{1,0:T(4,128)} %param.12) | copy-start | bytes 1572868
  20.1 3.1 %copy-start.11 = (f32[6,256,1280]{2,1,0:T(8,128)}, f32[6,256,1280]{2,1,0:T(8,128)S(1)}, u32[]{:S(2)}) copy-start(f32[6,256,1280]{2,1,0:T(8,128)S(1)} %get-tuple-element.20.pre_ref) | copy-start | bytes 23592964
  23.2 20.9 %copy-start.13 = (f32[256,1280]{1,0:T(8,128)}, f32[256,1280]{1,0:T(8,128)S(1)}, u32[]{:S(2)}) copy-start(f32[256,1280]{1,0:T(8,128)S(1)} %get-tuple-element.21.first_ref) | copy-start | bytes 3932164
  40.9 14.0 %copy-start.2 = (s32[256,1]{0,1:T(1,128)S(1)}, s32[256,1]{0,1:T(1,128)}, u32[]{:S(2)}) copy-start(s32[256,1]{0,1:T(1,128)} %param.13) | copy-start | bytes 3076
  40.9 14.0 %copy-start.4 = (f32[6,256,256]{2,1,0:T(8,128)S(1)}, f32[6,256,256]{2,1,0:T(8,128)}, u32[]{:S(2)}) copy-start(f32[6,256,256]{2,1,0:T(8,128)} %weights_ref.3) | copy-start | bytes 4718596
  40.9 14.0 %copy-start.9 = (f32[256]{0:T(256)S(1)}, f32[256]{0:T(256)}, u32[]{:S(2)}) copy-start(f32[256]{0:T(256)} %param.17) | copy-start | bytes 3076
  40.9 14.0 %copy-start.10 = (f32[256]{0:T(256)S(1)}, f32[256]{0:T(256)}, u32[]{:S(2)}) copy-start(f32[256]{0:T(256)} %param.18) | copy-start | bytes 3076
  44.0 10.8 %all-to-all-start.1 = ((f32[32,8,128]{2,1,0:T(8,128)}), f32[32,8,128]{2,1,0:T(8,128)S(1)}, u32[]{:S(2)}, u32[]{:S(2)}) async-start(f32[32,8,128]{2,1,0:T(8,128)} %get-tuple-element.18), calls=%async_computation.1 | async-start | bytes 262144 | tf_op jit(solution)/shard_map/all_to_all | solution.py:620
  54.8 3.2 %copy-start.12 = (f32[6,256,1280]{2,1,0:T(8,128)S(1)}, f32[6,256,1280]{2,1,0:T(8,128)}, u32[]{:S(2)}) copy-start(f32[6,256,1280]{2,1,0:T(8,128)} %copy-done.11) | copy-start | bytes 23592964
  58.1 1.3 copy-start.14
  77.4 2.5 %collective-permute-start.2 = (f32[776,256]{1,0:T(8,128)}, f32[776,256]{1,0:T(8,128)S(1)}, u32[]{:S(2)}, u32[]{:S(2)}) collective-permute-start(f32[776,256]{1,0:T(8,128)} %get-tuple-element.23), channel_id=1, source_target_pairs={{0,1},{1,0},{2,3},{3,2},{4,5},{5,4},{6,7},{7,6},{8,9},{9,8},{10,11... | collective-permute-start | bytes 2383880 | tf_op jit(solution)/shard_map/ppermute | solution.py:667
  80.1 11.5 %collective-permute-start.3 = (f32[392,256]{1,0:T(8,128)S(1)}, f32[392,256]{1,0:T(8,128)S(1)}, u32[]{:S(2)}, u32[]{:S(2)}) collective-permute-start(f32[392,256]{1,0:T(8,128)S(1)} %pad_maximum_fusion.3), channel_id=1, source_target_pairs={{0,2},{1,3},{2,0},{3,1},{4,6},{5,7},{6,4},{7,5},{8,10},{9,11},{10,... | collective-permute-start | bytes 1204232 | tf_op jit(solution)/shard_map/ppermute | solution.py:667
  91.7 6.4 %collective-permute-start.4 = (f32[200,256]{1,0:T(8,128)S(1)}, f32[200,256]{1,0:T(8,128)S(1)}, u32[]{:S(2)}, u32[]{:S(2)}) collective-permute-start(f32[200,256]{1,0:T(8,128)S(1)} %pad_maximum_fusion.6), channel_id=1, source_target_pairs={{0,4},{1,5},{2,6},{3,7},{4,0},{5,1},{6,2},{7,3},{8,12},{9,13},{10,... | collective-permute-start | bytes 614408 | tf_op jit(solution)/shard_map/ppermute | solution.py:667
  98.2 4.8 %collective-permute-start.5 = (f32[104,256]{1,0:T(8,128)S(1)}, f32[104,256]{1,0:T(8,128)S(1)}, u32[]{:S(2)}, u32[]{:S(2)}) collective-permute-start(f32[104,256]{1,0:T(8,128)S(1)} %pad_maximum_fusion.9), channel_id=1, source_target_pairs={{0,8},{1,9},{2,10},{3,11},{4,12},{5,13},{6,14},{7,15},{8,0},{9,1},... | collective-permute-start | bytes 319496 | tf_op jit(solution)/shard_map/ppermute | solution.py:667
  98.8 8.7 %collective-permute-start = (f32[32,4,128]{2,1,0:T(4,128)S(1)}, f32[32,4,128]{2,1,0:T(4,128)S(1)}, u32[]{:S(2)}, u32[]{:S(2)}) collective-permute-start(f32[32,4,128]{2,1,0:T(4,128)S(1)} %get-tuple-element.30), channel_id=1, source_target_pairs={{0,1},{1,2},{2,3},{3,4},{4,5},{5,6},{6,7},{7,8},{8,9},{9,10},{10,1... | collective-permute-start | bytes 196616 | tf_op jit(solution)/shard_map/ppermute | solution.py:624
  100.1 7.4 %collective-permute-start.1 = (f32[32,4,128]{2,1,0:T(4,128)S(1)}, f32[32,4,128]{2,1,0:T(4,128)S(1)}, u32[]{:S(2)}, u32[]{:S(2)}) collective-permute-start(f32[32,4,128]{2,1,0:T(4,128)S(1)} %get-tuple-element.29), channel_id=1, source_target_pairs={{1,0},{2,1},{3,2},{4,3},{5,4},{6,5},{7,6},{8,7},{9,8},{10,9},{11,1... | collective-permute-start | bytes 196616 | tf_op jit(solution)/shard_map/ppermute | solution.py:625
  103.0 13.0 %collective-permute-start.6 = (f32[56,256]{1,0:T(8,128)S(1)}, f32[56,256]{1,0:T(8,128)S(1)}, u32[]{:S(2)}, u32[]{:S(2)}) collective-permute-start(f32[56,256]{1,0:T(8,128)S(1)} %pad_maximum_fusion.12), channel_id=1, source_target_pairs={{0,16},{1,17},{2,18},{3,19},{4,20},{5,21},{6,22},{7,23},{8,24},{9,... | collective-permute-start | bytes 172040 | tf_op jit(solution)/shard_map/ppermute | solution.py:667
  117.3 5.1 %collective-permute-start.7 = (f32[56,256]{1,0:T(8,128)S(1)}, f32[56,256]{1,0:T(8,128)S(1)}, u32[]{:S(2)}, u32[]{:S(2)}) collective-permute-start(f32[56,256]{1,0:T(8,128)S(1)} %pad_maximum_fusion.13), channel_id=1, source_target_pairs={{0,16},{1,17},{2,18},{3,19},{4,20},{5,21},{6,22},{7,23},{8,24},{9,... | collective-permute-start | bytes 172040 | tf_op jit(solution)/shard_map/ppermute | solution.py:667
  122.5 5.8 %collective-permute-start.8 = (f32[104,256]{1,0:T(8,128)S(1)}, f32[104,256]{1,0:T(8,128)S(1)}, u32[]{:S(2)}, u32[]{:S(2)}) collective-permute-start(f32[104,256]{1,0:T(8,128)S(1)} %pad_maximum_fusion.10), channel_id=1, source_target_pairs={{0,8},{1,9},{2,10},{3,11},{4,12},{5,13},{6,14},{7,15},{8,0},{9,1},... | collective-permute-start | bytes 319496 | tf_op jit(solution)/shard_map/ppermute | solution.py:667
  128.4 5.8 %collective-permute-start.9 = (f32[200,256]{1,0:T(8,128)S(1)}, f32[200,256]{1,0:T(8,128)S(1)}, u32[]{:S(2)}, u32[]{:S(2)}) collective-permute-start(f32[200,256]{1,0:T(8,128)S(1)} %pad_maximum_fusion.7), channel_id=1, source_target_pairs={{0,4},{1,5},{2,6},{3,7},{4,0},{5,1},{6,2},{7,3},{8,12},{9,13},{10,... | collective-permute-start | bytes 614408 | tf_op jit(solution)/shard_map/ppermute | solution.py:667
  134.3 10.5 %collective-permute-start.10 = (f32[392,256]{1,0:T(8,128)S(1)}, f32[392,256]{1,0:T(8,128)S(1)}, u32[]{:S(2)}, u32[]{:S(2)}) collective-permute-start(f32[392,256]{1,0:T(8,128)S(1)} %pad_maximum_fusion.4), channel_id=1, source_target_pairs={{0,2},{1,3},{2,0},{3,1},{4,6},{5,7},{6,4},{7,5},{8,10},{9,11},{10,... | collective-permute-start | bytes 1204232 | tf_op jit(solution)/shard_map/ppermute | solution.py:667
  144.9 5.2 %collective-permute-start.11 = (f32[776,256]{1,0:T(8,128)S(1)}, f32[776,256]{1,0:T(8,128)S(1)}, u32[]{:S(2)}, u32[]{:S(2)}) collective-permute-start(f32[776,256]{1,0:T(8,128)S(1)} %pad_maximum_fusion.1), channel_id=1, source_target_pairs={{0,1},{1,0},{2,3},{3,2},{4,5},{5,4},{6,7},{7,6},{8,9},{9,8},{10,11... | collective-permute-start | bytes 2383880 | tf_op jit(solution)/shard_map/ppermute | solution.py:667

commit v2 on v1

v2 whole, which is shorter than its diff:
```python
import functools

import jax
import jax.numpy as jnp
from jax import lax
from jax.experimental import pallas as pl
from jax.experimental.pallas import tpu as pltpu
from jax.sharding import PartitionSpec as P

TILE_SIDE = 32
LANES = 128
data_weight = 1.0
smooth_weight = 0.05
AXES = ("gx", "gy")
f32 = jnp.float32
bf16 = jnp.bfloat16
NN = (((1,), (0,)), ((), ()))
NT = (((1,), (1,)), ((), ()))


def dot(a, b, dims=NN):
    return lax.dot_general(a, b, dims, preferred_element_type=f32)


def split2(x):
    hi = x.astype(bf16)
    return hi, (x - hi.astype(f32)).astype(bf16)


def split3(x):
    hi = x.astype(bf16)
    rest = x - hi.astype(f32)
    mid = rest.astype(bf16)
    return hi, mid, (rest - mid.astype(f32)).astype(bf16)


def iota(shape, dim):
    return lax.broadcasted_iota(jnp.int32, shape, dim)


def sin_cos(phase):
    turns = jnp.floor(phase * 0.6366197723675814 + 0.5)
    y = phase - turns * 1.5703125
    y = y - turns * 4.837512969970703125e-4
    y = y - turns * 7.549789954891882e-8
    quarter = turns.astype(jnp.int32)
    y2 = y * y
    s = y + y * y2 * (-1.6666654611e-1 + y2 * (8.3321608736e-3 - y2 * 1.9515295891e-4))
    c = (
        1.0
        - 0.5 * y2
        + y2
        * y2
        * (4.166664568298827e-2 + y2 * (-1.388731625493765e-3 + y2 * 2.443315711809948e-5))
    )
    odd = (quarter & 1) == 1
    sin_part = jnp.where(odd, c, s)
    cos_part = jnp.where(odd, s, c)
    sin_part = jnp.where((quarter & 2) == 2, -sin_part, sin_part)
    cos_part = jnp.where(((quarter + 1) & 2) == 2, -cos_part, cos_part)
    return sin_part, cos_part


def activations(v, z1, z2, z3, z4):
    s = 1.0 - v * v
    q = z1 * z1 + z2 * z2 + z3 * z3
    return s, q, s * z4 - 2.0 * v * s * q


def column_of(row):
    wide = jnp.broadcast_to(row.astype(f32), (8, row.shape[1]))
    return jnp.transpose(wide)[:, 0:1].astype(row.dtype)


def slot_ranks_row(owner_col, owner_row):
    n = owner_row.shape[1]
    same = (owner_col == owner_row) & (iota((n, n), 0) < iota((n, n), 1))
    return jnp.sum(jnp.where(same, 1.0, 0.0), axis=0, keepdims=True).astype(jnp.int32)


def slot_ranks_col(owner_col, owner_row):
    n = owner_row.shape[1]
    same = (owner_col == owner_row) & (iota((n, n), 1) < iota((n, n), 0))
    return jnp.sum(jnp.where(same, 1.0, 0.0), axis=1, keepdims=True).astype(jnp.int32)


ROWS = 32
FILL = 4 * 10**9
FORWARD_LIMIT, PREPARE_LIMIT, LOOKUP_LIMIT, SPREAD_LIMIT, BACKWARD_LIMIT = 64, 8, 12, 14, 58


def forward_kernel(
    devices, layers, tiles, lanes_each,
    live_ref, owner_hbm, slot_hbm, offsets_hbm, fractions_hbm, source_hbm,
    fourier_hbm, weights_hbm, biases_hbm, readout_hbm,
    request_ref, outputs_ref, pre_hbm, parts_hbm,
    pre_ref, parts_ref, weights_ref, z_ref, col_ref, bias_ref,
    owner_ref, slot_ref, offsets_ref, fractions_ref, source_ref, fourier_ref, small_ref,
    freq_ref, biases_ref, readout_ref, sems, out_sems,
):
    small_ref[...] = jnp.zeros(small_ref.shape, f32)
    fourier_ref[...] = jnp.zeros(fourier_ref.shape, f32)
    copies = [
        pltpu.make_async_copy(source, target, sems.at[k])
        for k, (source, target) in enumerate(
            (
                (owner_hbm, owner_ref), (slot_hbm, slot_ref), (offsets_hbm, offsets_ref),
                (fractions_hbm, fractions_ref), (fourier_hbm, freq_ref),
                (source_hbm, source_ref), (biases_hbm, biases_ref),
                (readout_hbm, readout_ref), (weights_hbm, weights_ref),
            )
        )
    ]
    for copy in copies:
        copy.start()
    for copy in copies[:-1]:
        copy.wait()
    fourier_ref[0:3, :] = freq_ref[...]
    small_ref[0:layers, :] = biases_ref[...]
    small_ref[layers : layers + 1, :] = readout_ref[...]
    points = slot_ref.shape[1]
    width = weights_ref.shape[1]
    streams = 5
    off = offsets_ref[...]
    fractions = fractions_ref[...]
    owner_row = owner_ref[...]
    slot = slot_ref[...]
    cells = jnp.concatenate(
        [TILE_SIDE * slot + off[0:1], TILE_SIDE * owner_row + off[1:2], off[2:3]], axis=0
    )
    position = cells.astype(f32) + fractions
    f = jnp.transpose(fourier_ref[...])
    phases = f[:, 0:1] * position[0:1] + f[:, 1:2] * position[1:2] + f[:, 2:3] * position[2:3]
    sin_part, cos_part = sin_cos(phases)
    squared = f[:, 0:1] * f[:, 0:1] + f[:, 1:2] * f[:, 1:2] + f[:, 2:3] * f[:, 2:3]
    freqs = f.shape[0]

    def put(stream, top, bottom):
        for start, value in ((0, top), (freqs, bottom)):
            lanes = pl.ds(stream * points, points)
            hi, lo = split2(value)
            parts_ref[0, pl.ds(start, freqs), lanes] = hi
            parts_ref[0, pl.ds(width + start, freqs), lanes] = lo

    put(0, sin_part, cos_part)
    for k in range(3):
        put(k + 1, cos_part * f[:, k : k + 1], -sin_part * f[:, k : k + 1])
    put(4, -sin_part * squared, -cos_part * squared)

    small_cols = jnp.transpose(small_ref[...])
    col_ref[...] = small_cols
    copies[-1].wait()

    def leave_parts(depth):
        return pltpu.make_async_copy(
            parts_ref.at[depth], parts_hbm.at[depth], out_sems.at[0, depth]
        )

    def leave_pre(depth):
        return pltpu.make_async_copy(pre_ref.at[depth], pre_hbm.at[depth], out_sems.at[1, depth])

    def layer(depth, carry):
        leave_parts(depth).start()
        w_hi, w_lo = split2(weights_ref[depth])
        for k in range(streams):
            lanes = pl.ds(k * points, points)
            h_hi = parts_ref[depth, 0:width, lanes]
            h_lo = parts_ref[depth, width:, lanes]
            z_ref[:, lanes] = dot(w_hi, h_hi) + dot(w_hi, h_lo) + dot(w_lo, h_hi)
        bias = jnp.sum(
            jnp.where(iota(small_cols.shape, 1) == depth, small_cols, 0.0), axis=1, keepdims=True
        )
        bias_ref[...] = bias

        def chunk(c, inner):
            rows = pl.ds(pl.multiple_of(c * ROWS, ROWS), ROWS)
            low_rows = pl.ds(pl.multiple_of(width + c * ROWS, ROWS), ROWS)

            def z_of(k):
                return z_ref[rows, pl.ds(k * points, points)]

            v = jnp.tanh(z_of(0) + bias_ref[rows, :])
            z1, z2, z3, z4 = z_of(1), z_of(2), z_of(3), z_of(4)
            s, _, curve = activations(v, z1, z2, z3, z4)
            for k, (kept, h) in enumerate(
                ((v, v), (z1, s * z1), (z2, s * z2), (z3, s * z3), (z4, curve))
            ):
                lanes = pl.ds(k * points, points)
                pre_ref[depth, rows, lanes] = kept
                hi, lo = split2(h)
                parts_ref[depth + 1, rows, lanes] = hi
                parts_ref[depth + 1, low_rows, lanes] = lo
            return inner

        lax.fori_loop(0, width // ROWS, chunk, 0)
        leave_pre(depth).start()
        return carry

    lax.fori_loop(0, layers, layer, 0)

    def readout_chunk(c, totals):
        rows = pl.ds(pl.multiple_of(c * ROWS, ROWS), ROWS)
        v, z1, z2, z3, z4 = [
            pre_ref[layers - 1, rows, pl.ds(k * points, points)] for k in range(streams)
        ]
        s, _, curve = activations(v, z1, z2, z3, z4)
        r = col_ref[rows, layers : layers + 1]
        hs = (v, s * z1, s * z2, s * z3, curve)
        return tuple(t + jnp.sum(r * h, axis=0, keepdims=True) for t, h in zip(totals, hs))

    zero = tuple(jnp.zeros((1, points), f32) for _ in range(streams))
    out = lax.fori_loop(0, width // ROWS, readout_chunk, zero)
    outputs = jnp.concatenate(list(out) + [jnp.zeros((3, points), f32)], axis=0)
    outputs_ref[...] = outputs

    live = jnp.where(iota((1, points), 1) < live_ref[0, 0], 1.0, 0.0)
    row_index = ((off[0:1] * (TILE_SIDE // 4) + off[1:2] // 4) * tiles + slot).astype(f32)
    lane_index = ((off[1:2] % 4) * TILE_SIDE + off[2:3]).astype(f32)
    comps = [
        row_index, lane_index, fractions[0:1], fractions[1:2], fractions[2:3],
        outputs[1:2], outputs[2:3], outputs[3:4], outputs[4:5], source_ref[...], live,
    ]
    to_owner = owner_row == iota((devices, points), 0)
    ranks = slot_ranks_col(column_of(owner_row), owner_row)
    place = jnp.where(ranks == iota((points, LANES), 1), 1.0, 0.0).astype(bf16)
    spread = jnp.concatenate([jnp.where(to_owner, c, 0.0) for c in comps], axis=0)
    a, b, c = split3(spread)
    packed = dot(a, place) + dot(b, place) + dot(c, place)
    rows_each, lane_groups = request_ref.shape[1], LANES // lanes_each
    for j in range(rows_each):
        total = jnp.zeros((devices, LANES), f32)
        for m in range(lane_groups):
            k = rows_each * m + j
            if k < len(comps):
                part = packed[k * devices : (k + 1) * devices]
                total = total + (pltpu.roll(part, lanes_each * m, 1) if m else part)
        request_ref[:, j, :] = total
    for depth in range(layers):
        leave_parts(depth).wait()
        leave_pre(depth).wait()


def owner_kernel(
    devices, tiles, lanes_each,
    received_ref, window_hi, window_lo,
    response_ref, kept_ref,
    x_ref,
):
    cells = window_hi.shape[1]
    group = LANES // lanes_each
    blocks = devices // group
    slots = blocks * LANES
    rows_each = received_ref.shape[1]
    lane_block = iota((rows_each * group, LANES), 1) // lanes_each
    for j in range(blocks):
        total = None
        for g in range(group):
            part = received_ref[group * j + g]
            moved = jnp.concatenate(
                [
                    pltpu.roll(part, lanes_each * ((g - m) % group), 1) if g != m else part
                    for m in range(group)
                ],
                axis=0,
            )
            total = moved if total is None else jnp.where(lane_block == g, moved, total)
        x_ref[:, j * LANES : (j + 1) * LANES] = total

    step = 2 * LANES
    for start in range(0, slots, step):
        x = x_ref[:, start : start + step]
        rows = x[0:1].astype(jnp.int32)
        place = x[1:2].astype(jnp.int32)
        hot = jnp.where(iota((cells, step), 0) == rows, 1.0, 0.0).astype(bf16)
        found = dot(window_hi[...], hot) + dot(window_lo[...], hot)
        y_mod = place // TILE_SIDE
        z_cell = place % TILE_SIDE
        z_iota = iota((TILE_SIDE, step), 0)
        at_z = (z_iota == z_cell, z_iota == z_cell + 1)
        corner = {}
        for a in range(2):
            parts = [found[a * 160 + TILE_SIDE * j : a * 160 + TILE_SIDE * (j + 1)] for j in range(5)]
            for b in range(2):
                rows_y = jnp.where(y_mod == 0, parts[b], 0.0)
                for j in range(1, 4):
                    rows_y = jnp.where(y_mod == j, parts[j + b], rows_y)
                for c in range(2):
                    corner[a, b, c] = jnp.sum(
                        jnp.where(at_z[c], rows_y, 0.0), axis=0, keepdims=True
                    )
        fr = [x[2:3], x[3:4], x[4:5]]
        w = [(1.0 - t, t) for t in fr]
        sign = (-1.0, 1.0)
        values = [jnp.zeros((1, step), f32) for _ in range(4)]
        for (a, b, c), k in corner.items():
            values[0] = values[0] + w[0][a] * w[1][b] * w[2][c] * k
            values[1] = values[1] + sign[a] * w[1][b] * w[2][c] * k
            values[2] = values[2] + w[0][a] * sign[b] * w[2][c] * k
            values[3] = values[3] + w[0][a] * w[1][b] * sign[c] * k
        du = [x[5:6], x[6:7], x[7:8]]
        lap = x[8:9]
        residual = (
            -(values[0] * lap + (values[1] * du[0] + values[2] * du[1] + values[3] * du[2]))
            - x[9:10]
        )
        scaled = 2.0 * x[10:11] * residual
        zeros = jnp.zeros((4, step), f32)
        answer = jnp.concatenate(values + [zeros], axis=0)
        sub = iota((8, LANES), 0)
        lane_of = iota((8, LANES), 1) // lanes_each
        for j in range(step // LANES):
            block = start // LANES + j
            part = answer[:, j * LANES : (j + 1) * LANES]
            turned = [pltpu.roll(part, lanes_each * k, 1) if k else part for k in range(group)]
            for g in range(group):
                picked = jnp.zeros((8, LANES), f32)
                for c in range(4):
                    picked = jnp.where((sub == c) & (lane_of == c), turned[(c - g) % group], picked)
                response_ref[group * block + g] = jnp.sum(picked, axis=0, keepdims=True)
        kept_ref[:, start : start + step] = jnp.concatenate(
            [x[0:5], -scaled * lap, -scaled * du[0], -scaled * du[1], -scaled * du[2]]
            + [jnp.zeros((7, step), f32)],
            axis=0,
        )


def spread_kernel(
    tiles,
    kept_ref, smooth_ref,
    grad_ref,
    hot_ref, c_hi, c_lo, sum_ref, part_ref,
):
    cells = smooth_ref.shape[0]
    slots = kept_ref.shape[1]
    plane = (TILE_SIDE // 4) * tiles
    step = 2 * LANES
    for start in range(0, slots, step):
        lanes = slice(start, start + step)
        x = kept_ref[:, lanes]
        rows = x[0:1].astype(jnp.int32)
        place = x[1:2].astype(jnp.int32)
        hot_ref[:, lanes] = jnp.where(iota((cells, step), 0) == rows, 1.0, 0.0).astype(bf16)
        y_mod = place // TILE_SIDE
        z_cell = place % TILE_SIDE
        z_iota = iota((TILE_SIDE, step), 0)
        at_z = (z_iota == z_cell, z_iota == z_cell + 1)
        w = [(1.0 - x[k : k + 1], x[k : k + 1]) for k in (2, 3, 4)]
        g = [x[k : k + 1] for k in (5, 6, 7, 8)]
        sign = (-1.0, 1.0)
        for a in range(2):
            along = []
            for b in range(2):
                pair = []
                for c in range(2):
                    pair.append(
                        g[0] * w[0][a] * w[1][b] * w[2][c]
                        + g[1] * sign[a] * w[1][b] * w[2][c]
                        + g[2] * w[0][a] * sign[b] * w[2][c]
                        + g[3] * w[0][a] * w[1][b] * sign[c]
                    )
                along.append(jnp.where(at_z[0], pair[0], 0.0) + jnp.where(at_z[1], pair[1], 0.0))
            for j in range(5):
                value = jnp.where(y_mod == j, along[0], 0.0) + jnp.where(
                    y_mod == j - 1, along[1], 0.0
                )
                hi, lo = split2(value)
                at = a * 128 + TILE_SIDE * j if j < 4 else 256 + a * TILE_SIDE
                c_hi[at : at + TILE_SIDE, lanes] = hi
                c_lo[at : at + TILE_SIDE, lanes] = lo
    sum_ref[...] = jnp.zeros(sum_ref.shape, f32)
    block = 2 * LANES
    for start in range(0, cells, block):
        hot = hot_ref[start : start + block, :]
        part = dot(hot, c_hi[...], NT) + dot(hot, c_lo[...], NT)
        part_ref[start : start + block, :] = part
    sum_ref[0:cells, :] = smooth_ref[...] + part_ref[:, 0:128]
    sum_ref[plane : plane + cells, :] += part_ref[:, 128:256]
    low = slice(0, TILE_SIDE)
    sum_ref[tiles : tiles + cells, low] += part_ref[:, 256 : 256 + TILE_SIDE]
    sum_ref[plane + tiles : plane + tiles + cells, low] += part_ref[
        :, 256 + TILE_SIDE : 256 + 2 * TILE_SIDE
    ]
    grad_ref[...] = sum_ref[0:cells, :]


def prepare_kernel(
    devices, tiles,
    index_ref, field_ref, before_ref, after_ref,
    grad_ref, energy_ref, window_hi, window_lo,
    padded_ref,
):
    cells = field_ref.shape[0]
    plane = (TILE_SIDE // 4) * tiles
    padded_ref[0:cells, :] = field_ref[...]
    padded_ref[cells:, :] = jnp.zeros((padded_ref.shape[0] - cells, LANES), f32)
    for a in range(2):
        base = a * plane
        main = jnp.transpose(padded_ref[base : base + cells, :])
        hi, lo = split2(main)
        window_hi[a * 160 : a * 160 + 128, :] = hi
        window_lo[a * 160 : a * 160 + 128, :] = lo
        extra = jnp.transpose(padded_ref[base + tiles : base + tiles + cells, :])[0:TILE_SIDE]
        hi, lo = split2(extra)
        window_hi[a * 160 + 128 : a * 160 + 160, :] = hi
        window_lo[a * 160 + 128 : a * 160 + 160, :] = lo

    me = index_ref[0, 0]
    row = iota((plane, LANES), 0)
    lane = iota((plane, LANES), 1)
    z_inner = (lane % TILE_SIDE) < TILE_SIDE - 1
    first_row = row < tiles
    last_row = row >= plane - tiles
    low_lane = lane < TILE_SIDE
    high_lane = lane >= LANES - TILE_SIDE
    has_after = jnp.where(me < devices - 1, 1.0, 0.0)
    has_before = jnp.where(me > 0, 1.0, 0.0)
    after_mask = jnp.where(last_row & high_lane, has_after, 1.0)
    before_mask = jnp.where(first_row & low_lane, has_before, 1.0)
    next_tile = (row % tiles) < tiles - 1
    prev_tile = (row % tiles) > 0

    def load(x):
        return field_ref[pl.ds(pl.multiple_of(x * plane, plane), plane), :]

    def plane_step(x, energy):
        here = load(x)
        diff_z = jnp.where(z_inner, pltpu.roll(here, LANES - 1, 1) - here, 0.0)
        grad = pltpu.roll(diff_z, 1, 1) - diff_z
        energy = energy + diff_z * diff_z
        above = jnp.concatenate([here[tiles:], after_ref[x]], axis=0)
        up = pltpu.roll(jnp.where(low_lane, above, here), LANES - TILE_SIDE, 1)
        below = jnp.concatenate([before_ref[x], here[: plane - tiles]], axis=0)
        down = pltpu.roll(jnp.where(high_lane, below, here), TILE_SIDE, 1)
        diff_up = (up - here) * after_mask
        diff_down = (here - down) * before_mask
        grad = grad + diff_down - diff_up
        energy = energy + diff_down * diff_down
        first = x == 0
        last = x == TILE_SIDE - 1
        nxt = load(jnp.where(last, 0, x + 1))
        nxt = jnp.where(last, pltpu.roll(nxt, plane - 1, 0), nxt)
        prv = load(jnp.where(first, TILE_SIDE - 1, x - 1))
        prv = jnp.where(first, pltpu.roll(prv, 1, 0), prv)
        diff_next = jnp.where(jnp.logical_not(last) | next_tile, nxt - here, 0.0)
        diff_prev = jnp.where(jnp.logical_not(first) | prev_tile, here - prv, 0.0)
        grad = grad + diff_prev - diff_next
        energy = energy + diff_prev * diff_prev
        at = pl.ds(pl.multiple_of(x * plane, plane), plane)
        grad_ref[at, :] = 2.0 * smooth_weight * grad
        return energy

    energy = lax.fori_loop(0, TILE_SIDE, plane_step, jnp.zeros((plane, LANES), f32))
    energy_ref[...] = jnp.sum(energy, axis=0, keepdims=True)


def backward_kernel(
    devices, layers, lanes_each,
    scalars_ref, owner_row_ref, source_ref, observed_ref, response_ref, energy_ref,
    outputs_ref, readout_ref, weights_hbm, pre_hbm, parts_hbm,
    keep_a_ref, keep_b_ref, send_a_ref, send_b_ref,
    pre_ref, parts_ref, weights_ref, bar_ref, zh_ref, zl_ref, col_ref, cols_ref, sems,
):
    def fetch_pre(k):
        return pltpu.make_async_copy(pre_hbm.at[k], pre_ref.at[k], sems.at[0, k])

    def fetch_parts(k):
        return pltpu.make_async_copy(parts_hbm.at[k], parts_ref.at[k], sems.at[1, k])

    weight_copy = pltpu.make_async_copy(weights_hbm, weights_ref, sems.at[0, layers])
    fetch_pre(layers - 1).start()
    weight_copy.start()
    fetch_parts(layers - 1).start()
    points = owner_row_ref.shape[1]
    width = weights_hbm.shape[1]
    owner_row = owner_row_ref[...]
    ranks = slot_ranks_row(column_of(owner_row), owner_row)
    picked = jnp.where(ranks == iota((lanes_each, points), 0), 1.0, 0.0)
    from_owner = jnp.where(owner_row == iota((devices, points), 0), 1.0, 0.0).astype(bf16)
    a, b, c = split3(jnp.transpose(response_ref[...])[0 : 4 * lanes_each])
    wide = dot(a, from_owner) + dot(b, from_owner) + dot(c, from_owner)
    values = [
        jnp.sum(picked * wide[k * lanes_each : (k + 1) * lanes_each], axis=0, keepdims=True)
        for k in range(4)
    ]
    outputs = outputs_ref[...]
    out = [outputs[k : k + 1] for k in range(5)]
    live = jnp.where(iota((1, points), 1) < scalars_ref[0, 0], 1.0, 0.0)
    misfit = out[0] - observed_ref[...]
    residual = (
        -(values[0] * out[4] + (values[1] * out[1] + values[2] * out[2] + values[3] * out[3]))
        - source_ref[...]
    )
    scaled = 2.0 * live * residual
    out_grad = [2.0 * data_weight * live * misfit] + [-scaled * values[k] for k in (1, 2, 3, 0)]
    residual_sum = jnp.sum(live * residual * residual, axis=1, keepdims=True)
    misfit_sum = jnp.sum(live * misfit * misfit, axis=1, keepdims=True)
    col_ref[...] = column_of(readout_ref[...])
    cols_ref[...] = jnp.zeros(cols_ref.shape, f32)
    lane8 = iota((ROWS, cols_ref.shape[1]), 1)
    chunks = width // ROWS

    def rows_of(c):
        return pl.ds(pl.multiple_of(c * ROWS, ROWS), ROWS)

    def pre_of(depth, rows):
        return [pre_ref[depth, rows, pl.ds(k * points, points)] for k in range(5)]

    def readout_chunk(c, carry):
        rows = rows_of(c)
        v, z1, z2, z3, z4 = pre_of(layers - 1, rows)
        s, _, curve = activations(v, z1, z2, z3, z4)
        total = out_grad[0] * v + out_grad[1] * (s * z1) + out_grad[2] * (s * z2)
        total = total + out_grad[3] * (s * z3) + out_grad[4] * curve
        grad = jnp.sum(total, axis=1, keepdims=True)
        cols_ref[rows, :] += jnp.where(lane8 == layers, grad, 0.0)
        r = col_ref[rows, :]
        for k in range(5):
            bar_ref[rows, pl.ds(k * points, points)] = r * out_grad[k]
        return carry

    fetch_pre(layers - 1).wait()
    lax.fori_loop(0, chunks, readout_chunk, 0)
    weight_copy.wait()
    mine = scalars_ref[0, 1]
    half = layers // 2

    def layer(step, carry):
        depth = layers - 1 - step
        before = jnp.maximum(depth - 1, 0)

        @pl.when(depth > 0)
        def _():
            fetch_pre(before).start()
            fetch_parts(before).start()

        def bars(c, inner):
            rows = rows_of(c)
            v, z1, z2, z3, z4 = pre_of(depth, rows)
            b = [bar_ref[rows, pl.ds(k * points, points)] for k in range(5)]
            s = 1.0 - v * v
            q = z1 * z1 + z2 * z2 + z3 * z3
            slope = b[1] * z1 + b[2] * z2 + b[3] * z3
            v4c = 4.0 * v * b[4]
            z_bar = [
                s
                * (
                    b[0]
                    - 2.0 * v * slope
                    + b[4] * (q * (4.0 * v * v - 2.0 * s) - 2.0 * v * z4)
                ),
                s * (b[1] - v4c * z1),
                s * (b[2] - v4c * z2),
                s * (b[3] - v4c * z3),
                s * b[4],
            ]
            grad = jnp.sum(z_bar[0], axis=1, keepdims=True)
            cols_ref[rows, :] += jnp.where(lane8 == depth, grad, 0.0)
            for k in range(5):
                lanes = pl.ds(k * points, points)
                hi, lo = split2(z_bar[k])
                zh_ref[rows, lanes] = hi
                zl_ref[rows, lanes] = lo
            return inner

        lax.fori_loop(0, chunks, bars, 0)
        fetch_parts(depth).wait()
        h_hi, h_lo = parts_ref[depth, 0:width], parts_ref[depth, width:]
        z_hi, z_lo = zh_ref[...], zl_ref[...]
        grad = dot(z_hi, h_hi, NT) + dot(z_hi, h_lo, NT) + dot(z_lo, h_hi, NT)
        upper = (depth >= half).astype(jnp.int32)
        part = width // 2
        at = pl.ds(pl.multiple_of((depth - upper * half) * part, part), part)

        @pl.when(mine == upper)
        def _():
            keep_a_ref[at, :] = grad[:part]
            keep_b_ref[at, :] = grad[part:]

        @pl.when(mine != upper)
        def _():
            send_a_ref[at, :] = grad[:part]
            send_b_ref[at, :] = grad[part:]

        @pl.when(depth > 0)
        def _():
            w_hi, w_lo = split2(jnp.transpose(weights_ref[depth]))
            for k in range(5):
                lanes = pl.ds(k * points, points)
                z_hi = zh_ref[:, lanes]
                bar_ref[:, lanes] = dot(w_hi, z_hi) + dot(w_hi, zl_ref[:, lanes]) + dot(w_lo, z_hi)
            fetch_pre(before).wait()

        return carry

    lax.fori_loop(0, layers, layer, 0)
    small = jnp.transpose(cols_ref[...])
    lane = iota((1, width), 1)
    count = jnp.full((1, 1), scalars_ref[0, 0], jnp.int32).astype(f32)
    last = jnp.where(lane == 0, residual_sum, 0.0) + jnp.where(lane == 1, misfit_sum, 0.0)
    energy = jnp.sum(energy_ref[...], axis=1, keepdims=True)
    last = last + jnp.where(lane == 2, count, 0.0) + jnp.where(lane == 3, energy, 0.0)
    small = jnp.where(iota(small.shape, 0) == small.shape[0] - 1, last, small)
    keep_b_ref[half * width // 2 :, :] = small
    send_b_ref[half * width // 2 :, :] = small


def vmem():
    return pl.BlockSpec(memory_space=pltpu.VMEM)


def smem():
    return pl.BlockSpec(memory_space=pltpu.SMEM)


def hbm():
    return pl.BlockSpec(memory_space=pltpu.HBM)


def call(kernel, name, specs, out_shapes, scratch, flops, limit, outs=None):
    return pl.pallas_call(
        kernel,
        name=name,
        out_shape=out_shapes,
        in_specs=specs,
        out_specs=outs or jax.tree.map(lambda _: vmem(), out_shapes),
        scratch_shapes=scratch,
        compiler_params=pltpu.CompilerParams(vmem_limit_bytes=min(limit << 20, 67043328)),
        cost_estimate=pl.CostEstimate(flops=flops, bytes_accessed=1 << 20, transcendentals=0),
    )


def shape(*dims, dtype=f32):
    return jax.ShapeDtypeStruct(dims, dtype)


def on_device(
    conductivity, owner_rank, tile_slot, offsets, fractions, source, observed, live_count,
    fourier, weights, biases, readout,
):
    devices = lax.axis_size(AXES)
    index = lax.axis_index(AXES)
    points = tile_slot.shape[0]
    tiles = conductivity.shape[0]
    layers, width = biases.shape
    capacity = (2 * points + devices - 1) // devices + 1
    lanes_each = 1 << (capacity - 1).bit_length()
    lanes_each = max(lanes_each, 2 * LANES // devices)
    rows_each = 1 << (-(-11 * lanes_each // LANES) - 1).bit_length()
    slots = devices * lanes_each
    cells = conductivity.size // LANES
    plane = (TILE_SIDE // 4) * tiles
    wide = 5 * points

    owner_row = owner_rank.reshape(1, points)
    source_row = source.reshape(1, points)
    readout_row = readout.reshape(1, width)
    field = conductivity.reshape(tiles, cells // tiles, LANES).transpose(1, 0, 2)
    field = field.reshape(cells, LANES)

    request, outputs, pre, parts = call(
        functools.partial(forward_kernel, devices, layers, tiles, lanes_each),
        "forward",
        [smem()] + [hbm()] * 9,
        (
            shape(devices, rows_each, LANES), shape(8, points),
            shape(layers, width, wide), shape(layers, 2 * width, wide, dtype=bf16),
        ),
        [
            pltpu.VMEM((layers, width, wide), f32),
            pltpu.VMEM((layers + 1, 2 * width, wide), bf16),
            pltpu.VMEM((layers, width, width), f32),
            pltpu.VMEM((width, wide), f32),
            pltpu.VMEM((width, 8), f32),
            pltpu.VMEM((width, 1), f32),
            pltpu.VMEM((1, points), jnp.int32),
            pltpu.VMEM((1, points), jnp.int32),
            pltpu.VMEM((3, points), jnp.int32),
            pltpu.VMEM((3, points), f32),
            pltpu.VMEM((1, points), f32),
            pltpu.VMEM((8, fourier.shape[0]), f32),
            pltpu.VMEM((8, width), f32),
            pltpu.VMEM((3, fourier.shape[0]), f32),
            pltpu.VMEM((layers, width), f32),
            pltpu.VMEM((1, width), f32),
            pltpu.SemaphoreType.DMA((9,)),
            pltpu.SemaphoreType.DMA((2, layers)),
        ],
        6 * 2 * layers * width * width * wide,
        FORWARD_LIMIT,
        outs=(vmem(), vmem(), hbm(), hbm()),
    )(
        live_count.reshape(1, 1), owner_row, tile_slot.reshape(1, points), offsets, fractions,
        source_row, fourier.T, weights, biases, readout_row,
    )
    received = lax.all_to_all(request, AXES, split_axis=0, concat_axis=0, tiled=True)

    planes, _ = lax.optimization_barrier((field.reshape(TILE_SIDE, plane, LANES), outputs))
    up = [(i, i + 1) for i in range(devices - 1)]
    down = [(j, i) for i, j in up]
    before = lax.ppermute(planes[:, plane - tiles :, :], AXES, up)
    after = lax.ppermute(planes[:, :tiles, :], AXES, down)
    smooth, energy, window_hi, window_lo = call(
        functools.partial(prepare_kernel, devices, tiles),
        "prepare",
        [smem()] + [vmem()] * 3,
        (
            shape(cells, LANES), shape(1, LANES),
            shape(320, cells, dtype=bf16), shape(320, cells, dtype=bf16),
        ),
        [pltpu.VMEM((cells + 2 * plane, LANES), f32)],
        FILL,
        PREPARE_LIMIT,
    )(index.reshape(1, 1), field, before, after)

    response, kept = call(
        functools.partial(owner_kernel, devices, tiles, lanes_each),
        "lookup",
        [vmem()] * 3,
        (shape(devices, 1, LANES), shape(16, slots)),
        [pltpu.VMEM((16, slots), f32)],
        2 * 640 * cells * slots,
        LOOKUP_LIMIT,
    )(received, window_hi, window_lo)
    answered = lax.all_to_all(response, AXES, split_axis=0, concat_axis=0, tiled=True)
    grad = call(
        functools.partial(spread_kernel, tiles),
        "spread",
        [vmem()] * 2,
        shape(cells, LANES),
        [
            pltpu.VMEM((cells, slots), bf16),
            pltpu.VMEM((320, slots), bf16),
            pltpu.VMEM((320, slots), bf16),
            pltpu.VMEM((cells + 2 * plane, LANES), f32),
            pltpu.VMEM((cells, 320), f32),
        ],
        FILL,
        SPREAD_LIMIT,
    )(kept, smooth)
    answered, grad = lax.optimization_barrier((answered, grad))

    part_rows = layers * width // 4
    scalars = jnp.stack([live_count[0], index % 2]).reshape(1, 2)
    keep_a, keep_b, send_a, send_b = call(
        functools.partial(backward_kernel, devices, layers, lanes_each),
        "backward",
        [smem()] + [vmem()] * 7 + [hbm()] * 3,
        tuple(shape(rows, width) for rows in (part_rows, part_rows + 8) * 2),
        [
            pltpu.VMEM((layers, width, wide), f32),
            pltpu.VMEM((layers, 2 * width, wide), bf16),
            pltpu.VMEM((layers, width, width), f32),
            pltpu.VMEM((width, wide), f32),
            pltpu.VMEM((width, wide), bf16),
            pltpu.VMEM((width, wide), bf16),
            pltpu.VMEM((width, 1), f32),
            pltpu.VMEM((width, 8), f32),
            pltpu.SemaphoreType.DMA((2, layers + 1)),
        ],
        12 * 2 * layers * width * width * wide,
        BACKWARD_LIMIT,
    )(
        scalars, owner_row, source_row, observed.reshape(1, points),
        answered.reshape(devices, LANES), energy, outputs, readout_row, weights, pre, parts,
    )

    even = [1 << k for k in range(devices.bit_length() - 1)]
    odd = list(even)
    for k in range(1, len(odd) - 1, 2):
        odd[k], odd[k + 1] = odd[k + 1], odd[k]

    def exchange(value, step):
        bits = (even[step], odd[step])
        return lax.ppermute(value, AXES, [(i, i ^ bits[i % 2]) for i in range(devices)])

    def upper_of(step):
        bit = jnp.where(index % 2 == 1, odd[step], even[step])
        return (index & bit) != 0

    main = [keep_a + exchange(send_a, 0), keep_b + exchange(send_b, 0)]
    main[1], extra = main[1][:part_rows], main[1][part_rows:]
    for step in range(1, len(even)):
        half = main[0].shape[0] // 2
        upper = upper_of(step)
        outgoing = [jnp.where(upper, m[:half], m[half:]) for m in main]
        outgoing[1] = jnp.concatenate([outgoing[1], extra], axis=0)
        arrived = [exchange(value, step) for value in outgoing]
        main = [jnp.where(upper, m[half:], m[:half]) + a[:half] for m, a in zip(main, arrived)]
        extra = extra + arrived[1][half:]
    scale = 1.0 / extra[7, 2]
    main = [m * scale for m in main]
    sums = extra[7]
    losses = jnp.stack(
        [sums[0] * scale, sums[1] * scale, sums[3] / (devices * conductivity.size)]
    )
    bias_grad, readout_grad = extra[:layers] * scale, extra[layers] * scale
    for step in reversed(range(len(even))):
        upper = upper_of(step)
        arrived = [exchange(m, step) for m in main]
        main = [
            jnp.concatenate([jnp.where(upper, a, m), jnp.where(upper, m, a)], axis=0)
            for m, a in zip(main, arrived)
        ]
        if step == len(even) - 1:
            main[1], losses, bias_grad, readout_grad = lax.optimization_barrier(
                (main[1], losses, bias_grad, readout_grad)
            )
    weight_grad = jnp.concatenate([m.reshape(layers, width // 2, width) for m in main], axis=1)
    conductivity_grad = grad.reshape(cells // tiles, tiles, LANES).transpose(1, 0, 2)
    return (
        conductivity_grad.reshape(conductivity.shape),
        weight_grad,
        bias_grad,
        readout_grad,
        losses,
    )


def solution(mesh):
    in_specs = (
        P(AXES, None), P(AXES, None), P(AXES), P(None, AXES), P(None, AXES), P(AXES), P(AXES),
        P(AXES), P(), P(), P(), P(),
    )
    out_specs = (P(AXES, None), P(), P(), P(), P())
    return jax.shard_map(
        on_device, mesh=mesh, in_specs=in_specs, out_specs=out_specs, check_vma=False
    )
```

time: 154 us -> 129 us (0.84)
  starting transfers between devices: 17.2 us -> 35.9 us
  blocking collectives: 17.7 us -> 0 us
  waiting for transfers between devices: 50.4 us -> 36 us
  local copies, waits for them, and re-layouts: 14.7 us -> 3.81 us
  Pallas kernels: 41.1 us -> 42.9 us
  other arithmetic: 7.17 us -> 5.56 us
    all_to_all x1 -> x0, blocking collectives: 17.7 us -> none  [on_device(): lax.all_to_all(request, AXES, split_axis=0, concat_axis=0, tiled=True)]
    ppermute x10 -> x20, waiting for transfers between devices: 42.3 us -> 30.4 us  [exchange(): lax.ppermute(value, AXES, [(i, i ^ bits[i % 2]) for i in range(devices)])]
    unnamed x32 -> x8, local copies, waits for them, and re-layouts: 14 us -> 2.15 us
    all_to_all x0 -> x1, starting transfers between devices: none -> 7.32 us  [on_device(): lax.all_to_all(request, AXES, split_axis=0, concat_axis=0, tiled=True)]
    all_to_all x1, starting transfers between devices: 2.58 us -> 8.92 us  [on_device(): lax.all_to_all(response, AXES, split_axis=0, concat_axis=0, tiled=True)]
    all_to_all x1, waiting for transfers between devices: 8.11 us -> 3.33 us  [on_device(): lax.all_to_all(response, AXES, split_axis=0, concat_axis=0, tiled=True)]
    ppermute x10 -> x20, starting transfers between devices: 12 us -> 16.2 us  [exchange(): lax.ppermute(value, AXES, [(i, i ^ bits[i % 2]) for i in range(devices)])]
    div x3 -> x0, other arithmetic: 3.12 us -> none  [the longest x1 1.25 us: on_device(): extra[:layers] / live_total]
  transfers between devices with their start and end apart: 13 -> 24, of which waited for: 9 -> 18; matrix products, arithmetic and copies ran while one was open for 2% -> 5% of each run, Pallas kernels for 6% -> 7%
where the time goes in v2:
time: 129 us; the launch traced here: 128 us
  Pallas kernels  42.9 us (33%)
  waiting for transfers between devices  36 us (28%)
  starting transfers between devices  35.9 us (28%)
  other arithmetic  5.56 us (4%)
  between operations  4.31 us (3%)
  local copies, waits for them, and re-layouts  3.81 us (3%)
    ppermute x20, waiting for transfers between devices, exchange(): lax.ppermute(value, AXES, [(i, i ^ bits[i % 2]) for i in range(devices)])  30.4 us
    pallas_call x1, Pallas kernels, on_device(): call(functools.partial(backward_kernel, devices, layers, lanes_each), 'ba...  17.6 us
    ppermute x20, starting transfers between devices, exchange(): lax.ppermute(value, AXES, [(i, i ^ bits[i % 2]) for i in range(devices)])  16.2 us
    pallas_call x1, Pallas kernels, on_device(): call(functools.partial(forward_kernel, devices, layers, tiles, lanes_each...  13.2 us
    all_to_all x1, starting transfers between devices, on_device(): lax.all_to_all(response, AXES, split_axis=0, concat_axis=0, tiled=True)  8.92 us
    all_to_all x1, starting transfers between devices, on_device(): lax.all_to_all(request, AXES, split_axis=0, concat_axis=0, tiled=True)  7.32 us
    pallas_call x1, Pallas kernels, on_device(): call(functools.partial(prepare_kernel, devices, tiles), 'prepare', [smem(...  5.37 us
    pallas_call x1, Pallas kernels, on_device(): call(functools.partial(spread_kernel, tiles), 'spread', [vmem()] * 2, sha...  3.77 us
  transfers between devices with their start and end apart: 24, of which 18 were waited for; matrix products, arithmetic and copies ran while one was open for 5% of the time, Pallas kernels for 7%

profile of v2, /device:TPU:0, one launch (start us, length us, event | category | flops | bytes accessed | tf_op | source)
XLA Modules:
  0.0 128.4 jit_solution(13253725975054866790)
XLA Ops:
  1.3 13.2 %forward.1 = (f32[32,4,128]{2,1,0:T(4,128)}, f32[8,256]{1,0:T(8,128)}, f32[6,256,1280]{2,1,0:T(8,128)}, bf16[6,512,1280]{2,1,0:T(8,128)(2,1)}) custom-call(s32[1,1]{1,0:T(1,128)} %bitcast.33.live_ref, s32[1,256]{1,0:T(1,128)} %bitcast.42, s32[1,256]{1,0:T(1,128)} %bitcast.41, s32[3,256]{1,0:T(4,128)} %offsets_hbm.1, f32[3,256]{1,0:T(4,128)} %fractions_hbm.1, ...), custom_call_target="tpu_custom_call" | custom-call | flops 6039797760 | bytes 1048576 | tf_op jit(solution)/shard_map/forward/pallas_call | solution.py:660
  14.5 7.3 %all-to-all-start = ((f32[32,4,128]{2,1,0:T(4,128)}), f32[32,4,128]{2,1,0:T(4,128)S(1)}, u32[]{:S(2)}, u32[]{:S(2)}) async-start(f32[32,4,128]{2,1,0:T(4,128)} %get-tuple-element.26), calls=%async_computation | async-start | bytes 131072 | tf_op jit(solution)/shard_map/all_to_all | solution.py:695
  21.9 1.0 fusion.1
  22.9 2.2 %collective-permute-start = (f32[32,4,128]{2,1,0:T(4,128)S(1)}, f32[32,4,128]{2,1,0:T(4,128)S(1)}, u32[]{:S(2)}, u32[]{:S(2)}) collective-permute-start(f32[32,4,128]{2,1,0:T(4,128)S(1)} %get-tuple-element.52), channel_id=1, source_target_pairs={{0,1},{1,2},{2,3},{3,4},{4,5},{5,6},{6,7},{7,8},{8,9},{9,10},{10,1... | collective-permute-start | bytes 196616 | tf_op jit(solution)/shard_map/ppermute | solution.py:700
  25.0 1.3 %collective-permute-start.1 = (f32[32,4,128]{2,1,0:T(4,128)S(1)}, f32[32,4,128]{2,1,0:T(4,128)S(1)}, u32[]{:S(2)}, u32[]{:S(2)}) collective-permute-start(f32[32,4,128]{2,1,0:T(4,128)S(1)} %get-tuple-element.51), channel_id=1, source_target_pairs={{1,0},{2,1},{3,2},{4,3},{5,4},{6,5},{7,6},{8,7},{9,8},{10,9},{11,1... | collective-permute-start | bytes 196616 | tf_op jit(solution)/shard_map/ppermute | solution.py:701
  26.3 0.7 add_bitcast_fusion.scalars_ref
  27.0 2.3 %collective-permute-done.1.after_ref = f32[32,4,128]{2,1,0:T(4,128)S(1)} collective-permute-done((f32[32,4,128]{2,1,0:T(4,128)S(1)}, f32[32,4,128]{2,1,0:T(4,128)S(1)}, u32[]{:S(2)}, u32[]{:S(2)}) %collective-permute-start.1) | collective-permute-done | bytes 65568 | tf_op jit(solution)/shard_map/ppermute | solution.py:701
  29.3 1.0 copy-done
  30.3 5.4 %prepare.1 = (f32[1024,128]{1,0:T(8,128)S(1)}, f32[1,128]{1,0:T(1,128)S(1)}, bf16[320,1024]{1,0:T(8,128)(2,1)S(1)}, bf16[320,1024]{1,0:T(8,128)(2,1)S(1)}) custom-call(s32[1,1]{1,0:T(1,128)} %bitcast.6.index_ref, f32[1024,128]{1,0:T(8,128)S(1)} %bitcast.35, f32[32,4,128]{2,1,0:T(4,128)S(1)} %collective-permute-done.before_ref, ...), custom_call_target="tpu_custom_call" | custom-call | flops 4000000000 | bytes 1048576 | tf_op jit(solution)/shard_map/prepare/pallas_call | solution.py:702
  35.7 0.0 copy-start.1
  35.7 0.5 copy-done.1
  36.2 2.9 %lookup.1 = (f32[32,1,128]{2,1,0:T(1,128)}, f32[16,1024]{1,0:T(8,128)S(1)}) custom-call(f32[32,4,128]{2,1,0:T(4,128)S(1)} %all-to-all-done.received_ref, bf16[320,1024]{1,0:T(8,128)(2,1)S(1)} %get-tuple-element.29.window_hi, bf16[320,1024]{1,0:T(8,128)(2,1)S(1)} %get-tuple-element.30.window_lo), custom_call_target="tpu_custom_call" | custom-call | flops 1342177280 | bytes 1048576 | tf_op jit(solution)/shard_map/lookup/pallas_call | solution.py:715
  39.1 8.9 %all-to-all-start.1 = ((f32[32,1,128]{2,1,0:T(1,128)}), f32[32,1,128]{2,1,0:T(1,128)S(1)}, u32[]{:S(2)}, u32[]{:S(2)}) async-start(f32[32,1,128]{2,1,0:T(1,128)} %get-tuple-element.31), calls=%async_computation.1 | async-start | bytes 32768 | tf_op jit(solution)/shard_map/all_to_all | solution.py:724
  48.0 3.8 %spread.1 = f32[1024,128]{1,0:T(8,128)} custom-call(f32[16,1024]{1,0:T(8,128)S(1)} %get-tuple-element.32.kept_ref, f32[1024,128]{1,0:T(8,128)S(1)} %get-tuple-element.33.smooth_ref), custom_call_target="tpu_custom_call" | custom-call | flops 4000000000 | bytes 1048576 | tf_op jit(solution)/shard_map/spread/pallas_call | solution.py:725
  51.8 3.3 %all-to-all-done.1 = f32[32,1,128]{2,1,0:T(1,128)S(1)} async-done(((f32[32,1,128]{2,1,0:T(1,128)}), f32[32,1,128]{2,1,0:T(1,128)S(1)}, u32[]{:S(2)}, u32[]{:S(2)}) %all-to-all-start.1) | async-done | bytes 16416 | tf_op jit(solution)/shard_map/all_to_all | solution.py:724
  55.1 0.6 copy-done.3
  55.7 17.6 %backward.1 = (f32[384,256]{1,0:T(8,128)}, f32[392,256]{1,0:T(8,128)}, f32[384,256]{1,0:T(8,128)}, f32[392,256]{1,0:T(8,128)}) custom-call(s32[1,2]{1,0:T(1,128)} %add_bitcast_fusion.scalars_ref, s32[1,256]{1,0:T(1,128)} %bitcast.43, f32[1,256]{1,0:T(1,128)} %bitcast.45, f32[1,256]{1,0:T(1,128)} %bitcast.48, f32[32,128]{1,0:T(8,128)} %bitcast.38, ...), custom_call_target="tpu_custom_call" | custom-call | flops 12079595520 | bytes 1048576 | tf_op jit(solution)/shard_map/backward/pallas_call | solution.py:744
  73.4 0.0 copy-start.2
  73.4 0.1 collective-permute-start.2
  73.4 0.5 collective-permute-start.7
  73.9 1.4 %collective-permute-done.2 = f32[384,256]{1,0:T(8,128)S(1)} collective-permute-done((f32[384,256]{1,0:T(8,128)}, f32[384,256]{1,0:T(8,128)S(1)}, u32[]{:S(2)}, u32[]{:S(2)}) %collective-permute-start.2) | collective-permute-done | bytes 393248 | tf_op jit(solution)/shard_map/ppermute | solution.py:774
  75.4 1.0 add.60
  76.5 0.6 collective-permute-start.3
  77.1 0.1 add.65
  77.2 1.6 %collective-permute-start.8 = (f32[200,256]{1,0:T(8,128)S(1)}, f32[200,256]{1,0:T(8,128)S(1)}, u32[]{:S(2)}, u32[]{:S(2)}) collective-permute-start(f32[200,256]{1,0:T(8,128)S(1)} %pad_maximum_fusion.5), channel_id=1, source_target_pairs={{0,2},{1,5},{2,0},{3,7},{4,6},{5,1},{6,4},{7,3},{8,10},{9,13},{10,... | collective-permute-start | bytes 614408 | tf_op jit(solution)/shard_map/ppermute | solution.py:774
  78.8 3.4 %collective-permute-done.3 = f32[192,256]{1,0:T(8,128)S(1)} collective-permute-done((f32[192,256]{1,0:T(8,128)S(1)}, f32[192,256]{1,0:T(8,128)S(1)}, u32[]{:S(2)}, u32[]{:S(2)}) %collective-permute-start.3) | collective-permute-done | bytes 196640 | tf_op jit(solution)/shard_map/ppermute | solution.py:774
  82.2 0.6 collective-permute-start.4
  82.9 1.7 %collective-permute-done.8 = f32[200,256]{1,0:T(8,128)S(1)} collective-permute-done((f32[200,256]{1,0:T(8,128)S(1)}, f32[200,256]{1,0:T(8,128)S(1)}, u32[]{:S(2)}, u32[]{:S(2)}) %collective-permute-start.8) | collective-permute-done | bytes 204832 | tf_op jit(solution)/shard_map/ppermute | solution.py:774
  84.7 0.6 collective-permute-start.9
  85.3 1.7 %collective-permute-done.4 = f32[96,256]{1,0:T(8,128)S(1)} collective-permute-done((f32[96,256]{1,0:T(8,128)S(1)}, f32[96,256]{1,0:T(8,128)S(1)}, u32[]{:S(2)}, u32[]{:S(2)}) %collective-permute-start.4) | collective-permute-done | bytes 98336 | tf_op jit(solution)/shard_map/ppermute | solution.py:774
  87.0 0.6 collective-permute-start.5
  87.6 1.8 %collective-permute-done.9 = f32[104,256]{1,0:T(8,128)S(1)} collective-permute-done((f32[104,256]{1,0:T(8,128)S(1)}, f32[104,256]{1,0:T(8,128)S(1)}, u32[]{:S(2)}, u32[]{:S(2)}) %collective-permute-start.9) | collective-permute-done | bytes 106528 | tf_op jit(solution)/shard_map/ppermute | solution.py:774
  89.5 0.6 collective-permute-start.10
  90.1 1.1 collective-permute-done.5
  91.3 2.5 %collective-permute-done.10 = f32[56,256]{1,0:T(8,128)S(1)} collective-permute-done((f32[56,256]{1,0:T(8,128)S(1)}, f32[56,256]{1,0:T(8,128)S(1)}, u32[]{:S(2)}, u32[]{:S(2)}) %collective-permute-start.10) | collective-permute-done | bytes 57376 | tf_op jit(solution)/shard_map/ppermute | solution.py:774
  93.8 0.7 collective-permute-start.11
  94.4 2.3 %collective-permute-start.6 = (f32[24,256]{1,0:T(8,128)S(1)}, f32[24,256]{1,0:T(8,128)S(1)}, u32[]{:S(2)}, u32[]{:S(2)}) collective-permute-start(f32[24,256]{1,0:T(8,128)S(1)} %slice_select_fusion.7), channel_id=1, source_target_pairs={{0,16},{1,9},{2,18},{3,11},{4,20},{5,13},{6,22},{7,15},{8,24},{9,1... | collective-permute-start | bytes 73736 | tf_op jit(solution)/shard_map/ppermute | solution.py:774
  96.8 2.5 %collective-permute-done.11 = f32[32,256]{1,0:T(8,128)S(1)} collective-permute-done((f32[32,256]{1,0:T(8,128)S(1)}, f32[32,256]{1,0:T(8,128)S(1)}, u32[]{:S(2)}, u32[]{:S(2)}) %collective-permute-start.11) | collective-permute-done | bytes 32800 | tf_op jit(solution)/shard_map/ppermute | solution.py:774
  99.3 0.7 fusion.2
  100.6 0.6 slice_multiply_fusion
  101.2 0.6 slice_multiply_fusion.1
  103.1 3.0 %collective-permute-start.12 = (f32[24,256]{1,0:T(8,128)S(1)}, f32[24,256]{1,0:T(8,128)S(1)}, u32[]{:S(2)}, u32[]{:S(2)}) collective-permute-start(f32[24,256]{1,0:T(8,128)S(1)} %add_multiply_fusion), channel_id=1, source_target_pairs={{0,16},{1,9},{2,18},{3,11},{4,20},{5,13},{6,22},{7,15},{8,24},{9,1... | collective-permute-start | bytes 73736 | tf_op jit(solution)/shard_map/ppermute | solution.py:774
  106.8 0.6 pad_maximum_fusion.15
  107.4 0.1 collective-permute-start.18
  107.5 0.6 collective-permute-done.12
  108.1 1.4 %collective-permute-start.13 = (f32[48,256]{1,0:T(8,128)S(1)}, f32[48,256]{1,0:T(8,128)S(1)}, u32[]{:S(2)}, u32[]{:S(2)}) collective-permute-start(f32[48,256]{1,0:T(8,128)S(1)} %pad_maximum_fusion.12), channel_id=1, source_target_pairs={{0,8},{1,17},{2,10},{3,19},{4,12},{5,21},{6,14},{7,23},{8,0},{9,25... | collective-permute-start | bytes 147464 | tf_op jit(solution)/shard_map/ppermute | solution.py:774
  109.6 2.0 %collective-permute-done.18 = f32[48,256]{1,0:T(8,128)S(1)} collective-permute-done((f32[48,256]{1,0:T(8,128)S(1)}, f32[48,256]{1,0:T(8,128)S(1)}, u32[]{:S(2)}, u32[]{:S(2)}) %collective-permute-start.18) | collective-permute-done | bytes 49184 | tf_op jit(solution)/shard_map/ppermute | solution.py:774
  111.6 0.3 collective-permute-start.19
  111.9 0.4 collective-permute-done.13
  112.3 1.4 %collective-permute-start.14 = (f32[96,256]{1,0:T(8,128)S(1)}, f32[96,256]{1,0:T(8,128)S(1)}, u32[]{:S(2)}, u32[]{:S(2)}) collective-permute-start(f32[96,256]{1,0:T(8,128)S(1)} %pad_maximum_fusion.9), channel_id=1, source_target_pairs={{0,4},{1,3},{2,6},{3,1},{4,0},{5,7},{6,2},{7,5},{8,12},{9,11},{10,... | collective-permute-start | bytes 294920 | tf_op jit(solution)/shard_map/ppermute | solution.py:774
  113.8 3.5 %collective-permute-done.19 = f32[96,256]{1,0:T(8,128)S(1)} collective-permute-done((f32[96,256]{1,0:T(8,128)S(1)}, f32[96,256]{1,0:T(8,128)S(1)}, u32[]{:S(2)}, u32[]{:S(2)}) %collective-permute-start.19) | collective-permute-done | bytes 98336 | tf_op jit(solution)/shard_map/ppermute | solution.py:774
  117.3 0.3 collective-permute-start.20
  117.7 0.9 collective-permute-done.14
  118.6 1.2 collective-permute-start.15
  119.8 3.3 %collective-permute-done.20 = f32[192,256]{1,0:T(8,128)S(1)} collective-permute-done((f32[192,256]{1,0:T(8,128)S(1)}, f32[192,256]{1,0:T(8,128)S(1)}, u32[]{:S(2)}, u32[]{:S(2)}) %collective-permute-start.20) | collective-permute-done | bytes 196640 | tf_op jit(solution)/shard_map/ppermute | solution.py:774
  123.2 0.1 collective-permute-start.21
  123.2 2.0 %collective-permute-done.15 = f32[192,256]{1,0:T(8,128)S(1)} collective-permute-done((f32[192,256]{1,0:T(8,128)S(1)}, f32[192,256]{1,0:T(8,128)S(1)}, u32[]{:S(2)}, u32[]{:S(2)}) %collective-permute-start.15) | collective-permute-done | bytes 196640 | tf_op jit(solution)/shard_map/ppermute | solution.py:774
  125.3 0.1 collective-permute-start.16
  125.3 0.1 broadcast_select_fusion.1
  125.4 0.1 pad_maximum_fusion.2
  125.5 1.6 %collective-permute-done.16 = f32[384,256]{1,0:T(8,128)S(1)} collective-permute-done((f32[384,256]{1,0:T(8,128)S(1)}, f32[384,256]{1,0:T(8,128)S(1)}, u32[]{:S(2)}, u32[]{:S(2)}) %collective-permute-start.16) | collective-permute-done | bytes 393248 | tf_op jit(solution)/shard_map/ppermute | solution.py:774
  127.0 0.1 broadcast_select_fusion.3
  127.1 0.1 pad_maximum_fusion.1
  127.2 1.2 pad_maximum_fusion
  (51 shorter events, 0.6 us)
Async XLA Ops:
  14.5 21.7 %all-to-all-start = ((f32[32,4,128]{2,1,0:T(4,128)}), f32[32,4,128]{2,1,0:T(4,128)S(1)}, u32[]{:S(2)}, u32[]{:S(2)}) async-start(f32[32,4,128]{2,1,0:T(4,128)} %get-tuple-element.26), calls=%async_computation | async-start | bytes 131072 | tf_op jit(solution)/shard_map/all_to_all | solution.py:695
  22.9 4.2 %collective-permute-start = (f32[32,4,128]{2,1,0:T(4,128)S(1)}, f32[32,4,128]{2,1,0:T(4,128)S(1)}, u32[]{:S(2)}, u32[]{:S(2)}) collective-permute-start(f32[32,4,128]{2,1,0:T(4,128)S(1)} %get-tuple-element.52), channel_id=1, source_target_pairs={{0,1},{1,2},{2,3},{3,4},{4,5},{5,6},{6,7},{7,8},{8,9},{9,10},{10,1... | collective-permute-start | bytes 196616 | tf_op jit(solution)/shard_map/ppermute | solution.py:700
  25.0 4.3 %collective-permute-start.1 = (f32[32,4,128]{2,1,0:T(4,128)S(1)}, f32[32,4,128]{2,1,0:T(4,128)S(1)}, u32[]{:S(2)}, u32[]{:S(2)}) collective-permute-start(f32[32,4,128]{2,1,0:T(4,128)S(1)} %get-tuple-element.51), channel_id=1, source_target_pairs={{1,0},{2,1},{3,2},{4,3},{5,4},{6,5},{7,6},{8,7},{9,8},{10,9},{11,1... | collective-permute-start | bytes 196616 | tf_op jit(solution)/shard_map/ppermute | solution.py:701
  29.3 1.0 copy-start
  35.7 0.5 copy-start.1
  39.1 16.0 %all-to-all-start.1 = ((f32[32,1,128]{2,1,0:T(1,128)}), f32[32,1,128]{2,1,0:T(1,128)S(1)}, u32[]{:S(2)}, u32[]{:S(2)}) async-start(f32[32,1,128]{2,1,0:T(1,128)} %get-tuple-element.31), calls=%async_computation.1 | async-start | bytes 32768 | tf_op jit(solution)/shard_map/all_to_all | solution.py:724
  55.1 0.6 copy-start.3
  73.4 3.7 %copy-start.2 = (f32[392,256]{1,0:T(8,128)S(1)}, f32[392,256]{1,0:T(8,128)}, u32[]{:S(2)}) copy-start(f32[392,256]{1,0:T(8,128)} %get-tuple-element.41) | copy-start | bytes 1204228
  73.4 2.0 %collective-permute-start.2 = (f32[384,256]{1,0:T(8,128)}, f32[384,256]{1,0:T(8,128)S(1)}, u32[]{:S(2)}, u32[]{:S(2)}) collective-permute-start(f32[384,256]{1,0:T(8,128)} %get-tuple-element.40), channel_id=1, source_target_pairs={{0,1},{1,0},{2,3},{3,2},{4,5},{5,4},{6,7},{7,6},{8,9},{9,8},{10,11... | collective-permute-start | bytes 1179656 | tf_op jit(solution)/shard_map/ppermute | solution.py:774
  73.4 3.6 %collective-permute-start.7 = (f32[392,256]{1,0:T(8,128)}, f32[392,256]{1,0:T(8,128)S(1)}, u32[]{:S(2)}, u32[]{:S(2)}) collective-permute-start(f32[392,256]{1,0:T(8,128)} %get-tuple-element.42), channel_id=1, source_target_pairs={{0,1},{1,0},{2,3},{3,2},{4,5},{5,4},{6,7},{7,6},{8,9},{9,8},{10,11... | collective-permute-start | bytes 1204232 | tf_op jit(solution)/shard_map/ppermute | solution.py:774
  76.5 5.7 %collective-permute-start.3 = (f32[192,256]{1,0:T(8,128)S(1)}, f32[192,256]{1,0:T(8,128)S(1)}, u32[]{:S(2)}, u32[]{:S(2)}) collective-permute-start(f32[192,256]{1,0:T(8,128)S(1)} %slice_select_fusion.1), channel_id=1, source_target_pairs={{0,2},{1,5},{2,0},{3,7},{4,6},{5,1},{6,4},{7,3},{8,10},{9,13},{10,... | collective-permute-start | bytes 589832 | tf_op jit(solution)/shard_map/ppermute | solution.py:774
  77.2 7.4 %collective-permute-start.8 = (f32[200,256]{1,0:T(8,128)S(1)}, f32[200,256]{1,0:T(8,128)S(1)}, u32[]{:S(2)}, u32[]{:S(2)}) collective-permute-start(f32[200,256]{1,0:T(8,128)S(1)} %pad_maximum_fusion.5), channel_id=1, source_target_pairs={{0,2},{1,5},{2,0},{3,7},{4,6},{5,1},{6,4},{7,3},{8,10},{9,13},{10,... | collective-permute-start | bytes 614408 | tf_op jit(solution)/shard_map/ppermute | solution.py:774
  82.2 4.7 %collective-permute-start.4 = (f32[96,256]{1,0:T(8,128)S(1)}, f32[96,256]{1,0:T(8,128)S(1)}, u32[]{:S(2)}, u32[]{:S(2)}) collective-permute-start(f32[96,256]{1,0:T(8,128)S(1)} %slice_select_fusion.3), channel_id=1, source_target_pairs={{0,4},{1,3},{2,6},{3,1},{4,0},{5,7},{6,2},{7,5},{8,12},{9,11},{10,... | collective-permute-start | bytes 294920 | tf_op jit(solution)/shard_map/ppermute | solution.py:774
  84.7 4.8 %collective-permute-start.9 = (f32[104,256]{1,0:T(8,128)S(1)}, f32[104,256]{1,0:T(8,128)S(1)}, u32[]{:S(2)}, u32[]{:S(2)}) collective-permute-start(f32[104,256]{1,0:T(8,128)S(1)} %pad_maximum_fusion.8), channel_id=1, source_target_pairs={{0,4},{1,3},{2,6},{3,1},{4,0},{5,7},{6,2},{7,5},{8,12},{9,11},{10,... | collective-permute-start | bytes 319496 | tf_op jit(solution)/shard_map/ppermute | solution.py:774
  87.0 4.3 %collective-permute-start.5 = (f32[48,256]{1,0:T(8,128)S(1)}, f32[48,256]{1,0:T(8,128)S(1)}, u32[]{:S(2)}, u32[]{:S(2)}) collective-permute-start(f32[48,256]{1,0:T(8,128)S(1)} %slice_select_fusion.5), channel_id=1, source_target_pairs={{0,8},{1,17},{2,10},{3,19},{4,12},{5,21},{6,14},{7,23},{8,0},{9,25... | collective-permute-start | bytes 147464 | tf_op jit(solution)/shard_map/ppermute | solution.py:774
  89.5 4.2 %collective-permute-start.10 = (f32[56,256]{1,0:T(8,128)S(1)}, f32[56,256]{1,0:T(8,128)S(1)}, u32[]{:S(2)}, u32[]{:S(2)}) collective-permute-start(f32[56,256]{1,0:T(8,128)S(1)} %pad_maximum_fusion.11), channel_id=1, source_target_pairs={{0,8},{1,17},{2,10},{3,19},{4,12},{5,21},{6,14},{7,23},{8,0},{9,25... | collective-permute-start | bytes 172040 | tf_op jit(solution)/shard_map/ppermute | solution.py:774
  93.8 5.5 %collective-permute-start.11 = (f32[32,256]{1,0:T(8,128)S(1)}, f32[32,256]{1,0:T(8,128)S(1)}, u32[]{:S(2)}, u32[]{:S(2)}) collective-permute-start(f32[32,256]{1,0:T(8,128)S(1)} %pad_maximum_fusion.14), channel_id=1, source_target_pairs={{0,16},{1,9},{2,18},{3,11},{4,20},{5,13},{6,22},{7,15},{8,24},{9,1... | collective-permute-start | bytes 98312 | tf_op jit(solution)/shard_map/ppermute | solution.py:774
  94.4 8.7 %collective-permute-start.6 = (f32[24,256]{1,0:T(8,128)S(1)}, f32[24,256]{1,0:T(8,128)S(1)}, u32[]{:S(2)}, u32[]{:S(2)}) collective-permute-start(f32[24,256]{1,0:T(8,128)S(1)} %slice_select_fusion.7), channel_id=1, source_target_pairs={{0,16},{1,9},{2,18},{3,11},{4,20},{5,13},{6,22},{7,15},{8,24},{9,1... | collective-permute-start | bytes 73736 | tf_op jit(solution)/shard_map/ppermute | solution.py:774
  101.8 5.5 %collective-permute-start.17 = (f32[24,256]{1,0:T(8,128)S(1)}, f32[24,256]{1,0:T(8,128)S(1)}, u32[]{:S(2)}, u32[]{:S(2)}) collective-permute-start(f32[24,256]{1,0:T(8,128)S(1)} %fusion), channel_id=1, source_target_pairs={{0,16},{1,9},{2,18},{3,11},{4,20},{5,13},{6,22},{7,15},{8,24},{9,1... | collective-permute-start | bytes 73736 | tf_op jit(solution)/shard_map/ppermute | solution.py:774
  103.1 5.0 %collective-permute-start.12 = (f32[24,256]{1,0:T(8,128)S(1)}, f32[24,256]{1,0:T(8,128)S(1)}, u32[]{:S(2)}, u32[]{:S(2)}) collective-permute-start(f32[24,256]{1,0:T(8,128)S(1)} %add_multiply_fusion), channel_id=1, source_target_pairs={{0,16},{1,9},{2,18},{3,11},{4,20},{5,13},{6,22},{7,15},{8,24},{9,1... | collective-permute-start | bytes 73736 | tf_op jit(solution)/shard_map/ppermute | solution.py:774
  107.4 4.2 %collective-permute-start.18 = (f32[48,256]{1,0:T(8,128)S(1)}, f32[48,256]{1,0:T(8,128)S(1)}, u32[]{:S(2)}, u32[]{:S(2)}) collective-permute-start(f32[48,256]{1,0:T(8,128)S(1)} %pad_maximum_fusion.13), channel_id=1, source_target_pairs={{0,8},{1,17},{2,10},{3,19},{4,12},{5,21},{6,14},{7,23},{8,0},{9,25... | collective-permute-start | bytes 147464 | tf_op jit(solution)/shard_map/ppermute | solution.py:774
  108.1 4.2 %collective-permute-start.13 = (f32[48,256]{1,0:T(8,128)S(1)}, f32[48,256]{1,0:T(8,128)S(1)}, u32[]{:S(2)}, u32[]{:S(2)}) collective-permute-start(f32[48,256]{1,0:T(8,128)S(1)} %pad_maximum_fusion.12), channel_id=1, source_target_pairs={{0,8},{1,17},{2,10},{3,19},{4,12},{5,21},{6,14},{7,23},{8,0},{9,25... | collective-permute-start | bytes 147464 | tf_op jit(solution)/shard_map/ppermute | solution.py:774
  111.6 5.7 %collective-permute-start.19 = (f32[96,256]{1,0:T(8,128)S(1)}, f32[96,256]{1,0:T(8,128)S(1)}, u32[]{:S(2)}, u32[]{:S(2)}) collective-permute-start(f32[96,256]{1,0:T(8,128)S(1)} %pad_maximum_fusion.10), channel_id=1, source_target_pairs={{0,4},{1,3},{2,6},{3,1},{4,0},{5,7},{6,2},{7,5},{8,12},{9,11},{10,... | collective-permute-start | bytes 294920 | tf_op jit(solution)/shard_map/ppermute | solution.py:774
  112.3 6.2 %collective-permute-start.14 = (f32[96,256]{1,0:T(8,128)S(1)}, f32[96,256]{1,0:T(8,128)S(1)}, u32[]{:S(2)}, u32[]{:S(2)}) collective-permute-start(f32[96,256]{1,0:T(8,128)S(1)} %pad_maximum_fusion.9), channel_id=1, source_target_pairs={{0,4},{1,3},{2,6},{3,1},{4,0},{5,7},{6,2},{7,5},{8,12},{9,11},{10,... | collective-permute-start | bytes 294920 | tf_op jit(solution)/shard_map/ppermute | solution.py:774
  117.3 5.7 %collective-permute-start.20 = (f32[192,256]{1,0:T(8,128)S(1)}, f32[192,256]{1,0:T(8,128)S(1)}, u32[]{:S(2)}, u32[]{:S(2)}) collective-permute-start(f32[192,256]{1,0:T(8,128)S(1)} %pad_maximum_fusion.7), channel_id=1, source_target_pairs={{0,2},{1,5},{2,0},{3,7},{4,6},{5,1},{6,4},{7,3},{8,10},{9,13},{10,... | collective-permute-start | bytes 589832 | tf_op jit(solution)/shard_map/ppermute | solution.py:774
  118.6 6.6 %collective-permute-start.15 = (f32[192,256]{1,0:T(8,128)S(1)}, f32[192,256]{1,0:T(8,128)S(1)}, u32[]{:S(2)}, u32[]{:S(2)}) collective-permute-start(f32[192,256]{1,0:T(8,128)S(1)} %pad_maximum_fusion.6), channel_id=1, source_target_pairs={{0,2},{1,5},{2,0},{3,7},{4,6},{5,1},{6,4},{7,3},{8,10},{9,13},{10,... | collective-permute-start | bytes 589832 | tf_op jit(solution)/shard_map/ppermute | solution.py:774
  123.2 2.2 %collective-permute-start.21 = (f32[384,256]{1,0:T(8,128)S(1)}, f32[384,256]{1,0:T(8,128)S(1)}, u32[]{:S(2)}, u32[]{:S(2)}) collective-permute-start(f32[384,256]{1,0:T(8,128)S(1)} %pad_maximum_fusion.4), channel_id=1, source_target_pairs={{0,1},{1,0},{2,3},{3,2},{4,5},{5,4},{6,7},{7,6},{8,9},{9,8},{10,11... | collective-permute-start | bytes 1179656 | tf_op jit(solution)/shard_map/ppermute | solution.py:774
  125.3 1.8 %collective-permute-start.16 = (f32[384,256]{1,0:T(8,128)S(1)}, f32[384,256]{1,0:T(8,128)S(1)}, u32[]{:S(2)}, u32[]{:S(2)}) collective-permute-start(f32[384,256]{1,0:T(8,128)S(1)} %pad_maximum_fusion.3), channel_id=1, source_target_pairs={{0,1},{1,0},{2,3},{3,2},{4,5},{5,4},{6,7},{7,6},{8,9},{9,8},{10,11... | collective-permute-start | bytes 1179656 | tf_op jit(solution)/shard_map/ppermute | solution.py:774

commit v3 on v2

--- a/solution.py
+++ b/solution.py
@@ -84,7 +84,7 @@
     return jnp.sum(jnp.where(same, 1.0, 0.0), axis=1, keepdims=True).astype(jnp.int32)
 
 
-ROWS = 32
+FORWARD_ROWS, ROWS = 256, 64
 FILL = 4 * 10**9
 FORWARD_LIMIT, PREPARE_LIMIT, LOOKUP_LIMIT, SPREAD_LIMIT, BACKWARD_LIMIT = 64, 8, 12, 14, 58
 
@@ -173,8 +173,8 @@
         bias_ref[...] = bias
 
         def chunk(c, inner):
-            rows = pl.ds(pl.multiple_of(c * ROWS, ROWS), ROWS)
-            low_rows = pl.ds(pl.multiple_of(width + c * ROWS, ROWS), ROWS)
+            rows = pl.ds(pl.multiple_of(c * FORWARD_ROWS, FORWARD_ROWS), FORWARD_ROWS)
+            low_rows = pl.ds(pl.multiple_of(width + c * FORWARD_ROWS, FORWARD_ROWS), FORWARD_ROWS)
 
             def z_of(k):
                 return z_ref[rows, pl.ds(k * points, points)]
@@ -192,14 +192,14 @@
                 parts_ref[depth + 1, low_rows, lanes] = lo
             return inner
 
-        lax.fori_loop(0, width // ROWS, chunk, 0)
+        lax.fori_loop(0, width // FORWARD_ROWS, chunk, 0)
         leave_pre(depth).start()
         return carry
 
     lax.fori_loop(0, layers, layer, 0)
 
     def readout_chunk(c, totals):
-        rows = pl.ds(pl.multiple_of(c * ROWS, ROWS), ROWS)
+        rows = pl.ds(pl.multiple_of(c * FORWARD_ROWS, FORWARD_ROWS), FORWARD_ROWS)
         v, z1, z2, z3, z4 = [
             pre_ref[layers - 1, rows, pl.ds(k * points, points)] for k in range(streams)
         ]
@@ -209,7 +209,7 @@
         return tuple(t + jnp.sum(r * h, axis=0, keepdims=True) for t, h in zip(totals, hs))
 
     zero = tuple(jnp.zeros((1, points), f32) for _ in range(streams))
-    out = lax.fori_loop(0, width // ROWS, readout_chunk, zero)
+    out = lax.fori_loop(0, width // FORWARD_ROWS, readout_chunk, zero)
     outputs = jnp.concatenate(list(out) + [jnp.zeros((3, points), f32)], axis=0)
     outputs_ref[...] = outputs
 
@@ -324,13 +324,13 @@
         )
 
 
-def spread_kernel(
-    tiles,
-    kept_ref, smooth_ref,
-    grad_ref,
+def field_kernel(
+    devices, tiles,
+    index_ref, kept_ref, field_ref, before_ref, after_ref,
+    grad_ref, energy_ref,
     hot_ref, c_hi, c_lo, sum_ref, part_ref,
 ):
-    cells = smooth_ref.shape[0]
+    cells = field_ref.shape[0]
     slots = kept_ref.shape[1]
     plane = (TILE_SIDE // 4) * tiles
     step = 2 * LANES
@@ -373,36 +373,13 @@
         hot = hot_ref[start : start + block, :]
         part = dot(hot, c_hi[...], NT) + dot(hot, c_lo[...], NT)
         part_ref[start : start + block, :] = part
-    sum_ref[0:cells, :] = smooth_ref[...] + part_ref[:, 0:128]
+    sum_ref[0:cells, :] = part_ref[:, 0:128]
     sum_ref[plane : plane + cells, :] += part_ref[:, 128:256]
     low = slice(0, TILE_SIDE)
     sum_ref[tiles : tiles + cells, low] += part_ref[:, 256 : 256 + TILE_SIDE]
     sum_ref[plane + tiles : plane + tiles + cells, low] += part_ref[
         :, 256 + TILE_SIDE : 256 + 2 * TILE_SIDE
     ]
-    grad_ref[...] = sum_ref[0:cells, :]
-
-
-def prepare_kernel(
-    devices, tiles,
-    index_ref, field_ref, before_ref, after_ref,
-    grad_ref, energy_ref, window_hi, window_lo,
-    padded_ref,
-):
-    cells = field_ref.shape[0]
-    plane = (TILE_SIDE // 4) * tiles
-    padded_ref[0:cells, :] = field_ref[...]
-    padded_ref[cells:, :] = jnp.zeros((padded_ref.shape[0] - cells, LANES), f32)
-    for a in range(2):
-        base = a * plane
-        main = jnp.transpose(padded_ref[base : base + cells, :])
-        hi, lo = split2(main)
-        window_hi[a * 160 : a * 160 + 128, :] = hi
-        window_lo[a * 160 : a * 160 + 128, :] = lo
-        extra = jnp.transpose(padded_ref[base + tiles : base + tiles + cells, :])[0:TILE_SIDE]
-        hi, lo = split2(extra)
-        window_hi[a * 160 + 128 : a * 160 + 160, :] = hi
-        window_lo[a * 160 + 128 : a * 160 + 160, :] = lo
 
     me = index_ref[0, 0]
     row = iota((plane, LANES), 0)
@@ -446,16 +423,43 @@
         grad = grad + diff_prev - diff_next
         energy = energy + diff_prev * diff_prev
         at = pl.ds(pl.multiple_of(x * plane, plane), plane)
-        grad_ref[at, :] = 2.0 * smooth_weight * grad
+        grad_ref[at, :] = sum_ref[at, :] + 2.0 * smooth_weight * grad
         return energy
 
-    energy = lax.fori_loop(0, TILE_SIDE, plane_step, jnp.zeros((plane, LANES), f32))
+    energy = lax.fori_loop(
+        0, TILE_SIDE, plane_step, jnp.zeros((plane, LANES), f32), unroll=4
+    )
     energy_ref[...] = jnp.sum(energy, axis=0, keepdims=True)
+
+
+def prepare_kernel(
+    tiles,
+    field_ref,
+    window_hi, window_lo, first_ref, last_ref,
+    padded_ref,
+):
+    cells = field_ref.shape[0]
+    plane = (TILE_SIDE // 4) * tiles
+    for x in range(TILE_SIDE):
+        first_ref[x] = field_ref[x * plane : x * plane + tiles, :]
+        last_ref[x] = field_ref[(x + 1) * plane - tiles : (x + 1) * plane, :]
+    padded_ref[0:cells, :] = field_ref[...]
+    padded_ref[cells:, :] = jnp.zeros((padded_ref.shape[0] - cells, LANES), f32)
+    for a in range(2):
+        base = a * plane
+        main = jnp.transpose(padded_ref[base : base + cells, :])
+        hi, lo = split2(main)
+        window_hi[a * 160 : a * 160 + 128, :] = hi
+        window_lo[a * 160 : a * 160 + 128, :] = lo
+        extra = jnp.transpose(padded_ref[base + tiles : base + tiles + cells, :])[0:TILE_SIDE]
+        hi, lo = split2(extra)
+        window_hi[a * 160 + 128 : a * 160 + 160, :] = hi
+        window_lo[a * 160 + 128 : a * 160 + 160, :] = lo
 
 
 def backward_kernel(
     devices, layers, lanes_each,
-    scalars_ref, owner_row_ref, source_ref, observed_ref, response_ref, energy_ref,
+    live_ref, index_ref, owner_row_ref, source_ref, observed_ref, response_ref, energy_ref,
     outputs_ref, readout_ref, weights_hbm, pre_hbm, parts_hbm,
     keep_a_ref, keep_b_ref, send_a_ref, send_b_ref,
     pre_ref, parts_ref, weights_ref, bar_ref, zh_ref, zl_ref, col_ref, cols_ref, sems,
@@ -484,7 +488,7 @@
     ]
     outputs = outputs_ref[...]
     out = [outputs[k : k + 1] for k in range(5)]
-    live = jnp.where(iota((1, points), 1) < scalars_ref[0, 0], 1.0, 0.0)
+    live = jnp.where(iota((1, points), 1) < live_ref[0, 0], 1.0, 0.0)
     misfit = out[0] - observed_ref[...]
     residual = (
         -(values[0] * out[4] + (values[1] * out[1] + values[2] * out[2] + values[3] * out[3]))
@@ -521,7 +525,7 @@
     fetch_pre(layers - 1).wait()
     lax.fori_loop(0, chunks, readout_chunk, 0)
     weight_copy.wait()
-    mine = scalars_ref[0, 1]
+    mine = index_ref[0, 0] % 2
     half = layers // 2
 
     def layer(step, carry):
@@ -562,7 +566,7 @@
                 zl_ref[rows, lanes] = lo
             return inner
 
-        lax.fori_loop(0, chunks, bars, 0)
+        lax.fori_loop(0, chunks, bars, 0, unroll=2)
         fetch_parts(depth).wait()
         h_hi, h_lo = parts_ref[depth, 0:width], parts_ref[depth, width:]
         z_hi, z_lo = zh_ref[...], zl_ref[...]
@@ -595,7 +599,7 @@
     lax.fori_loop(0, layers, layer, 0)
     small = jnp.transpose(cols_ref[...])
     lane = iota((1, width), 1)
-    count = jnp.full((1, 1), scalars_ref[0, 0], jnp.int32).astype(f32)
+    count = jnp.full((1, 1), live_ref[0, 0], jnp.int32).astype(f32)
     last = jnp.where(lane == 0, residual_sum, 0.0) + jnp.where(lane == 1, misfit_sum, 0.0)
     energy = jnp.sum(energy_ref[...], axis=1, keepdims=True)
     last = last + jnp.where(lane == 2, count, 0.0) + jnp.where(lane == 3, energy, 0.0)
@@ -651,6 +655,7 @@
     plane = (TILE_SIDE // 4) * tiles
     wide = 5 * points
 
+    live, place = live_count.reshape(1, 1), index.reshape(1, 1)
     owner_row = owner_rank.reshape(1, points)
     source_row = source.reshape(1, points)
     readout_row = readout.reshape(1, width)
@@ -689,28 +694,29 @@
         FORWARD_LIMIT,
         outs=(vmem(), vmem(), hbm(), hbm()),
     )(
-        live_count.reshape(1, 1), owner_row, tile_slot.reshape(1, points), offsets, fractions,
+        live, owner_row, tile_slot.reshape(1, points), offsets, fractions,
         source_row, fourier.T, weights, biases, readout_row,
     )
     received = lax.all_to_all(request, AXES, split_axis=0, concat_axis=0, tiled=True)
 
-    planes, _ = lax.optimization_barrier((field.reshape(TILE_SIDE, plane, LANES), outputs))
-    up = [(i, i + 1) for i in range(devices - 1)]
-    down = [(j, i) for i, j in up]
-    before = lax.ppermute(planes[:, plane - tiles :, :], AXES, up)
-    after = lax.ppermute(planes[:, :tiles, :], AXES, down)
-    smooth, energy, window_hi, window_lo = call(
-        functools.partial(prepare_kernel, devices, tiles),
+    field_here, _ = lax.optimization_barrier((field, outputs))
+    window_hi, window_lo, first, last = call(
+        functools.partial(prepare_kernel, tiles),
         "prepare",
-        [smem()] + [vmem()] * 3,
+        [vmem()],
         (
-            shape(cells, LANES), shape(1, LANES),
             shape(320, cells, dtype=bf16), shape(320, cells, dtype=bf16),
+            shape(TILE_SIDE, tiles, LANES), shape(TILE_SIDE, tiles, LANES),
         ),
         [pltpu.VMEM((cells + 2 * plane, LANES), f32)],
         FILL,
         PREPARE_LIMIT,
-    )(index.reshape(1, 1), field, before, after)
+    )(field_here)
+    up = [(i, i + 1) for i in range(devices - 1)]
+    down = [(j, i) for i, j in up]
+    before = lax.ppermute(last, AXES, up)
+    after = lax.ppermute(first, AXES, down)
+    received, before, after = lax.optimization_barrier((received, before, after))
 
     response, kept = call(
         functools.partial(owner_kernel, devices, tiles, lanes_each),
@@ -722,11 +728,11 @@
         LOOKUP_LIMIT,
     )(received, window_hi, window_lo)
     answered = lax.all_to_all(response, AXES, split_axis=0, concat_axis=0, tiled=True)
-    grad = call(
-        functools.partial(spread_kernel, tiles),
-        "spread",
-        [vmem()] * 2,
-        shape(cells, LANES),
+    grad, energy = call(
+        functools.partial(field_kernel, devices, tiles),
+        "field",
+        [smem()] + [vmem()] * 4,
+        (shape(cells, LANES), shape(1, LANES)),
         [
             pltpu.VMEM((cells, slots), bf16),
             pltpu.VMEM((320, slots), bf16),
@@ -736,15 +742,14 @@
         ],
         FILL,
         SPREAD_LIMIT,
-    )(kept, smooth)
+    )(place, kept, field_here, before, after)
     answered, grad = lax.optimization_barrier((answered, grad))
 
     part_rows = layers * width // 4
-    scalars = jnp.stack([live_count[0], index % 2]).reshape(1, 2)
     keep_a, keep_b, send_a, send_b = call(
         functools.partial(backward_kernel, devices, layers, lanes_each),
         "backward",
-        [smem()] + [vmem()] * 7 + [hbm()] * 3,
+        [smem()] * 2 + [vmem()] * 7 + [hbm()] * 3,
         tuple(shape(rows, width) for rows in (part_rows, part_rows + 8) * 2),
         [
             pltpu.VMEM((layers, width, wide), f32),
@@ -760,7 +765,7 @@
         12 * 2 * layers * width * width * wide,
         BACKWARD_LIMIT,
     )(
-        scalars, owner_row, source_row, observed.reshape(1, points),
+        live, place, owner_row, source_row, observed.reshape(1, points),
         answered.reshape(devices, LANES), energy, outputs, readout_row, weights, pre, parts,
     )
 

time: 129 us -> 114 us (0.88)
  Pallas kernels: 42.9 us -> 31.6 us
  waiting for transfers between devices: 36 us -> 34 us
    pallas_call x1, Pallas kernels: 13.2 us -> 8.12 us  [on_device(): call(functools.partial(forward_kernel, devices, layers, tiles, lanes_each...]
    pallas_call x2, Pallas kernels: 9.15 us -> 5.59 us  [the longest x1 5.01 us: on_device(): call(functools.partial(field_kernel, devices, tiles), 'field', [smem()] +...]
    pallas_call x1, Pallas kernels: 17.6 us -> 15.1 us  [on_device(): call(functools.partial(backward_kernel, devices, layers, lanes_each), 'ba...]
    all_to_all x1, waiting for transfers between devices: 3.33 us -> 1.39 us  [on_device(): lax.all_to_all(response, AXES, split_axis=0, concat_axis=0, tiled=True)]
  transfers between devices with their start and end apart: 24 -> 24, of which waited for: 18 -> 18; matrix products, arithmetic and copies ran while one was open for 5% -> 4% of each run, Pallas kernels for 7% -> 5%
where the time goes in v3:
time: 114 us
  starting transfers between devices  36.6 us (32%)
  waiting for transfers between devices  34 us (30%)
  Pallas kernels  31.6 us (28%)
  other arithmetic  4.89 us (4%)
  between operations  4.23 us (4%)
  local copies, waits for them, and re-layouts  2.74 us (2%)
    ppermute x20, waiting for transfers between devices, exchange(): lax.ppermute(value, AXES, [(i, i ^ bits[i % 2]) for i in range(devices)])  29.6 us
    ppermute x20, starting transfers between devices, exchange(): lax.ppermute(value, AXES, [(i, i ^ bits[i % 2]) for i in range(devices)])  16.7 us
    pallas_call x1, Pallas kernels, on_device(): call(functools.partial(backward_kernel, devices, layers, lanes_each), 'ba...  15.1 us
    all_to_all x1, starting transfers between devices, on_device(): lax.all_to_all(response, AXES, split_axis=0, concat_axis=0, tiled=True)  9.1 us
    pallas_call x1, Pallas kernels, on_device(): call(functools.partial(forward_kernel, devices, layers, tiles, lanes_each...  8.12 us
    all_to_all x1, starting transfers between devices, on_device(): lax.all_to_all(request, AXES, split_axis=0, concat_axis=0, tiled=True)  7.33 us
    pallas_call x1, Pallas kernels, on_device(): call(functools.partial(field_kernel, devices, tiles), 'field', [smem()] +...  5.01 us
    ppermute x1, waiting for transfers between devices, on_device(): after = lax.ppermute(first, AXES, down)  2.97 us
  transfers between devices with their start and end apart: 24, of which 18 were waited for; matrix products, arithmetic and copies ran while one was open for 4% of the time, Pallas kernels for 5%

profile of v3, /device:TPU:0, one launch (start us, length us, event | category | flops | bytes accessed | tf_op | source)
XLA Modules:
  0.0 114.0 jit_solution(1601222342576979203)
XLA Ops:
  1.3 8.1 %forward.1 = (f32[32,4,128]{2,1,0:T(4,128)}, f32[8,256]{1,0:T(8,128)}, f32[6,256,1280]{2,1,0:T(8,128)}, bf16[6,512,1280]{2,1,0:T(8,128)(2,1)}) custom-call(s32[1,1]{1,0:T(1,128)} %bitcast.28.live_ref, s32[1,256]{1,0:T(1,128)} %bitcast.38, s32[1,256]{1,0:T(1,128)} %bitcast.37, s32[3,256]{1,0:T(4,128)} %offsets_hbm.1, f32[3,256]{1,0:T(4,128)} %fractions_hbm.1, ...), custom_call_target="tpu_custom_call" | custom-call | flops 6039797760 | bytes 1048576 | tf_op jit(solution)/shard_map/forward/pallas_call | solution.py:665
  9.4 7.3 %all-to-all-start = ((f32[32,4,128]{2,1,0:T(4,128)}), f32[32,4,128]{2,1,0:T(4,128)S(1)}, u32[]{:S(2)}, u32[]{:S(2)}) async-start(f32[32,4,128]{2,1,0:T(4,128)} %get-tuple-element.31), calls=%async_computation | async-start | bytes 131072 | tf_op jit(solution)/shard_map/all_to_all | solution.py:700
  16.7 0.0 copy-start
  16.8 1.0 copy-done
  17.8 0.6 prepare.1
  18.4 2.2 %collective-permute-start = (f32[32,4,128]{2,1,0:T(4,128)S(1)}, f32[32,4,128]{2,1,0:T(4,128)S(1)}, u32[]{:S(2)}, u32[]{:S(2)}) collective-permute-start(f32[32,4,128]{2,1,0:T(4,128)S(1)} %get-tuple-element.34), channel_id=1, source_target_pairs={{0,1},{1,2},{2,3},{3,4},{4,5},{5,6},{6,7},{7,8},{8,9},{9,10},{10,1... | collective-permute-start | bytes 196616 | tf_op jit(solution)/shard_map/ppermute | solution.py:717
  20.5 1.3 %collective-permute-start.1 = (f32[32,4,128]{2,1,0:T(4,128)S(1)}, f32[32,4,128]{2,1,0:T(4,128)S(1)}, u32[]{:S(2)}, u32[]{:S(2)}) collective-permute-start(f32[32,4,128]{2,1,0:T(4,128)S(1)} %get-tuple-element.35), channel_id=1, source_target_pairs={{1,0},{2,1},{3,2},{4,3},{5,4},{6,5},{7,6},{8,7},{9,8},{10,9},{11,1... | collective-permute-start | bytes 196616 | tf_op jit(solution)/shard_map/ppermute | solution.py:718
  21.9 3.0 %collective-permute-done.1.after_ref = f32[32,4,128]{2,1,0:T(4,128)S(1)} collective-permute-done((f32[32,4,128]{2,1,0:T(4,128)S(1)}, f32[32,4,128]{2,1,0:T(4,128)S(1)}, u32[]{:S(2)}, u32[]{:S(2)}) %collective-permute-start.1) | collective-permute-done | bytes 65568 | tf_op jit(solution)/shard_map/ppermute | solution.py:718
  24.8 0.0 all-to-all-done.received_ref
  24.8 2.9 %lookup.1 = (f32[32,1,128]{2,1,0:T(1,128)}, f32[16,1024]{1,0:T(8,128)S(1)}) custom-call(f32[32,4,128]{2,1,0:T(4,128)S(1)} %all-to-all-done.received_ref, bf16[320,1024]{1,0:T(8,128)(2,1)S(1)} %get-tuple-element.37.window_hi, bf16[320,1024]{1,0:T(8,128)(2,1)S(1)} %get-tuple-element.38.window_lo), custom_call_target="tpu_custom_call" | custom-call | flops 1342177280 | bytes 1048576 | tf_op jit(solution)/shard_map/lookup/pallas_call | solution.py:721
  27.7 9.1 %all-to-all-start.1 = ((f32[32,1,128]{2,1,0:T(1,128)}), f32[32,1,128]{2,1,0:T(1,128)S(1)}, u32[]{:S(2)}, u32[]{:S(2)}) async-start(f32[32,1,128]{2,1,0:T(1,128)} %get-tuple-element.39), calls=%async_computation.1 | async-start | bytes 32768 | tf_op jit(solution)/shard_map/all_to_all | solution.py:730
  36.8 5.0 %field.1 = (f32[1024,128]{1,0:T(8,128)}, f32[1,128]{1,0:T(1,128)S(1)}) custom-call(s32[1,1]{1,0:T(1,128)} %bitcast.9.index_ref, f32[16,1024]{1,0:T(8,128)S(1)} %get-tuple-element.40.kept_ref, f32[1024,128]{1,0:T(8,128)S(1)} %bitcast.31, f32[32,4,128]{2,1,0:T(4,128)S(1)} %collective-permute-done.before_ref, f32[32,4,128]{2,1,0:T(4,128)S(1)} %collective-permute-done.1.after_ref), custom_call_target="tpu_custom_call" | custom-call | flops 4000000000 | bytes 1048576 | tf_op jit(solution)/shard_map/field/pallas_call | solution.py:731
  41.8 0.5 copy-done.2
  42.3 1.4 %all-to-all-done.1 = f32[32,1,128]{2,1,0:T(1,128)S(1)} async-done(((f32[32,1,128]{2,1,0:T(1,128)}), f32[32,1,128]{2,1,0:T(1,128)S(1)}, u32[]{:S(2)}, u32[]{:S(2)}) %all-to-all-start.1) | async-done | bytes 16416 | tf_op jit(solution)/shard_map/all_to_all | solution.py:730
  43.7 0.6 copy-done.4
  44.3 15.1 %backward.1 = (f32[384,256]{1,0:T(8,128)}, f32[392,256]{1,0:T(8,128)}, f32[384,256]{1,0:T(8,128)}, f32[392,256]{1,0:T(8,128)}) custom-call(s32[1,1]{1,0:T(1,128)} %bitcast.29.live_ref, s32[1,1]{1,0:T(1,128)} %bitcast.9.index_ref, s32[1,256]{1,0:T(1,128)} %bitcast.39, f32[1,256]{1,0:T(1,128)} %bitcast.41, f32[1,256]{1,0:T(1,128)} %bitcast.44, ...), custom_call_target="tpu_custom_call" | custom-call | flops 12079595520 | bytes 1048576 | tf_op jit(solution)/shard_map/backward/pallas_call | solution.py:749
  59.4 0.0 copy-start.3
  59.4 0.1 collective-permute-start.2
  59.5 0.5 collective-permute-start.7
  60.0 1.4 %collective-permute-done.2 = f32[384,256]{1,0:T(8,128)S(1)} collective-permute-done((f32[384,256]{1,0:T(8,128)}, f32[384,256]{1,0:T(8,128)S(1)}, u32[]{:S(2)}, u32[]{:S(2)}) %collective-permute-start.2) | collective-permute-done | bytes 393248 | tf_op jit(solution)/shard_map/ppermute | solution.py:779
  61.4 1.0 add.59
  62.5 0.6 collective-permute-start.3
  63.1 0.1 add.64
  63.2 1.6 %collective-permute-start.8 = (f32[200,256]{1,0:T(8,128)S(1)}, f32[200,256]{1,0:T(8,128)S(1)}, u32[]{:S(2)}, u32[]{:S(2)}) collective-permute-start(f32[200,256]{1,0:T(8,128)S(1)} %pad_maximum_fusion.5), channel_id=1, source_target_pairs={{0,2},{1,5},{2,0},{3,7},{4,6},{5,1},{6,4},{7,3},{8,10},{9,13},{10,... | collective-permute-start | bytes 614408 | tf_op jit(solution)/shard_map/ppermute | solution.py:779
  64.8 3.4 %collective-permute-done.3 = f32[192,256]{1,0:T(8,128)S(1)} collective-permute-done((f32[192,256]{1,0:T(8,128)S(1)}, f32[192,256]{1,0:T(8,128)S(1)}, u32[]{:S(2)}, u32[]{:S(2)}) %collective-permute-start.3) | collective-permute-done | bytes 196640 | tf_op jit(solution)/shard_map/ppermute | solution.py:779
  68.3 0.6 collective-permute-start.4
  68.9 1.7 %collective-permute-done.8 = f32[200,256]{1,0:T(8,128)S(1)} collective-permute-done((f32[200,256]{1,0:T(8,128)S(1)}, f32[200,256]{1,0:T(8,128)S(1)}, u32[]{:S(2)}, u32[]{:S(2)}) %collective-permute-start.8) | collective-permute-done | bytes 204832 | tf_op jit(solution)/shard_map/ppermute | solution.py:779
  70.7 0.6 collective-permute-start.9
  71.3 1.7 %collective-permute-done.4 = f32[96,256]{1,0:T(8,128)S(1)} collective-permute-done((f32[96,256]{1,0:T(8,128)S(1)}, f32[96,256]{1,0:T(8,128)S(1)}, u32[]{:S(2)}, u32[]{:S(2)}) %collective-permute-start.4) | collective-permute-done | bytes 98336 | tf_op jit(solution)/shard_map/ppermute | solution.py:779
  73.0 0.6 collective-permute-start.5
  73.6 1.8 %collective-permute-done.9 = f32[104,256]{1,0:T(8,128)S(1)} collective-permute-done((f32[104,256]{1,0:T(8,128)S(1)}, f32[104,256]{1,0:T(8,128)S(1)}, u32[]{:S(2)}, u32[]{:S(2)}) %collective-permute-start.9) | collective-permute-done | bytes 106528 | tf_op jit(solution)/shard_map/ppermute | solution.py:779
  75.5 0.6 collective-permute-start.10
  76.2 1.1 collective-permute-done.5
  77.3 2.5 %collective-permute-done.10 = f32[56,256]{1,0:T(8,128)S(1)} collective-permute-done((f32[56,256]{1,0:T(8,128)S(1)}, f32[56,256]{1,0:T(8,128)S(1)}, u32[]{:S(2)}, u32[]{:S(2)}) %collective-permute-start.10) | collective-permute-done | bytes 57376 | tf_op jit(solution)/shard_map/ppermute | solution.py:779
  79.8 1.2 %collective-permute-start.11 = (f32[32,256]{1,0:T(8,128)S(1)}, f32[32,256]{1,0:T(8,128)S(1)}, u32[]{:S(2)}, u32[]{:S(2)}) collective-permute-start(f32[32,256]{1,0:T(8,128)S(1)} %pad_maximum_fusion.14), channel_id=1, source_target_pairs={{0,16},{1,9},{2,18},{3,11},{4,20},{5,13},{6,22},{7,15},{8,24},{9,1... | collective-permute-start | bytes 98312 | tf_op jit(solution)/shard_map/ppermute | solution.py:779
  81.0 1.8 %collective-permute-start.6 = (f32[24,256]{1,0:T(8,128)S(1)}, f32[24,256]{1,0:T(8,128)S(1)}, u32[]{:S(2)}, u32[]{:S(2)}) collective-permute-start(f32[24,256]{1,0:T(8,128)S(1)} %slice_select_fusion.7), channel_id=1, source_target_pairs={{0,16},{1,9},{2,18},{3,11},{4,20},{5,13},{6,22},{7,15},{8,24},{9,1... | collective-permute-start | bytes 73736 | tf_op jit(solution)/shard_map/ppermute | solution.py:779
  82.8 2.2 %collective-permute-done.11 = f32[32,256]{1,0:T(8,128)S(1)} collective-permute-done((f32[32,256]{1,0:T(8,128)S(1)}, f32[32,256]{1,0:T(8,128)S(1)}, u32[]{:S(2)}, u32[]{:S(2)}) %collective-permute-start.11) | collective-permute-done | bytes 32800 | tf_op jit(solution)/shard_map/ppermute | solution.py:779
  85.1 0.6 fusion.1
  86.3 0.6 slice_multiply_fusion
  87.0 0.6 slice_multiply_fusion.1
  87.5 0.8 collective-permute-start.17
  89.5 2.2 %collective-permute-start.12 = (f32[24,256]{1,0:T(8,128)S(1)}, f32[24,256]{1,0:T(8,128)S(1)}, u32[]{:S(2)}, u32[]{:S(2)}) collective-permute-start(f32[24,256]{1,0:T(8,128)S(1)} %add_multiply_fusion), channel_id=1, source_target_pairs={{0,16},{1,9},{2,18},{3,11},{4,20},{5,13},{6,22},{7,15},{8,24},{9,1... | collective-permute-start | bytes 73736 | tf_op jit(solution)/shard_map/ppermute | solution.py:779
  92.4 0.6 pad_maximum_fusion.15
  93.0 0.4 collective-permute-start.18
  93.4 0.9 collective-permute-done.12
  94.3 1.9 %collective-permute-start.13 = (f32[48,256]{1,0:T(8,128)S(1)}, f32[48,256]{1,0:T(8,128)S(1)}, u32[]{:S(2)}, u32[]{:S(2)}) collective-permute-start(f32[48,256]{1,0:T(8,128)S(1)} %pad_maximum_fusion.12), channel_id=1, source_target_pairs={{0,8},{1,17},{2,10},{3,19},{4,12},{5,21},{6,14},{7,23},{8,0},{9,25... | collective-permute-start | bytes 147464 | tf_op jit(solution)/shard_map/ppermute | solution.py:779
  96.2 1.0 collective-permute-done.18
  97.2 0.6 collective-permute-start.19
  97.8 0.7 collective-permute-done.13
  98.5 1.5 %collective-permute-start.14 = (f32[96,256]{1,0:T(8,128)S(1)}, f32[96,256]{1,0:T(8,128)S(1)}, u32[]{:S(2)}, u32[]{:S(2)}) collective-permute-start(f32[96,256]{1,0:T(8,128)S(1)} %pad_maximum_fusion.9), channel_id=1, source_target_pairs={{0,4},{1,3},{2,6},{3,1},{4,0},{5,7},{6,2},{7,5},{8,12},{9,11},{10,... | collective-permute-start | bytes 294920 | tf_op jit(solution)/shard_map/ppermute | solution.py:779
  100.1 2.9 %collective-permute-done.19 = f32[96,256]{1,0:T(8,128)S(1)} collective-permute-done((f32[96,256]{1,0:T(8,128)S(1)}, f32[96,256]{1,0:T(8,128)S(1)}, u32[]{:S(2)}, u32[]{:S(2)}) %collective-permute-start.19) | collective-permute-done | bytes 98336 | tf_op jit(solution)/shard_map/ppermute | solution.py:779
  103.0 0.6 collective-permute-start.20
  103.5 1.5 %collective-permute-done.14 = f32[96,256]{1,0:T(8,128)S(1)} collective-permute-done((f32[96,256]{1,0:T(8,128)S(1)}, f32[96,256]{1,0:T(8,128)S(1)}, u32[]{:S(2)}, u32[]{:S(2)}) %collective-permute-start.14) | collective-permute-done | bytes 98336 | tf_op jit(solution)/shard_map/ppermute | solution.py:779
  105.1 0.4 collective-permute-start.15
  105.5 3.2 %collective-permute-done.20 = f32[192,256]{1,0:T(8,128)S(1)} collective-permute-done((f32[192,256]{1,0:T(8,128)S(1)}, f32[192,256]{1,0:T(8,128)S(1)}, u32[]{:S(2)}, u32[]{:S(2)}) %collective-permute-start.20) | collective-permute-done | bytes 196640 | tf_op jit(solution)/shard_map/ppermute | solution.py:779
  108.8 0.1 collective-permute-start.21
  108.9 2.0 %collective-permute-done.15 = f32[192,256]{1,0:T(8,128)S(1)} collective-permute-done((f32[192,256]{1,0:T(8,128)S(1)}, f32[192,256]{1,0:T(8,128)S(1)}, u32[]{:S(2)}, u32[]{:S(2)}) %collective-permute-start.15) | collective-permute-done | bytes 196640 | tf_op jit(solution)/shard_map/ppermute | solution.py:779
  110.9 0.1 collective-permute-start.16
  111.0 0.1 broadcast_select_fusion.1
  111.0 0.1 pad_maximum_fusion.2
  111.1 1.6 %collective-permute-done.16 = f32[384,256]{1,0:T(8,128)S(1)} collective-permute-done((f32[384,256]{1,0:T(8,128)S(1)}, f32[384,256]{1,0:T(8,128)S(1)}, u32[]{:S(2)}, u32[]{:S(2)}) %collective-permute-start.16) | collective-permute-done | bytes 393248 | tf_op jit(solution)/shard_map/ppermute | solution.py:779
  112.7 0.1 broadcast_select_fusion.3
  112.7 0.1 pad_maximum_fusion.1
  112.8 1.2 %pad_maximum_fusion = f32[6,256,256]{2,1,0:T(8,128)} fusion(f32[6,128,256]{2,1,0:T(8,128)S(1)} %bitcast.32, f32[6,128,256]{2,1,0:T(8,128)S(1)} %bitcast.33), kind=kLoop, calls=%fused_computation | loop fusion | flops 393216 | bytes 3145728 | tf_op jit(solution)/shard_map/concatenate | solution.py:813
  (51 shorter events, 0.6 us)
Async XLA Ops:
  9.4 15.4 %all-to-all-start = ((f32[32,4,128]{2,1,0:T(4,128)}), f32[32,4,128]{2,1,0:T(4,128)S(1)}, u32[]{:S(2)}, u32[]{:S(2)}) async-start(f32[32,4,128]{2,1,0:T(4,128)} %get-tuple-element.31), calls=%async_computation | async-start | bytes 131072 | tf_op jit(solution)/shard_map/all_to_all | solution.py:700
  16.7 1.0 copy-start
  18.4 3.5 %collective-permute-start = (f32[32,4,128]{2,1,0:T(4,128)S(1)}, f32[32,4,128]{2,1,0:T(4,128)S(1)}, u32[]{:S(2)}, u32[]{:S(2)}) collective-permute-start(f32[32,4,128]{2,1,0:T(4,128)S(1)} %get-tuple-element.34), channel_id=1, source_target_pairs={{0,1},{1,2},{2,3},{3,4},{4,5},{5,6},{6,7},{7,8},{8,9},{9,10},{10,1... | collective-permute-start | bytes 196616 | tf_op jit(solution)/shard_map/ppermute | solution.py:717
  20.5 4.3 %collective-permute-start.1 = (f32[32,4,128]{2,1,0:T(4,128)S(1)}, f32[32,4,128]{2,1,0:T(4,128)S(1)}, u32[]{:S(2)}, u32[]{:S(2)}) collective-permute-start(f32[32,4,128]{2,1,0:T(4,128)S(1)} %get-tuple-element.35), channel_id=1, source_target_pairs={{1,0},{2,1},{3,2},{4,3},{5,4},{6,5},{7,6},{8,7},{9,8},{10,9},{11,1... | collective-permute-start | bytes 196616 | tf_op jit(solution)/shard_map/ppermute | solution.py:718
  24.8 12.0 %copy-start.1 = (f32[4,32768]{1,0:T(4,128)S(1)}, f32[4,32768]{1,0:T(4,128)}, u32[]{:S(2)}) copy-start(f32[4,32768]{1,0:T(4,128)} %param.12) | copy-start | bytes 1572868
  27.7 16.0 %all-to-all-start.1 = ((f32[32,1,128]{2,1,0:T(1,128)}), f32[32,1,128]{2,1,0:T(1,128)S(1)}, u32[]{:S(2)}, u32[]{:S(2)}) async-start(f32[32,1,128]{2,1,0:T(1,128)} %get-tuple-element.39), calls=%async_computation.1 | async-start | bytes 32768 | tf_op jit(solution)/shard_map/all_to_all | solution.py:730
  41.8 0.5 copy-start.2
  43.7 0.6 copy-start.4
  59.4 3.7 %copy-start.3 = (f32[392,256]{1,0:T(8,128)S(1)}, f32[392,256]{1,0:T(8,128)}, u32[]{:S(2)}) copy-start(f32[392,256]{1,0:T(8,128)} %get-tuple-element.51) | copy-start | bytes 1204228
  59.4 2.0 %collective-permute-start.2 = (f32[384,256]{1,0:T(8,128)}, f32[384,256]{1,0:T(8,128)S(1)}, u32[]{:S(2)}, u32[]{:S(2)}) collective-permute-start(f32[384,256]{1,0:T(8,128)} %get-tuple-element.50), channel_id=1, source_target_pairs={{0,1},{1,0},{2,3},{3,2},{4,5},{5,4},{6,7},{7,6},{8,9},{9,8},{10,11... | collective-permute-start | bytes 1179656 | tf_op jit(solution)/shard_map/ppermute | solution.py:779
  59.5 3.6 %collective-permute-start.7 = (f32[392,256]{1,0:T(8,128)}, f32[392,256]{1,0:T(8,128)S(1)}, u32[]{:S(2)}, u32[]{:S(2)}) collective-permute-start(f32[392,256]{1,0:T(8,128)} %get-tuple-element.52), channel_id=1, source_target_pairs={{0,1},{1,0},{2,3},{3,2},{4,5},{5,4},{6,7},{7,6},{8,9},{9,8},{10,11... | collective-permute-start | bytes 1204232 | tf_op jit(solution)/shard_map/ppermute | solution.py:779
  62.5 5.7 %collective-permute-start.3 = (f32[192,256]{1,0:T(8,128)S(1)}, f32[192,256]{1,0:T(8,128)S(1)}, u32[]{:S(2)}, u32[]{:S(2)}) collective-permute-start(f32[192,256]{1,0:T(8,128)S(1)} %slice_select_fusion.1), channel_id=1, source_target_pairs={{0,2},{1,5},{2,0},{3,7},{4,6},{5,1},{6,4},{7,3},{8,10},{9,13},{10,... | collective-permute-start | bytes 589832 | tf_op jit(solution)/shard_map/ppermute | solution.py:779
  63.2 7.4 %collective-permute-start.8 = (f32[200,256]{1,0:T(8,128)S(1)}, f32[200,256]{1,0:T(8,128)S(1)}, u32[]{:S(2)}, u32[]{:S(2)}) collective-permute-start(f32[200,256]{1,0:T(8,128)S(1)} %pad_maximum_fusion.5), channel_id=1, source_target_pairs={{0,2},{1,5},{2,0},{3,7},{4,6},{5,1},{6,4},{7,3},{8,10},{9,13},{10,... | collective-permute-start | bytes 614408 | tf_op jit(solution)/shard_map/ppermute | solution.py:779
  68.3 4.7 %collective-permute-start.4 = (f32[96,256]{1,0:T(8,128)S(1)}, f32[96,256]{1,0:T(8,128)S(1)}, u32[]{:S(2)}, u32[]{:S(2)}) collective-permute-start(f32[96,256]{1,0:T(8,128)S(1)} %slice_select_fusion.3), channel_id=1, source_target_pairs={{0,4},{1,3},{2,6},{3,1},{4,0},{5,7},{6,2},{7,5},{8,12},{9,11},{10,... | collective-permute-start | bytes 294920 | tf_op jit(solution)/shard_map/ppermute | solution.py:779
  70.7 4.8 %collective-permute-start.9 = (f32[104,256]{1,0:T(8,128)S(1)}, f32[104,256]{1,0:T(8,128)S(1)}, u32[]{:S(2)}, u32[]{:S(2)}) collective-permute-start(f32[104,256]{1,0:T(8,128)S(1)} %pad_maximum_fusion.8), channel_id=1, source_target_pairs={{0,4},{1,3},{2,6},{3,1},{4,0},{5,7},{6,2},{7,5},{8,12},{9,11},{10,... | collective-permute-start | bytes 319496 | tf_op jit(solution)/shard_map/ppermute | solution.py:779
  73.0 4.3 %collective-permute-start.5 = (f32[48,256]{1,0:T(8,128)S(1)}, f32[48,256]{1,0:T(8,128)S(1)}, u32[]{:S(2)}, u32[]{:S(2)}) collective-permute-start(f32[48,256]{1,0:T(8,128)S(1)} %slice_select_fusion.5), channel_id=1, source_target_pairs={{0,8},{1,17},{2,10},{3,19},{4,12},{5,21},{6,14},{7,23},{8,0},{9,25... | collective-permute-start | bytes 147464 | tf_op jit(solution)/shard_map/ppermute | solution.py:779
  75.5 4.2 %collective-permute-start.10 = (f32[56,256]{1,0:T(8,128)S(1)}, f32[56,256]{1,0:T(8,128)S(1)}, u32[]{:S(2)}, u32[]{:S(2)}) collective-permute-start(f32[56,256]{1,0:T(8,128)S(1)} %pad_maximum_fusion.11), channel_id=1, source_target_pairs={{0,8},{1,17},{2,10},{3,19},{4,12},{5,21},{6,14},{7,23},{8,0},{9,25... | collective-permute-start | bytes 172040 | tf_op jit(solution)/shard_map/ppermute | solution.py:779
  79.8 5.2 %collective-permute-start.11 = (f32[32,256]{1,0:T(8,128)S(1)}, f32[32,256]{1,0:T(8,128)S(1)}, u32[]{:S(2)}, u32[]{:S(2)}) collective-permute-start(f32[32,256]{1,0:T(8,128)S(1)} %pad_maximum_fusion.14), channel_id=1, source_target_pairs={{0,16},{1,9},{2,18},{3,11},{4,20},{5,13},{6,22},{7,15},{8,24},{9,1... | collective-permute-start | bytes 98312 | tf_op jit(solution)/shard_map/ppermute | solution.py:779
  81.0 8.5 %collective-permute-start.6 = (f32[24,256]{1,0:T(8,128)S(1)}, f32[24,256]{1,0:T(8,128)S(1)}, u32[]{:S(2)}, u32[]{:S(2)}) collective-permute-start(f32[24,256]{1,0:T(8,128)S(1)} %slice_select_fusion.7), channel_id=1, source_target_pairs={{0,16},{1,9},{2,18},{3,11},{4,20},{5,13},{6,22},{7,15},{8,24},{9,1... | collective-permute-start | bytes 73736 | tf_op jit(solution)/shard_map/ppermute | solution.py:779
  87.5 5.5 %collective-permute-start.17 = (f32[24,256]{1,0:T(8,128)S(1)}, f32[24,256]{1,0:T(8,128)S(1)}, u32[]{:S(2)}, u32[]{:S(2)}) collective-permute-start(f32[24,256]{1,0:T(8,128)S(1)} %fusion), channel_id=1, source_target_pairs={{0,16},{1,9},{2,18},{3,11},{4,20},{5,13},{6,22},{7,15},{8,24},{9,1... | collective-permute-start | bytes 73736 | tf_op jit(solution)/shard_map/ppermute | solution.py:779
  89.5 4.8 %collective-permute-start.12 = (f32[24,256]{1,0:T(8,128)S(1)}, f32[24,256]{1,0:T(8,128)S(1)}, u32[]{:S(2)}, u32[]{:S(2)}) collective-permute-start(f32[24,256]{1,0:T(8,128)S(1)} %add_multiply_fusion), channel_id=1, source_target_pairs={{0,16},{1,9},{2,18},{3,11},{4,20},{5,13},{6,22},{7,15},{8,24},{9,1... | collective-permute-start | bytes 73736 | tf_op jit(solution)/shard_map/ppermute | solution.py:779
  93.0 4.2 %collective-permute-start.18 = (f32[48,256]{1,0:T(8,128)S(1)}, f32[48,256]{1,0:T(8,128)S(1)}, u32[]{:S(2)}, u32[]{:S(2)}) collective-permute-start(f32[48,256]{1,0:T(8,128)S(1)} %pad_maximum_fusion.13), channel_id=1, source_target_pairs={{0,8},{1,17},{2,10},{3,19},{4,12},{5,21},{6,14},{7,23},{8,0},{9,25... | collective-permute-start | bytes 147464 | tf_op jit(solution)/shard_map/ppermute | solution.py:779
  94.3 4.2 %collective-permute-start.13 = (f32[48,256]{1,0:T(8,128)S(1)}, f32[48,256]{1,0:T(8,128)S(1)}, u32[]{:S(2)}, u32[]{:S(2)}) collective-permute-start(f32[48,256]{1,0:T(8,128)S(1)} %pad_maximum_fusion.12), channel_id=1, source_target_pairs={{0,8},{1,17},{2,10},{3,19},{4,12},{5,21},{6,14},{7,23},{8,0},{9,25... | collective-permute-start | bytes 147464 | tf_op jit(solution)/shard_map/ppermute | solution.py:779
  97.2 5.7 %collective-permute-start.19 = (f32[96,256]{1,0:T(8,128)S(1)}, f32[96,256]{1,0:T(8,128)S(1)}, u32[]{:S(2)}, u32[]{:S(2)}) collective-permute-start(f32[96,256]{1,0:T(8,128)S(1)} %pad_maximum_fusion.10), channel_id=1, source_target_pairs={{0,4},{1,3},{2,6},{3,1},{4,0},{5,7},{6,2},{7,5},{8,12},{9,11},{10,... | collective-permute-start | bytes 294920 | tf_op jit(solution)/shard_map/ppermute | solution.py:779
  98.5 6.5 %collective-permute-start.14 = (f32[96,256]{1,0:T(8,128)S(1)}, f32[96,256]{1,0:T(8,128)S(1)}, u32[]{:S(2)}, u32[]{:S(2)}) collective-permute-start(f32[96,256]{1,0:T(8,128)S(1)} %pad_maximum_fusion.9), channel_id=1, source_target_pairs={{0,4},{1,3},{2,6},{3,1},{4,0},{5,7},{6,2},{7,5},{8,12},{9,11},{10,... | collective-permute-start | bytes 294920 | tf_op jit(solution)/shard_map/ppermute | solution.py:779
  103.0 5.7 %collective-permute-start.20 = (f32[192,256]{1,0:T(8,128)S(1)}, f32[192,256]{1,0:T(8,128)S(1)}, u32[]{:S(2)}, u32[]{:S(2)}) collective-permute-start(f32[192,256]{1,0:T(8,128)S(1)} %pad_maximum_fusion.7), channel_id=1, source_target_pairs={{0,2},{1,5},{2,0},{3,7},{4,6},{5,1},{6,4},{7,3},{8,10},{9,13},{10,... | collective-permute-start | bytes 589832 | tf_op jit(solution)/shard_map/ppermute | solution.py:779
  105.1 5.7 %collective-permute-start.15 = (f32[192,256]{1,0:T(8,128)S(1)}, f32[192,256]{1,0:T(8,128)S(1)}, u32[]{:S(2)}, u32[]{:S(2)}) collective-permute-start(f32[192,256]{1,0:T(8,128)S(1)} %pad_maximum_fusion.6), channel_id=1, source_target_pairs={{0,2},{1,5},{2,0},{3,7},{4,6},{5,1},{6,4},{7,3},{8,10},{9,13},{10,... | collective-permute-start | bytes 589832 | tf_op jit(solution)/shard_map/ppermute | solution.py:779
  108.8 2.2 %collective-permute-start.21 = (f32[384,256]{1,0:T(8,128)S(1)}, f32[384,256]{1,0:T(8,128)S(1)}, u32[]{:S(2)}, u32[]{:S(2)}) collective-permute-start(f32[384,256]{1,0:T(8,128)S(1)} %pad_maximum_fusion.4), channel_id=1, source_target_pairs={{0,1},{1,0},{2,3},{3,2},{4,5},{5,4},{6,7},{7,6},{8,9},{9,8},{10,11... | collective-permute-start | bytes 1179656 | tf_op jit(solution)/shard_map/ppermute | solution.py:779
  110.9 1.8 %collective-permute-start.16 = (f32[384,256]{1,0:T(8,128)S(1)}, f32[384,256]{1,0:T(8,128)S(1)}, u32[]{:S(2)}, u32[]{:S(2)}) collective-permute-start(f32[384,256]{1,0:T(8,128)S(1)} %pad_maximum_fusion.3), channel_id=1, source_target_pairs={{0,1},{1,0},{2,3},{3,2},{4,5},{5,4},{6,7},{7,6},{8,9},{9,8},{10,11... | collective-permute-start | bytes 1179656 | tf_op jit(solution)/shard_map/ppermute | solution.py:779

commit v4 on v3

--- a/solution.py
+++ b/solution.py
@@ -608,6 +608,22 @@
     send_b_ref[half * width // 2 :, :] = small
 
 
+def finish_kernel(cells_total, sums_ref, bias_ref, readout_ref, losses_ref, scale_ref):
+    layers = bias_ref.shape[0]
+    width = bias_ref.shape[1]
+    sums = sums_ref[...]
+    lane = iota((1, width), 1)
+    last = sums[7:8]
+    count = jnp.sum(jnp.where(lane == 2, last, 0.0), axis=1, keepdims=True)
+    scale = jnp.broadcast_to(1.0 / count, (1, width))
+    bias_ref[...] = sums[:layers] * scale
+    readout_ref[...] = sums[layers : layers + 1] * scale
+    energy = jnp.sum(jnp.where(lane == 3, last, 0.0), axis=1, keepdims=True)
+    losses = jnp.where(lane == 2, energy / cells_total, last * scale)
+    losses_ref[...] = losses[:, 0:3]
+    scale_ref[...] = scale
+
+
 def vmem():
     return pl.BlockSpec(memory_space=pltpu.VMEM)
 
@@ -792,32 +808,38 @@
         arrived = [exchange(value, step) for value in outgoing]
         main = [jnp.where(upper, m[half:], m[:half]) + a[:half] for m, a in zip(main, arrived)]
         extra = extra + arrived[1][half:]
-    scale = 1.0 / extra[7, 2]
-    main = [m * scale for m in main]
-    sums = extra[7]
-    losses = jnp.stack(
-        [sums[0] * scale, sums[1] * scale, sums[3] / (devices * conductivity.size)]
-    )
-    bias_grad, readout_grad = extra[:layers] * scale, extra[layers] * scale
     for step in reversed(range(len(even))):
         upper = upper_of(step)
-        arrived = [exchange(m, step) for m in main]
+        outgoing = list(main)
+        if step == len(even) - 1:
+            outgoing[1] = jnp.concatenate([main[1], extra], axis=0)
+        arrived = [exchange(value, step) for value in outgoing]
+        if step == len(even) - 1:
+            rows = main[1].shape[0]
+            arrived[1], extra = arrived[1][:rows], arrived[1][rows:]
         main = [
             jnp.concatenate([jnp.where(upper, a, m), jnp.where(upper, m, a)], axis=0)
             for m, a in zip(main, arrived)
         ]
-        if step == len(even) - 1:
-            main[1], losses, bias_grad, readout_grad = lax.optimization_barrier(
-                (main[1], losses, bias_grad, readout_grad)
-            )
-    weight_grad = jnp.concatenate([m.reshape(layers, width // 2, width) for m in main], axis=1)
+    bias_grad, readout_grad, losses, scale = call(
+        functools.partial(finish_kernel, float(devices * conductivity.size)),
+        "finish",
+        [vmem()],
+        (shape(layers, width), shape(1, width), shape(1, 3), shape(1, width)),
+        [],
+        FILL,
+        4,
+    )(extra)
+    weight_grad = scale * jnp.concatenate(
+        [m.reshape(layers, width // 2, width) for m in main], axis=1
+    )
     conductivity_grad = grad.reshape(cells // tiles, tiles, LANES).transpose(1, 0, 2)
     return (
         conductivity_grad.reshape(conductivity.shape),
         weight_grad,
         bias_grad,
-        readout_grad,
-        losses,
+        readout_grad.reshape(readout.shape),
+        losses.reshape(3),
     )
 
 

time: 114 us -> 112 us (0.982)
  between operations: 4.23 us -> 1.66 us
  starting transfers between devices: 36.6 us -> 38.6 us
  other arithmetic: 4.89 us -> 3.19 us
    ppermute x20, starting transfers between devices: 16.7 us -> 18.7 us  [exchange(): lax.ppermute(value, AXES, [(i, i ^ bits[i % 2]) for i in range(devices)])]
    concatenate x1, other arithmetic: 1.25 us -> 0.01 us  [on_device(): outgoing[1] = jnp.concatenate([main[1], extra], axis=0)]
  transfers between devices with their start and end apart: 24 -> 24, of which waited for: 18 -> 18; matrix products, arithmetic and copies ran while one was open for 4% -> 2% of each run, Pallas kernels for 5% -> 6%
where the time goes in v4:
time: 112 us
  starting transfers between devices  38.6 us (34%)
  waiting for transfers between devices  33.8 us (30%)
  Pallas kernels  32.3 us (29%)
  other arithmetic  3.19 us (3%)
  local copies, waits for them, and re-layouts  2.24 us (2%)
  between operations  1.66 us (1%)
    ppermute x20, waiting for transfers between devices, exchange(): lax.ppermute(value, AXES, [(i, i ^ bits[i % 2]) for i in range(devices)])  29.5 us
    ppermute x20, starting transfers between devices, exchange(): lax.ppermute(value, AXES, [(i, i ^ bits[i % 2]) for i in range(devices)])  18.7 us
    pallas_call x1, Pallas kernels, on_device(): call(functools.partial(backward_kernel, devices, layers, lanes_each), 'ba...  15.1 us
    all_to_all x1, starting transfers between devices, on_device(): lax.all_to_all(response, AXES, split_axis=0, concat_axis=0, tiled=True)  9.1 us
    pallas_call x1, Pallas kernels, on_device(): call(functools.partial(forward_kernel, devices, layers, tiles, lanes_each...  8.12 us
    all_to_all x1, starting transfers between devices, on_device(): lax.all_to_all(request, AXES, split_axis=0, concat_axis=0, tiled=True)  7.33 us
    pallas_call x1, Pallas kernels, on_device(): call(functools.partial(field_kernel, devices, tiles), 'field', [smem()] +...  5.01 us
    ppermute x1, waiting for transfers between devices, on_device(): after = lax.ppermute(first, AXES, down)  2.97 us
  transfers between devices with their start and end apart: 24, of which 18 were waited for; matrix products, arithmetic and copies ran while one was open for 2% of the time, Pallas kernels for 6%

profile of v4, /device:TPU:0, one launch (start us, length us, event | category | flops | bytes accessed | tf_op | source)
XLA Modules:
  0.0 111.9 jit_solution(12672972111346826422)
XLA Ops:
  1.3 8.1 %forward.1 = (f32[32,4,128]{2,1,0:T(4,128)}, f32[8,256]{1,0:T(8,128)}, f32[6,256,1280]{2,1,0:T(8,128)}, bf16[6,512,1280]{2,1,0:T(8,128)(2,1)}) custom-call(s32[1,1]{1,0:T(1,128)} %bitcast.24.live_ref, s32[1,256]{1,0:T(1,128)} %bitcast.34, s32[1,256]{1,0:T(1,128)} %bitcast.33, s32[3,256]{1,0:T(4,128)} %offsets_hbm.1, f32[3,256]{1,0:T(4,128)} %fractions_hbm.1, ...), custom_call_target="tpu_custom_call" | custom-call | flops 6039797760 | bytes 1048576 | tf_op jit(solution)/shard_map/forward/pallas_call | solution.py:681
  9.4 7.3 %all-to-all-start = ((f32[32,4,128]{2,1,0:T(4,128)}), f32[32,4,128]{2,1,0:T(4,128)S(1)}, u32[]{:S(2)}, u32[]{:S(2)}) async-start(f32[32,4,128]{2,1,0:T(4,128)} %get-tuple-element.31), calls=%async_computation | async-start | bytes 131072 | tf_op jit(solution)/shard_map/all_to_all | solution.py:716
  16.7 0.0 copy-start
  16.8 1.0 copy-done
  17.8 0.6 prepare.1
  18.4 2.2 %collective-permute-start = (f32[32,4,128]{2,1,0:T(4,128)S(1)}, f32[32,4,128]{2,1,0:T(4,128)S(1)}, u32[]{:S(2)}, u32[]{:S(2)}) collective-permute-start(f32[32,4,128]{2,1,0:T(4,128)S(1)} %get-tuple-element.34), channel_id=1, source_target_pairs={{0,1},{1,2},{2,3},{3,4},{4,5},{5,6},{6,7},{7,8},{8,9},{9,10},{10,1... | collective-permute-start | bytes 196616 | tf_op jit(solution)/shard_map/ppermute | solution.py:733
  20.5 1.3 %collective-permute-start.1 = (f32[32,4,128]{2,1,0:T(4,128)S(1)}, f32[32,4,128]{2,1,0:T(4,128)S(1)}, u32[]{:S(2)}, u32[]{:S(2)}) collective-permute-start(f32[32,4,128]{2,1,0:T(4,128)S(1)} %get-tuple-element.35), channel_id=1, source_target_pairs={{1,0},{2,1},{3,2},{4,3},{5,4},{6,5},{7,6},{8,7},{9,8},{10,9},{11,1... | collective-permute-start | bytes 196616 | tf_op jit(solution)/shard_map/ppermute | solution.py:734
  21.8 0.0 collective-permute-done.before_ref
  21.9 3.0 %collective-permute-done.1.after_ref = f32[32,4,128]{2,1,0:T(4,128)S(1)} collective-permute-done((f32[32,4,128]{2,1,0:T(4,128)S(1)}, f32[32,4,128]{2,1,0:T(4,128)S(1)}, u32[]{:S(2)}, u32[]{:S(2)}) %collective-permute-start.1) | collective-permute-done | bytes 65568 | tf_op jit(solution)/shard_map/ppermute | solution.py:734
  24.8 0.0 all-to-all-done.received_ref
  24.8 2.9 %lookup.1 = (f32[32,1,128]{2,1,0:T(1,128)}, f32[16,1024]{1,0:T(8,128)S(1)}) custom-call(f32[32,4,128]{2,1,0:T(4,128)S(1)} %all-to-all-done.received_ref, bf16[320,1024]{1,0:T(8,128)(2,1)S(1)} %get-tuple-element.37.window_hi, bf16[320,1024]{1,0:T(8,128)(2,1)S(1)} %get-tuple-element.38.window_lo), custom_call_target="tpu_custom_call" | custom-call | flops 1342177280 | bytes 1048576 | tf_op jit(solution)/shard_map/lookup/pallas_call | solution.py:737
  27.7 9.1 %all-to-all-start.1 = ((f32[32,1,128]{2,1,0:T(1,128)}), f32[32,1,128]{2,1,0:T(1,128)S(1)}, u32[]{:S(2)}, u32[]{:S(2)}) async-start(f32[32,1,128]{2,1,0:T(1,128)} %get-tuple-element.39), calls=%async_computation.1 | async-start | bytes 32768 | tf_op jit(solution)/shard_map/all_to_all | solution.py:746
  36.8 5.0 %field.1 = (f32[1024,128]{1,0:T(8,128)}, f32[1,128]{1,0:T(1,128)S(1)}) custom-call(s32[1,1]{1,0:T(1,128)} %bitcast.9.index_ref, f32[16,1024]{1,0:T(8,128)S(1)} %get-tuple-element.40.kept_ref, f32[1024,128]{1,0:T(8,128)S(1)} %bitcast.28, f32[32,4,128]{2,1,0:T(4,128)S(1)} %collective-permute-done.before_ref, f32[32,4,128]{2,1,0:T(4,128)S(1)} %collective-permute-done.1.after_ref), custom_call_target="tpu_custom_call" | custom-call | flops 4000000000 | bytes 1048576 | tf_op jit(solution)/shard_map/field/pallas_call | solution.py:747
  41.8 0.6 copy-done.2
  42.4 1.3 %all-to-all-done.1 = f32[32,1,128]{2,1,0:T(1,128)S(1)} async-done(((f32[32,1,128]{2,1,0:T(1,128)}), f32[32,1,128]{2,1,0:T(1,128)S(1)}, u32[]{:S(2)}, u32[]{:S(2)}) %all-to-all-start.1) | async-done | bytes 16416 | tf_op jit(solution)/shard_map/all_to_all | solution.py:746
  43.7 0.6 copy-done.4
  44.3 15.1 %backward.1 = (f32[384,256]{1,0:T(8,128)}, f32[392,256]{1,0:T(8,128)}, f32[384,256]{1,0:T(8,128)}, f32[392,256]{1,0:T(8,128)}) custom-call(s32[1,1]{1,0:T(1,128)} %bitcast.25.live_ref, s32[1,1]{1,0:T(1,128)} %bitcast.9.index_ref, s32[1,256]{1,0:T(1,128)} %bitcast.35, f32[1,256]{1,0:T(1,128)} %bitcast.37, f32[1,256]{1,0:T(1,128)} %bitcast.40, ...), custom_call_target="tpu_custom_call" | custom-call | flops 12079595520 | bytes 1048576 | tf_op jit(solution)/shard_map/backward/pallas_call | solution.py:765
  59.4 0.0 copy-start.3
  59.4 0.1 collective-permute-start.8
  59.5 0.5 collective-permute-start.2
  60.0 1.4 %collective-permute-done.8 = f32[384,256]{1,0:T(8,128)S(1)} collective-permute-done((f32[384,256]{1,0:T(8,128)}, f32[384,256]{1,0:T(8,128)S(1)}, u32[]{:S(2)}, u32[]{:S(2)}) %collective-permute-start.8) | collective-permute-done | bytes 393248 | tf_op jit(solution)/shard_map/ppermute | solution.py:795
  61.4 1.0 add.68
  62.5 0.6 collective-permute-start.9
  63.1 0.0 collective-permute-done.2
  63.1 0.1 add.59
  63.2 1.6 %collective-permute-start.3 = (f32[200,256]{1,0:T(8,128)S(1)}, f32[200,256]{1,0:T(8,128)S(1)}, u32[]{:S(2)}, u32[]{:S(2)}) collective-permute-start(f32[200,256]{1,0:T(8,128)S(1)} %pad_maximum_fusion.4), channel_id=1, source_target_pairs={{0,2},{1,5},{2,0},{3,7},{4,6},{5,1},{6,4},{7,3},{8,10},{9,13},{10,... | collective-permute-start | bytes 614408 | tf_op jit(solution)/shard_map/ppermute | solution.py:795
  64.8 3.4 %collective-permute-done.9 = f32[192,256]{1,0:T(8,128)S(1)} collective-permute-done((f32[192,256]{1,0:T(8,128)S(1)}, f32[192,256]{1,0:T(8,128)S(1)}, u32[]{:S(2)}, u32[]{:S(2)}) %collective-permute-start.9) | collective-permute-done | bytes 196640 | tf_op jit(solution)/shard_map/ppermute | solution.py:795
  68.3 0.6 collective-permute-start.10
  68.9 1.7 %collective-permute-done.3 = f32[200,256]{1,0:T(8,128)S(1)} collective-permute-done((f32[200,256]{1,0:T(8,128)S(1)}, f32[200,256]{1,0:T(8,128)S(1)}, u32[]{:S(2)}, u32[]{:S(2)}) %collective-permute-start.3) | collective-permute-done | bytes 204832 | tf_op jit(solution)/shard_map/ppermute | solution.py:795
  70.7 0.6 collective-permute-start.4
  71.3 1.7 %collective-permute-done.10 = f32[96,256]{1,0:T(8,128)S(1)} collective-permute-done((f32[96,256]{1,0:T(8,128)S(1)}, f32[96,256]{1,0:T(8,128)S(1)}, u32[]{:S(2)}, u32[]{:S(2)}) %collective-permute-start.10) | collective-permute-done | bytes 98336 | tf_op jit(solution)/shard_map/ppermute | solution.py:795
  73.0 0.6 collective-permute-start.11
  73.6 1.8 %collective-permute-done.4 = f32[104,256]{1,0:T(8,128)S(1)} collective-permute-done((f32[104,256]{1,0:T(8,128)S(1)}, f32[104,256]{1,0:T(8,128)S(1)}, u32[]{:S(2)}, u32[]{:S(2)}) %collective-permute-start.4) | collective-permute-done | bytes 106528 | tf_op jit(solution)/shard_map/ppermute | solution.py:795
  75.5 1.6 %collective-permute-done.11 = f32[48,256]{1,0:T(8,128)S(1)} collective-permute-done((f32[48,256]{1,0:T(8,128)S(1)}, f32[48,256]{1,0:T(8,128)S(1)}, u32[]{:S(2)}, u32[]{:S(2)}) %collective-permute-start.11) | collective-permute-done | bytes 49184 | tf_op jit(solution)/shard_map/ppermute | solution.py:795
  77.2 1.3 %collective-permute-start.12 = (f32[24,256]{1,0:T(8,128)S(1)}, f32[24,256]{1,0:T(8,128)S(1)}, u32[]{:S(2)}, u32[]{:S(2)}) collective-permute-start(f32[24,256]{1,0:T(8,128)S(1)} %slice_select_fusion.8), channel_id=1, source_target_pairs={{0,16},{1,9},{2,18},{3,11},{4,20},{5,13},{6,22},{7,15},{8,24},{9,1... | collective-permute-start | bytes 73736 | tf_op jit(solution)/shard_map/ppermute | solution.py:795
  78.4 1.5 %collective-permute-start.5 = (f32[56,256]{1,0:T(8,128)S(1)}, f32[56,256]{1,0:T(8,128)S(1)}, u32[]{:S(2)}, u32[]{:S(2)}) collective-permute-start(f32[56,256]{1,0:T(8,128)S(1)} %pad_maximum_fusion.10), channel_id=1, source_target_pairs={{0,8},{1,17},{2,10},{3,19},{4,12},{5,21},{6,14},{7,23},{8,0},{9,25... | collective-permute-start | bytes 172040 | tf_op jit(solution)/shard_map/ppermute | solution.py:795
  80.0 2.4 %collective-permute-done.12 = f32[24,256]{1,0:T(8,128)S(1)} collective-permute-done((f32[24,256]{1,0:T(8,128)S(1)}, f32[24,256]{1,0:T(8,128)S(1)}, u32[]{:S(2)}, u32[]{:S(2)}) %collective-permute-start.12) | collective-permute-done | bytes 24608 | tf_op jit(solution)/shard_map/ppermute | solution.py:795
  82.3 0.8 collective-permute-start.13
  83.3 2.1 %collective-permute-start.6 = (f32[32,256]{1,0:T(8,128)S(1)}, f32[32,256]{1,0:T(8,128)S(1)}, u32[]{:S(2)}, u32[]{:S(2)}) collective-permute-start(f32[32,256]{1,0:T(8,128)S(1)} %pad_maximum_fusion.13), channel_id=1, source_target_pairs={{0,16},{1,9},{2,18},{3,11},{4,20},{5,13},{6,22},{7,15},{8,24},{9,1... | collective-permute-start | bytes 98312 | tf_op jit(solution)/shard_map/ppermute | solution.py:795
  85.4 1.7 %collective-permute-done.13 = f32[24,256]{1,0:T(8,128)S(1)} collective-permute-done((f32[24,256]{1,0:T(8,128)S(1)}, f32[24,256]{1,0:T(8,128)S(1)}, u32[]{:S(2)}, u32[]{:S(2)}) %collective-permute-start.13) | collective-permute-done | bytes 24608 | tf_op jit(solution)/shard_map/ppermute | solution.py:795
  87.1 1.9 %collective-permute-done.6 = f32[32,256]{1,0:T(8,128)S(1)} collective-permute-done((f32[32,256]{1,0:T(8,128)S(1)}, f32[32,256]{1,0:T(8,128)S(1)}, u32[]{:S(2)}, u32[]{:S(2)}) %collective-permute-start.6) | collective-permute-done | bytes 32800 | tf_op jit(solution)/shard_map/ppermute | solution.py:795
  89.0 1.4 %collective-permute-start.7 = (f32[32,256]{1,0:T(8,128)S(1)}, f32[32,256]{1,0:T(8,128)S(1)}, u32[]{:S(2)}, u32[]{:S(2)}) collective-permute-start(f32[32,256]{1,0:T(8,128)S(1)} %pad_maximum_fusion.14), channel_id=1, source_target_pairs={{0,16},{1,9},{2,18},{3,11},{4,20},{5,13},{6,22},{7,15},{8,24},{9,1... | collective-permute-start | bytes 98312 | tf_op jit(solution)/shard_map/ppermute | solution.py:795
  90.4 1.1 collective-permute-start.14
  91.5 2.4 %collective-permute-done.7 = f32[32,256]{1,0:T(8,128)S(1)} collective-permute-done((f32[32,256]{1,0:T(8,128)S(1)}, f32[32,256]{1,0:T(8,128)S(1)}, u32[]{:S(2)}, u32[]{:S(2)}) %collective-permute-start.7) | collective-permute-done | bytes 32800 | tf_op jit(solution)/shard_map/ppermute | solution.py:795
  93.9 1.1 collective-permute-start.18
  95.0 0.0 collective-permute-done.14
  95.1 1.4 %collective-permute-start.15 = (f32[96,256]{1,0:T(8,128)S(1)}, f32[96,256]{1,0:T(8,128)S(1)}, u32[]{:S(2)}, u32[]{:S(2)}) collective-permute-start(f32[96,256]{1,0:T(8,128)S(1)} %pad_maximum_fusion.8), channel_id=1, source_target_pairs={{0,4},{1,3},{2,6},{3,1},{4,0},{5,7},{6,2},{7,5},{8,12},{9,11},{10,... | collective-permute-start | bytes 294920 | tf_op jit(solution)/shard_map/ppermute | solution.py:795
  96.4 1.7 %collective-permute-done.18 = f32[48,256]{1,0:T(8,128)S(1)} collective-permute-done((f32[48,256]{1,0:T(8,128)S(1)}, f32[48,256]{1,0:T(8,128)S(1)}, u32[]{:S(2)}, u32[]{:S(2)}) %collective-permute-start.18) | collective-permute-done | bytes 49184 | tf_op jit(solution)/shard_map/ppermute | solution.py:795
  98.1 1.3 %collective-permute-start.19 = (f32[96,256]{1,0:T(8,128)S(1)}, f32[96,256]{1,0:T(8,128)S(1)}, u32[]{:S(2)}, u32[]{:S(2)}) collective-permute-start(f32[96,256]{1,0:T(8,128)S(1)} %pad_maximum_fusion.9), channel_id=1, source_target_pairs={{0,4},{1,3},{2,6},{3,1},{4,0},{5,7},{6,2},{7,5},{8,12},{9,11},{10,... | collective-permute-start | bytes 294920 | tf_op jit(solution)/shard_map/ppermute | solution.py:795
  99.4 1.3 %collective-permute-done.15 = f32[96,256]{1,0:T(8,128)S(1)} collective-permute-done((f32[96,256]{1,0:T(8,128)S(1)}, f32[96,256]{1,0:T(8,128)S(1)}, u32[]{:S(2)}, u32[]{:S(2)}) %collective-permute-start.15) | collective-permute-done | bytes 98336 | tf_op jit(solution)/shard_map/ppermute | solution.py:795
  100.7 0.8 collective-permute-start.16
  101.5 1.3 %collective-permute-done.19 = f32[96,256]{1,0:T(8,128)S(1)} collective-permute-done((f32[96,256]{1,0:T(8,128)S(1)}, f32[96,256]{1,0:T(8,128)S(1)}, u32[]{:S(2)}, u32[]{:S(2)}) %collective-permute-start.19) | collective-permute-done | bytes 98336 | tf_op jit(solution)/shard_map/ppermute | solution.py:795
  102.8 1.3 %collective-permute-start.20 = (f32[192,256]{1,0:T(8,128)S(1)}, f32[192,256]{1,0:T(8,128)S(1)}, u32[]{:S(2)}, u32[]{:S(2)}) collective-permute-start(f32[192,256]{1,0:T(8,128)S(1)} %pad_maximum_fusion.6), channel_id=1, source_target_pairs={{0,2},{1,5},{2,0},{3,7},{4,6},{5,1},{6,4},{7,3},{8,10},{9,13},{10,... | collective-permute-start | bytes 589832 | tf_op jit(solution)/shard_map/ppermute | solution.py:795
  104.1 2.3 %collective-permute-done.16 = f32[192,256]{1,0:T(8,128)S(1)} collective-permute-done((f32[192,256]{1,0:T(8,128)S(1)}, f32[192,256]{1,0:T(8,128)S(1)}, u32[]{:S(2)}, u32[]{:S(2)}) %collective-permute-start.16) | collective-permute-done | bytes 196640 | tf_op jit(solution)/shard_map/ppermute | solution.py:795
  106.5 0.1 collective-permute-start.17
  106.6 2.0 %collective-permute-done.20 = f32[192,256]{1,0:T(8,128)S(1)} collective-permute-done((f32[192,256]{1,0:T(8,128)S(1)}, f32[192,256]{1,0:T(8,128)S(1)}, u32[]{:S(2)}, u32[]{:S(2)}) %collective-permute-start.20) | collective-permute-done | bytes 196640 | tf_op jit(solution)/shard_map/ppermute | solution.py:795
  108.6 0.1 collective-permute-start.21
  108.7 0.7 finish.1
  109.4 0.1 broadcast_select_fusion.3
  109.5 0.1 pad_maximum_fusion
  109.5 0.9 collective-permute-done.21
  110.4 0.1 broadcast_select_fusion.1
  110.5 0.1 pad_maximum_fusion.1
  110.6 1.3 %maximum_multiply_fusion = f32[6,256,256]{2,1,0:T(8,128)} fusion(f32[6,128,256]{2,1,0:T(8,128)S(1)} %bitcast.30, f32[6,128,256]{2,1,0:T(8,128)S(1)} %bitcast.29, f32[256]{0:T(256)S(1)} %bitcast.26), kind=kLoop, calls=%fused_computation | loop fusion | flops 786432 | bytes 3146752 | tf_op jit(solution)/shard_map/mul | solution.py:833
  (50 shorter events, 0.6 us)
Async XLA Ops:
  9.4 15.4 %all-to-all-start = ((f32[32,4,128]{2,1,0:T(4,128)}), f32[32,4,128]{2,1,0:T(4,128)S(1)}, u32[]{:S(2)}, u32[]{:S(2)}) async-start(f32[32,4,128]{2,1,0:T(4,128)} %get-tuple-element.31), calls=%async_computation | async-start | bytes 131072 | tf_op jit(solution)/shard_map/all_to_all | solution.py:716
  16.7 1.0 copy-start
  18.4 3.5 %collective-permute-start = (f32[32,4,128]{2,1,0:T(4,128)S(1)}, f32[32,4,128]{2,1,0:T(4,128)S(1)}, u32[]{:S(2)}, u32[]{:S(2)}) collective-permute-start(f32[32,4,128]{2,1,0:T(4,128)S(1)} %get-tuple-element.34), channel_id=1, source_target_pairs={{0,1},{1,2},{2,3},{3,4},{4,5},{5,6},{6,7},{7,8},{8,9},{9,10},{10,1... | collective-permute-start | bytes 196616 | tf_op jit(solution)/shard_map/ppermute | solution.py:733
  20.5 4.3 %collective-permute-start.1 = (f32[32,4,128]{2,1,0:T(4,128)S(1)}, f32[32,4,128]{2,1,0:T(4,128)S(1)}, u32[]{:S(2)}, u32[]{:S(2)}) collective-permute-start(f32[32,4,128]{2,1,0:T(4,128)S(1)} %get-tuple-element.35), channel_id=1, source_target_pairs={{1,0},{2,1},{3,2},{4,3},{5,4},{6,5},{7,6},{8,7},{9,8},{10,9},{11,1... | collective-permute-start | bytes 196616 | tf_op jit(solution)/shard_map/ppermute | solution.py:734
  24.8 12.0 %copy-start.1 = (f32[4,32768]{1,0:T(4,128)S(1)}, f32[4,32768]{1,0:T(4,128)}, u32[]{:S(2)}) copy-start(f32[4,32768]{1,0:T(4,128)} %param.12) | copy-start | bytes 1572868
  27.7 16.0 %all-to-all-start.1 = ((f32[32,1,128]{2,1,0:T(1,128)}), f32[32,1,128]{2,1,0:T(1,128)S(1)}, u32[]{:S(2)}, u32[]{:S(2)}) async-start(f32[32,1,128]{2,1,0:T(1,128)} %get-tuple-element.39), calls=%async_computation.1 | async-start | bytes 32768 | tf_op jit(solution)/shard_map/all_to_all | solution.py:746
  41.8 0.6 copy-start.2
  43.7 0.6 copy-start.4
  59.4 3.7 %copy-start.3 = (f32[392,256]{1,0:T(8,128)S(1)}, f32[392,256]{1,0:T(8,128)}, u32[]{:S(2)}) copy-start(f32[392,256]{1,0:T(8,128)} %get-tuple-element.49) | copy-start | bytes 1204228
  59.4 2.0 %collective-permute-start.8 = (f32[384,256]{1,0:T(8,128)}, f32[384,256]{1,0:T(8,128)S(1)}, u32[]{:S(2)}, u32[]{:S(2)}) collective-permute-start(f32[384,256]{1,0:T(8,128)} %get-tuple-element.53), channel_id=1, source_target_pairs={{0,1},{1,0},{2,3},{3,2},{4,5},{5,4},{6,7},{7,6},{8,9},{9,8},{10,11... | collective-permute-start | bytes 1179656 | tf_op jit(solution)/shard_map/ppermute | solution.py:795
  59.5 3.6 %collective-permute-start.2 = (f32[392,256]{1,0:T(8,128)}, f32[392,256]{1,0:T(8,128)S(1)}, u32[]{:S(2)}, u32[]{:S(2)}) collective-permute-start(f32[392,256]{1,0:T(8,128)} %get-tuple-element.50), channel_id=1, source_target_pairs={{0,1},{1,0},{2,3},{3,2},{4,5},{5,4},{6,7},{7,6},{8,9},{9,8},{10,11... | collective-permute-start | bytes 1204232 | tf_op jit(solution)/shard_map/ppermute | solution.py:795
  62.5 5.7 %collective-permute-start.9 = (f32[192,256]{1,0:T(8,128)S(1)}, f32[192,256]{1,0:T(8,128)S(1)}, u32[]{:S(2)}, u32[]{:S(2)}) collective-permute-start(f32[192,256]{1,0:T(8,128)S(1)} %slice_select_fusion), channel_id=1, source_target_pairs={{0,2},{1,5},{2,0},{3,7},{4,6},{5,1},{6,4},{7,3},{8,10},{9,13},{10,... | collective-permute-start | bytes 589832 | tf_op jit(solution)/shard_map/ppermute | solution.py:795
  63.2 7.4 %collective-permute-start.3 = (f32[200,256]{1,0:T(8,128)S(1)}, f32[200,256]{1,0:T(8,128)S(1)}, u32[]{:S(2)}, u32[]{:S(2)}) collective-permute-start(f32[200,256]{1,0:T(8,128)S(1)} %pad_maximum_fusion.4), channel_id=1, source_target_pairs={{0,2},{1,5},{2,0},{3,7},{4,6},{5,1},{6,4},{7,3},{8,10},{9,13},{10,... | collective-permute-start | bytes 614408 | tf_op jit(solution)/shard_map/ppermute | solution.py:795
  68.3 4.7 %collective-permute-start.10 = (f32[96,256]{1,0:T(8,128)S(1)}, f32[96,256]{1,0:T(8,128)S(1)}, u32[]{:S(2)}, u32[]{:S(2)}) collective-permute-start(f32[96,256]{1,0:T(8,128)S(1)} %slice_select_fusion.2), channel_id=1, source_target_pairs={{0,4},{1,3},{2,6},{3,1},{4,0},{5,7},{6,2},{7,5},{8,12},{9,11},{10,... | collective-permute-start | bytes 294920 | tf_op jit(solution)/shard_map/ppermute | solution.py:795
  70.7 4.8 %collective-permute-start.4 = (f32[104,256]{1,0:T(8,128)S(1)}, f32[104,256]{1,0:T(8,128)S(1)}, u32[]{:S(2)}, u32[]{:S(2)}) collective-permute-start(f32[104,256]{1,0:T(8,128)S(1)} %pad_maximum_fusion.7), channel_id=1, source_target_pairs={{0,4},{1,3},{2,6},{3,1},{4,0},{5,7},{6,2},{7,5},{8,12},{9,11},{10,... | collective-permute-start | bytes 319496 | tf_op jit(solution)/shard_map/ppermute | solution.py:795
  73.0 4.2 %collective-permute-start.11 = (f32[48,256]{1,0:T(8,128)S(1)}, f32[48,256]{1,0:T(8,128)S(1)}, u32[]{:S(2)}, u32[]{:S(2)}) collective-permute-start(f32[48,256]{1,0:T(8,128)S(1)} %slice_select_fusion.4), channel_id=1, source_target_pairs={{0,8},{1,17},{2,10},{3,19},{4,12},{5,21},{6,14},{7,23},{8,0},{9,25... | collective-permute-start | bytes 147464 | tf_op jit(solution)/shard_map/ppermute | solution.py:795
  77.2 5.2 %collective-permute-start.12 = (f32[24,256]{1,0:T(8,128)S(1)}, f32[24,256]{1,0:T(8,128)S(1)}, u32[]{:S(2)}, u32[]{:S(2)}) collective-permute-start(f32[24,256]{1,0:T(8,128)S(1)} %slice_select_fusion.8), channel_id=1, source_target_pairs={{0,16},{1,9},{2,18},{3,11},{4,20},{5,13},{6,22},{7,15},{8,24},{9,1... | collective-permute-start | bytes 73736 | tf_op jit(solution)/shard_map/ppermute | solution.py:795
  78.4 4.8 %collective-permute-start.5 = (f32[56,256]{1,0:T(8,128)S(1)}, f32[56,256]{1,0:T(8,128)S(1)}, u32[]{:S(2)}, u32[]{:S(2)}) collective-permute-start(f32[56,256]{1,0:T(8,128)S(1)} %pad_maximum_fusion.10), channel_id=1, source_target_pairs={{0,8},{1,17},{2,10},{3,19},{4,12},{5,21},{6,14},{7,23},{8,0},{9,25... | collective-permute-start | bytes 172040 | tf_op jit(solution)/shard_map/ppermute | solution.py:795
  82.3 4.8 %collective-permute-start.13 = (f32[24,256]{1,0:T(8,128)S(1)}, f32[24,256]{1,0:T(8,128)S(1)}, u32[]{:S(2)}, u32[]{:S(2)}) collective-permute-start(f32[24,256]{1,0:T(8,128)S(1)} %select_add_fusion.3), channel_id=1, source_target_pairs={{0,16},{1,9},{2,18},{3,11},{4,20},{5,13},{6,22},{7,15},{8,24},{9,1... | collective-permute-start | bytes 73736 | tf_op jit(solution)/shard_map/ppermute | solution.py:795
  83.3 5.8 %collective-permute-start.6 = (f32[32,256]{1,0:T(8,128)S(1)}, f32[32,256]{1,0:T(8,128)S(1)}, u32[]{:S(2)}, u32[]{:S(2)}) collective-permute-start(f32[32,256]{1,0:T(8,128)S(1)} %pad_maximum_fusion.13), channel_id=1, source_target_pairs={{0,16},{1,9},{2,18},{3,11},{4,20},{5,13},{6,22},{7,15},{8,24},{9,1... | collective-permute-start | bytes 98312 | tf_op jit(solution)/shard_map/ppermute | solution.py:795
  89.0 4.9 %collective-permute-start.7 = (f32[32,256]{1,0:T(8,128)S(1)}, f32[32,256]{1,0:T(8,128)S(1)}, u32[]{:S(2)}, u32[]{:S(2)}) collective-permute-start(f32[32,256]{1,0:T(8,128)S(1)} %pad_maximum_fusion.14), channel_id=1, source_target_pairs={{0,16},{1,9},{2,18},{3,11},{4,20},{5,13},{6,22},{7,15},{8,24},{9,1... | collective-permute-start | bytes 98312 | tf_op jit(solution)/shard_map/ppermute | solution.py:795
  90.4 4.6 %collective-permute-start.14 = (f32[48,256]{1,0:T(8,128)S(1)}, f32[48,256]{1,0:T(8,128)S(1)}, u32[]{:S(2)}, u32[]{:S(2)}) collective-permute-start(f32[48,256]{1,0:T(8,128)S(1)} %pad_maximum_fusion.11), channel_id=1, source_target_pairs={{0,8},{1,17},{2,10},{3,19},{4,12},{5,21},{6,14},{7,23},{8,0},{9,25... | collective-permute-start | bytes 147464 | tf_op jit(solution)/shard_map/ppermute | solution.py:795
  93.9 4.2 %collective-permute-start.18 = (f32[48,256]{1,0:T(8,128)S(1)}, f32[48,256]{1,0:T(8,128)S(1)}, u32[]{:S(2)}, u32[]{:S(2)}) collective-permute-start(f32[48,256]{1,0:T(8,128)S(1)} %pad_maximum_fusion.12), channel_id=1, source_target_pairs={{0,8},{1,17},{2,10},{3,19},{4,12},{5,21},{6,14},{7,23},{8,0},{9,25... | collective-permute-start | bytes 147464 | tf_op jit(solution)/shard_map/ppermute | solution.py:795
  95.1 5.6 %collective-permute-start.15 = (f32[96,256]{1,0:T(8,128)S(1)}, f32[96,256]{1,0:T(8,128)S(1)}, u32[]{:S(2)}, u32[]{:S(2)}) collective-permute-start(f32[96,256]{1,0:T(8,128)S(1)} %pad_maximum_fusion.8), channel_id=1, source_target_pairs={{0,4},{1,3},{2,6},{3,1},{4,0},{5,7},{6,2},{7,5},{8,12},{9,11},{10,... | collective-permute-start | bytes 294920 | tf_op jit(solution)/shard_map/ppermute | solution.py:795
  98.1 4.7 %collective-permute-start.19 = (f32[96,256]{1,0:T(8,128)S(1)}, f32[96,256]{1,0:T(8,128)S(1)}, u32[]{:S(2)}, u32[]{:S(2)}) collective-permute-start(f32[96,256]{1,0:T(8,128)S(1)} %pad_maximum_fusion.9), channel_id=1, source_target_pairs={{0,4},{1,3},{2,6},{3,1},{4,0},{5,7},{6,2},{7,5},{8,12},{9,11},{10,... | collective-permute-start | bytes 294920 | tf_op jit(solution)/shard_map/ppermute | solution.py:795
  100.7 5.7 %collective-permute-start.16 = (f32[192,256]{1,0:T(8,128)S(1)}, f32[192,256]{1,0:T(8,128)S(1)}, u32[]{:S(2)}, u32[]{:S(2)}) collective-permute-start(f32[192,256]{1,0:T(8,128)S(1)} %pad_maximum_fusion.5), channel_id=1, source_target_pairs={{0,2},{1,5},{2,0},{3,7},{4,6},{5,1},{6,4},{7,3},{8,10},{9,13},{10,... | collective-permute-start | bytes 589832 | tf_op jit(solution)/shard_map/ppermute | solution.py:795
  102.8 5.7 %collective-permute-start.20 = (f32[192,256]{1,0:T(8,128)S(1)}, f32[192,256]{1,0:T(8,128)S(1)}, u32[]{:S(2)}, u32[]{:S(2)}) collective-permute-start(f32[192,256]{1,0:T(8,128)S(1)} %pad_maximum_fusion.6), channel_id=1, source_target_pairs={{0,2},{1,5},{2,0},{3,7},{4,6},{5,1},{6,4},{7,3},{8,10},{9,13},{10,... | collective-permute-start | bytes 589832 | tf_op jit(solution)/shard_map/ppermute | solution.py:795
  106.5 2.9 %collective-permute-start.17 = (f32[384,256]{1,0:T(8,128)S(1)}, f32[384,256]{1,0:T(8,128)S(1)}, u32[]{:S(2)}, u32[]{:S(2)}) collective-permute-start(f32[384,256]{1,0:T(8,128)S(1)} %pad_maximum_fusion.2), channel_id=1, source_target_pairs={{0,1},{1,0},{2,3},{3,2},{4,5},{5,4},{6,7},{7,6},{8,9},{9,8},{10,11... | collective-permute-start | bytes 1179656 | tf_op jit(solution)/shard_map/ppermute | solution.py:795
  108.6 1.8 %collective-permute-start.21 = (f32[384,256]{1,0:T(8,128)S(1)}, f32[384,256]{1,0:T(8,128)S(1)}, u32[]{:S(2)}, u32[]{:S(2)}) collective-permute-start(f32[384,256]{1,0:T(8,128)S(1)} %pad_maximum_fusion.3), channel_id=1, source_target_pairs={{0,1},{1,0},{2,3},{3,2},{4,5},{5,4},{6,7},{7,6},{8,9},{9,8},{10,11... | collective-permute-start | bytes 1179656 | tf_op jit(solution)/shard_map/ppermute | solution.py:795

commit v5 on v4

--- a/solution.py
+++ b/solution.py
@@ -86,7 +86,7 @@
 
 FORWARD_ROWS, ROWS = 256, 64
 FILL = 4 * 10**9
-FORWARD_LIMIT, PREPARE_LIMIT, LOOKUP_LIMIT, SPREAD_LIMIT, BACKWARD_LIMIT = 64, 8, 12, 14, 58
+FORWARD_LIMIT, PREPARE_LIMIT, LOOKUP_LIMIT, SPREAD_LIMIT, BACKWARD_LIMIT = 64, 8, 12, 14, 48
 
 
 def forward_kernel(

time: 112 us -> 109 us (0.973)
  waiting for transfers between devices: 33.8 us -> 35.8 us
  Pallas kernels: 32.3 us -> 30.5 us
  starting transfers between devices: 38.6 us -> 37.1 us
  local copies, waits for them, and re-layouts: 2.24 us -> 1.08 us
    pallas_call x1, Pallas kernels: 15.1 us -> 13.2 us  [on_device(): call(functools.partial(backward_kernel, devices, layers, lanes_each), 'ba...]
    ppermute x20, starting transfers between devices: 18.7 us -> 17.2 us  [exchange(): lax.ppermute(value, AXES, [(i, i ^ bits[i % 2]) for i in range(devices)])]
    ppermute x20, waiting for transfers between devices: 29.5 us -> 31 us  [exchange(): lax.ppermute(value, AXES, [(i, i ^ bits[i % 2]) for i in range(devices)])]
    unnamed x10 -> x16, local copies, waits for them, and re-layouts: 2.23 us -> 1.08 us
  transfers between devices with their start and end apart: 24 -> 24, of which waited for: 18 -> 19; matrix products, arithmetic and copies ran while one was open for 2% -> 1% of each run, Pallas kernels for 6% -> 6%
where the time goes in v5:
time: 109 us; the launch traced here: 108 us
  starting transfers between devices  37.1 us (34%)
  waiting for transfers between devices  35.8 us (33%)
  Pallas kernels  30.5 us (28%)
  other arithmetic  2.19 us (2%)
  between operations  1.73 us (2%)
    ppermute x20, waiting for transfers between devices, exchange(): lax.ppermute(value, AXES, [(i, i ^ bits[i % 2]) for i in range(devices)])  31 us
    ppermute x20, starting transfers between devices, exchange(): lax.ppermute(value, AXES, [(i, i ^ bits[i % 2]) for i in range(devices)])  17.2 us
    pallas_call x1, Pallas kernels, on_device(): call(functools.partial(backward_kernel, devices, layers, lanes_each), 'ba...  13.2 us
    all_to_all x1, starting transfers between devices, on_device(): lax.all_to_all(response, AXES, split_axis=0, concat_axis=0, tiled=True)  9.1 us
    pallas_call x1, Pallas kernels, on_device(): call(functools.partial(forward_kernel, devices, layers, tiles, lanes_each...  8.14 us
    all_to_all x1, starting transfers between devices, on_device(): lax.all_to_all(request, AXES, split_axis=0, concat_axis=0, tiled=True)  7.33 us
    pallas_call x1, Pallas kernels, on_device(): call(functools.partial(field_kernel, devices, tiles), 'field', [smem()] +...  5.01 us
    ppermute x1, waiting for transfers between devices, on_device(): after = lax.ppermute(first, AXES, down)  2.97 us
  transfers between devices with their start and end apart: 24, of which 19 were waited for; matrix products, arithmetic and copies ran while one was open for 1% of the time, Pallas kernels for 6%

profile of v5, /device:TPU:0, one launch (start us, length us, event | category | flops | bytes accessed | tf_op | source)
XLA Modules:
  0.0 108.4 jit_solution(8478562219347132725)
XLA Ops:
  1.3 8.1 %forward.1 = (f32[32,4,128]{2,1,0:T(4,128)}, f32[8,256]{1,0:T(8,128)}, f32[6,256,1280]{2,1,0:T(8,128)}, bf16[6,512,1280]{2,1,0:T(8,128)(2,1)}) custom-call(s32[1,1]{1,0:T(1,128)} %bitcast.24.live_ref, s32[1,256]{1,0:T(1,128)} %bitcast.30, s32[1,256]{1,0:T(1,128)} %bitcast.40, s32[3,256]{1,0:T(4,128)} %offsets_hbm.1, f32[3,256]{1,0:T(4,128)} %fractions_hbm.1, ...), custom_call_target="tpu_custom_call" | custom-call | flops 6039797760 | bytes 1048576 | tf_op jit(solution)/shard_map/forward/pallas_call | solution.py:681
  9.4 7.3 %all-to-all-start = ((f32[32,4,128]{2,1,0:T(4,128)}), f32[32,4,128]{2,1,0:T(4,128)S(1)}, u32[]{:S(2)}, u32[]{:S(2)}) async-start(f32[32,4,128]{2,1,0:T(4,128)} %get-tuple-element.31), calls=%async_computation | async-start | bytes 131072 | tf_op jit(solution)/shard_map/all_to_all | solution.py:716
  16.8 0.0 copy-start.1
  16.8 1.0 copy-done.1
  17.8 0.6 prepare.1
  18.4 2.2 %collective-permute-start = (f32[32,4,128]{2,1,0:T(4,128)S(1)}, f32[32,4,128]{2,1,0:T(4,128)S(1)}, u32[]{:S(2)}, u32[]{:S(2)}) collective-permute-start(f32[32,4,128]{2,1,0:T(4,128)S(1)} %get-tuple-element.34), channel_id=1, source_target_pairs={{0,1},{1,2},{2,3},{3,4},{4,5},{5,6},{6,7},{7,8},{8,9},{9,10},{10,1... | collective-permute-start | bytes 196616 | tf_op jit(solution)/shard_map/ppermute | solution.py:733
  20.6 1.3 %collective-permute-start.1 = (f32[32,4,128]{2,1,0:T(4,128)S(1)}, f32[32,4,128]{2,1,0:T(4,128)S(1)}, u32[]{:S(2)}, u32[]{:S(2)}) collective-permute-start(f32[32,4,128]{2,1,0:T(4,128)S(1)} %get-tuple-element.35), channel_id=1, source_target_pairs={{1,0},{2,1},{3,2},{4,3},{5,4},{6,5},{7,6},{8,7},{9,8},{10,9},{11,1... | collective-permute-start | bytes 196616 | tf_op jit(solution)/shard_map/ppermute | solution.py:734
  21.9 3.0 %collective-permute-done.1.after_ref = f32[32,4,128]{2,1,0:T(4,128)S(1)} collective-permute-done((f32[32,4,128]{2,1,0:T(4,128)S(1)}, f32[32,4,128]{2,1,0:T(4,128)S(1)}, u32[]{:S(2)}, u32[]{:S(2)}) %collective-permute-start.1) | collective-permute-done | bytes 65568 | tf_op jit(solution)/shard_map/ppermute | solution.py:734
  24.9 2.9 %lookup.1 = (f32[32,1,128]{2,1,0:T(1,128)}, f32[16,1024]{1,0:T(8,128)S(1)}) custom-call(f32[32,4,128]{2,1,0:T(4,128)S(1)} %all-to-all-done.received_ref, bf16[320,1024]{1,0:T(8,128)(2,1)S(1)} %get-tuple-element.37.window_hi, bf16[320,1024]{1,0:T(8,128)(2,1)S(1)} %get-tuple-element.38.window_lo), custom_call_target="tpu_custom_call" | custom-call | flops 1342177280 | bytes 1048576 | tf_op jit(solution)/shard_map/lookup/pallas_call | solution.py:737
  27.7 9.1 %all-to-all-start.1 = ((f32[32,1,128]{2,1,0:T(1,128)}), f32[32,1,128]{2,1,0:T(1,128)S(1)}, u32[]{:S(2)}, u32[]{:S(2)}) async-start(f32[32,1,128]{2,1,0:T(1,128)} %get-tuple-element.39), calls=%async_computation.1 | async-start | bytes 32768 | tf_op jit(solution)/shard_map/all_to_all | solution.py:746
  36.8 0.0 copy-start
  36.9 0.0 copy-start.3
  36.9 0.0 copy-start.4
  36.9 0.0 copy-start.5
  36.9 0.0 copy-start.6
  36.9 0.0 copy-start.7
  36.9 5.0 %field.1 = (f32[1024,128]{1,0:T(8,128)}, f32[1,128]{1,0:T(1,128)S(1)}) custom-call(s32[1,1]{1,0:T(1,128)} %bitcast.9.index_ref, f32[16,1024]{1,0:T(8,128)S(1)} %get-tuple-element.40.kept_ref, f32[1024,128]{1,0:T(8,128)S(1)} %bitcast.29, f32[32,4,128]{2,1,0:T(4,128)S(1)} %collective-permute-done.before_ref, f32[32,4,128]{2,1,0:T(4,128)S(1)} %collective-permute-done.1.after_ref), custom_call_target="tpu_custom_call" | custom-call | flops 4000000000 | bytes 1048576 | tf_op jit(solution)/shard_map/field/pallas_call | solution.py:747
  41.9 1.8 %all-to-all-done.1 = f32[32,1,128]{2,1,0:T(1,128)S(1)} async-done(((f32[32,1,128]{2,1,0:T(1,128)}), f32[32,1,128]{2,1,0:T(1,128)S(1)}, u32[]{:S(2)}, u32[]{:S(2)}) %all-to-all-start.1) | async-done | bytes 16416 | tf_op jit(solution)/shard_map/all_to_all | solution.py:746
  43.8 13.2 %backward.1 = (f32[384,256]{1,0:T(8,128)S(1)}, f32[392,256]{1,0:T(8,128)S(1)}, f32[384,256]{1,0:T(8,128)S(1)}, f32[392,256]{1,0:T(8,128)S(1)}) custom-call(s32[1,1]{1,0:T(1,128)} %bitcast.25.live_ref, s32[1,1]{1,0:T(1,128)} %bitcast.9.index_ref, s32[1,256]{1,0:T(1,128)S(1)} %bitcast.31, f32[1,256]{1,0:T(1,128)S(1)} %bitcast.33, f32[1,256]{1,0:T(1,128)S(1)} %bitcast.36, ...), custom_call_target="tpu_custom_call" | custom-call | flops 12079595520 | bytes 1048576 | tf_op jit(solution)/shard_map/backward/pallas_call | solution.py:765
  57.0 0.1 collective-permute-start.8
  57.1 0.5 collective-permute-start.2
  57.6 1.2 %collective-permute-done.8 = f32[384,256]{1,0:T(8,128)S(1)} collective-permute-done((f32[384,256]{1,0:T(8,128)S(1)}, f32[384,256]{1,0:T(8,128)S(1)}, u32[]{:S(2)}, u32[]{:S(2)}) %collective-permute-start.8) | collective-permute-done | bytes 393248 | tf_op jit(solution)/shard_map/ppermute | solution.py:795
  58.8 0.1 add.68
  58.9 0.6 collective-permute-start.9
  59.5 0.1 add.59
  59.6 1.6 %collective-permute-start.3 = (f32[200,256]{1,0:T(8,128)S(1)}, f32[200,256]{1,0:T(8,128)S(1)}, u32[]{:S(2)}, u32[]{:S(2)}) collective-permute-start(f32[200,256]{1,0:T(8,128)S(1)} %pad_maximum_fusion.4), channel_id=1, source_target_pairs={{0,2},{1,5},{2,0},{3,7},{4,6},{5,1},{6,4},{7,3},{8,10},{9,13},{10,... | collective-permute-start | bytes 614408 | tf_op jit(solution)/shard_map/ppermute | solution.py:795
  61.2 3.4 %collective-permute-done.9 = f32[192,256]{1,0:T(8,128)S(1)} collective-permute-done((f32[192,256]{1,0:T(8,128)S(1)}, f32[192,256]{1,0:T(8,128)S(1)}, u32[]{:S(2)}, u32[]{:S(2)}) %collective-permute-start.9) | collective-permute-done | bytes 196640 | tf_op jit(solution)/shard_map/ppermute | solution.py:795
  64.7 0.6 collective-permute-start.10
  65.3 1.7 %collective-permute-done.3 = f32[200,256]{1,0:T(8,128)S(1)} collective-permute-done((f32[200,256]{1,0:T(8,128)S(1)}, f32[200,256]{1,0:T(8,128)S(1)}, u32[]{:S(2)}, u32[]{:S(2)}) %collective-permute-start.3) | collective-permute-done | bytes 204832 | tf_op jit(solution)/shard_map/ppermute | solution.py:795
  67.1 0.6 collective-permute-start.4
  67.7 1.7 %collective-permute-done.10 = f32[96,256]{1,0:T(8,128)S(1)} collective-permute-done((f32[96,256]{1,0:T(8,128)S(1)}, f32[96,256]{1,0:T(8,128)S(1)}, u32[]{:S(2)}, u32[]{:S(2)}) %collective-permute-start.10) | collective-permute-done | bytes 98336 | tf_op jit(solution)/shard_map/ppermute | solution.py:795
  69.4 0.7 collective-permute-start.11
  70.1 1.8 %collective-permute-done.4 = f32[104,256]{1,0:T(8,128)S(1)} collective-permute-done((f32[104,256]{1,0:T(8,128)S(1)}, f32[104,256]{1,0:T(8,128)S(1)}, u32[]{:S(2)}, u32[]{:S(2)}) %collective-permute-start.4) | collective-permute-done | bytes 106528 | tf_op jit(solution)/shard_map/ppermute | solution.py:795
  71.9 1.6 %collective-permute-done.11 = f32[48,256]{1,0:T(8,128)S(1)} collective-permute-done((f32[48,256]{1,0:T(8,128)S(1)}, f32[48,256]{1,0:T(8,128)S(1)}, u32[]{:S(2)}, u32[]{:S(2)}) %collective-permute-start.11) | collective-permute-done | bytes 49184 | tf_op jit(solution)/shard_map/ppermute | solution.py:795
  73.6 0.7 collective-permute-start.12
  74.3 1.5 %collective-permute-start.5 = (f32[56,256]{1,0:T(8,128)S(1)}, f32[56,256]{1,0:T(8,128)S(1)}, u32[]{:S(2)}, u32[]{:S(2)}) collective-permute-start(f32[56,256]{1,0:T(8,128)S(1)} %pad_maximum_fusion.10), channel_id=1, source_target_pairs={{0,8},{1,17},{2,10},{3,19},{4,12},{5,21},{6,14},{7,23},{8,0},{9,25... | collective-permute-start | bytes 172040 | tf_op jit(solution)/shard_map/ppermute | solution.py:795
  75.9 2.8 %collective-permute-done.12 = f32[24,256]{1,0:T(8,128)S(1)} collective-permute-done((f32[24,256]{1,0:T(8,128)S(1)}, f32[24,256]{1,0:T(8,128)S(1)}, u32[]{:S(2)}, u32[]{:S(2)}) %collective-permute-start.12) | collective-permute-done | bytes 24608 | tf_op jit(solution)/shard_map/ppermute | solution.py:795
  78.7 0.7 collective-permute-start.13
  79.4 2.3 %collective-permute-start.6 = (f32[32,256]{1,0:T(8,128)S(1)}, f32[32,256]{1,0:T(8,128)S(1)}, u32[]{:S(2)}, u32[]{:S(2)}) collective-permute-start(f32[32,256]{1,0:T(8,128)S(1)} %pad_maximum_fusion.13), channel_id=1, source_target_pairs={{0,16},{1,9},{2,18},{3,11},{4,20},{5,13},{6,22},{7,15},{8,24},{9,1... | collective-permute-start | bytes 98312 | tf_op jit(solution)/shard_map/ppermute | solution.py:795
  81.7 1.8 %collective-permute-done.13 = f32[24,256]{1,0:T(8,128)S(1)} collective-permute-done((f32[24,256]{1,0:T(8,128)S(1)}, f32[24,256]{1,0:T(8,128)S(1)}, u32[]{:S(2)}, u32[]{:S(2)}) %collective-permute-start.13) | collective-permute-done | bytes 24608 | tf_op jit(solution)/shard_map/ppermute | solution.py:795
  83.6 1.9 %collective-permute-done.6 = f32[32,256]{1,0:T(8,128)S(1)} collective-permute-done((f32[32,256]{1,0:T(8,128)S(1)}, f32[32,256]{1,0:T(8,128)S(1)}, u32[]{:S(2)}, u32[]{:S(2)}) %collective-permute-start.6) | collective-permute-done | bytes 32800 | tf_op jit(solution)/shard_map/ppermute | solution.py:795
  85.5 1.1 %collective-permute-start.7 = (f32[32,256]{1,0:T(8,128)S(1)}, f32[32,256]{1,0:T(8,128)S(1)}, u32[]{:S(2)}, u32[]{:S(2)}) collective-permute-start(f32[32,256]{1,0:T(8,128)S(1)} %pad_maximum_fusion.14), channel_id=1, source_target_pairs={{0,16},{1,9},{2,18},{3,11},{4,20},{5,13},{6,22},{7,15},{8,24},{9,1... | collective-permute-start | bytes 98312 | tf_op jit(solution)/shard_map/ppermute | solution.py:795
  86.7 1.1 %collective-permute-start.14 = (f32[48,256]{1,0:T(8,128)S(1)}, f32[48,256]{1,0:T(8,128)S(1)}, u32[]{:S(2)}, u32[]{:S(2)}) collective-permute-start(f32[48,256]{1,0:T(8,128)S(1)} %pad_maximum_fusion.11), channel_id=1, source_target_pairs={{0,8},{1,17},{2,10},{3,19},{4,12},{5,21},{6,14},{7,23},{8,0},{9,25... | collective-permute-start | bytes 147464 | tf_op jit(solution)/shard_map/ppermute | solution.py:795
  87.8 2.6 %collective-permute-done.7 = f32[32,256]{1,0:T(8,128)S(1)} collective-permute-done((f32[32,256]{1,0:T(8,128)S(1)}, f32[32,256]{1,0:T(8,128)S(1)}, u32[]{:S(2)}, u32[]{:S(2)}) %collective-permute-start.7) | collective-permute-done | bytes 32800 | tf_op jit(solution)/shard_map/ppermute | solution.py:795
  90.4 0.2 collective-permute-start.18
  90.7 0.3 collective-permute-done.14
  91.0 1.5 %collective-permute-start.15 = (f32[96,256]{1,0:T(8,128)S(1)}, f32[96,256]{1,0:T(8,128)S(1)}, u32[]{:S(2)}, u32[]{:S(2)}) collective-permute-start(f32[96,256]{1,0:T(8,128)S(1)} %pad_maximum_fusion.8), channel_id=1, source_target_pairs={{0,4},{1,3},{2,6},{3,1},{4,0},{5,7},{6,2},{7,5},{8,12},{9,11},{10,... | collective-permute-start | bytes 294920 | tf_op jit(solution)/shard_map/ppermute | solution.py:795
  92.4 2.2 %collective-permute-done.18 = f32[48,256]{1,0:T(8,128)S(1)} collective-permute-done((f32[48,256]{1,0:T(8,128)S(1)}, f32[48,256]{1,0:T(8,128)S(1)}, u32[]{:S(2)}, u32[]{:S(2)}) %collective-permute-start.18) | collective-permute-done | bytes 49184 | tf_op jit(solution)/shard_map/ppermute | solution.py:795
  94.6 0.9 collective-permute-start.19
  95.5 1.2 %collective-permute-done.15 = f32[96,256]{1,0:T(8,128)S(1)} collective-permute-done((f32[96,256]{1,0:T(8,128)S(1)}, f32[96,256]{1,0:T(8,128)S(1)}, u32[]{:S(2)}, u32[]{:S(2)}) %collective-permute-start.15) | collective-permute-done | bytes 98336 | tf_op jit(solution)/shard_map/ppermute | solution.py:795
  96.7 1.5 %collective-permute-start.16 = (f32[192,256]{1,0:T(8,128)S(1)}, f32[192,256]{1,0:T(8,128)S(1)}, u32[]{:S(2)}, u32[]{:S(2)}) collective-permute-start(f32[192,256]{1,0:T(8,128)S(1)} %pad_maximum_fusion.5), channel_id=1, source_target_pairs={{0,2},{1,5},{2,0},{3,7},{4,6},{5,1},{6,4},{7,3},{8,10},{9,13},{10,... | collective-permute-start | bytes 589832 | tf_op jit(solution)/shard_map/ppermute | solution.py:795
  98.2 1.1 %collective-permute-done.19 = f32[96,256]{1,0:T(8,128)S(1)} collective-permute-done((f32[96,256]{1,0:T(8,128)S(1)}, f32[96,256]{1,0:T(8,128)S(1)}, u32[]{:S(2)}, u32[]{:S(2)}) %collective-permute-start.19) | collective-permute-done | bytes 98336 | tf_op jit(solution)/shard_map/ppermute | solution.py:795
  99.4 0.9 collective-permute-start.20
  100.3 2.2 %collective-permute-done.16 = f32[192,256]{1,0:T(8,128)S(1)} collective-permute-done((f32[192,256]{1,0:T(8,128)S(1)}, f32[192,256]{1,0:T(8,128)S(1)}, u32[]{:S(2)}, u32[]{:S(2)}) %collective-permute-start.16) | collective-permute-done | bytes 196640 | tf_op jit(solution)/shard_map/ppermute | solution.py:795
  102.5 0.1 collective-permute-start.17
  102.6 2.5 %collective-permute-done.20 = f32[192,256]{1,0:T(8,128)S(1)} collective-permute-done((f32[192,256]{1,0:T(8,128)S(1)}, f32[192,256]{1,0:T(8,128)S(1)}, u32[]{:S(2)}, u32[]{:S(2)}) %collective-permute-start.20) | collective-permute-done | bytes 196640 | tf_op jit(solution)/shard_map/ppermute | solution.py:795
  105.2 0.1 collective-permute-start.21
  105.2 0.7 finish.1
  105.9 0.1 broadcast_select_fusion.3
  106.0 0.1 pad_maximum_fusion
  106.0 0.9 collective-permute-done.21
  106.9 0.1 broadcast_select_fusion.1
  107.0 0.1 pad_maximum_fusion.1
  107.1 1.3 %maximum_multiply_fusion = f32[6,256,256]{2,1,0:T(8,128)} fusion(f32[6,128,256]{2,1,0:T(8,128)S(1)} %bitcast.38, f32[6,128,256]{2,1,0:T(8,128)S(1)} %bitcast.37, f32[256]{0:T(256)S(1)} %bitcast.27), kind=kLoop, calls=%fused_computation | loop fusion | flops 786432 | bytes 3146752 | tf_op jit(solution)/shard_map/mul | solution.py:833
  (56 shorter events, 0.6 us)
Async XLA Ops:
  9.4 15.4 %all-to-all-start = ((f32[32,4,128]{2,1,0:T(4,128)}), f32[32,4,128]{2,1,0:T(4,128)S(1)}, u32[]{:S(2)}, u32[]{:S(2)}) async-start(f32[32,4,128]{2,1,0:T(4,128)} %get-tuple-element.31), calls=%async_computation | async-start | bytes 131072 | tf_op jit(solution)/shard_map/all_to_all | solution.py:716
  16.8 1.0 copy-start.1
  18.4 3.5 %collective-permute-start = (f32[32,4,128]{2,1,0:T(4,128)S(1)}, f32[32,4,128]{2,1,0:T(4,128)S(1)}, u32[]{:S(2)}, u32[]{:S(2)}) collective-permute-start(f32[32,4,128]{2,1,0:T(4,128)S(1)} %get-tuple-element.34), channel_id=1, source_target_pairs={{0,1},{1,2},{2,3},{3,4},{4,5},{5,6},{6,7},{7,8},{8,9},{9,10},{10,1... | collective-permute-start | bytes 196616 | tf_op jit(solution)/shard_map/ppermute | solution.py:733
  20.6 4.3 %collective-permute-start.1 = (f32[32,4,128]{2,1,0:T(4,128)S(1)}, f32[32,4,128]{2,1,0:T(4,128)S(1)}, u32[]{:S(2)}, u32[]{:S(2)}) collective-permute-start(f32[32,4,128]{2,1,0:T(4,128)S(1)} %get-tuple-element.35), channel_id=1, source_target_pairs={{1,0},{2,1},{3,2},{4,3},{5,4},{6,5},{7,6},{8,7},{9,8},{10,9},{11,1... | collective-permute-start | bytes 196616 | tf_op jit(solution)/shard_map/ppermute | solution.py:734
  24.9 12.0 %copy-start.2 = (f32[4,32768]{1,0:T(4,128)S(1)}, f32[4,32768]{1,0:T(4,128)}, u32[]{:S(2)}) copy-start(f32[4,32768]{1,0:T(4,128)} %param.12) | copy-start | bytes 1572868
  27.7 16.0 %all-to-all-start.1 = ((f32[32,1,128]{2,1,0:T(1,128)}), f32[32,1,128]{2,1,0:T(1,128)S(1)}, u32[]{:S(2)}, u32[]{:S(2)}) async-start(f32[32,1,128]{2,1,0:T(1,128)} %get-tuple-element.39), calls=%async_computation.1 | async-start | bytes 32768 | tf_op jit(solution)/shard_map/all_to_all | solution.py:746
  36.8 6.9 %copy-start = (f32[6,256,256]{2,1,0:T(8,128)S(1)}, f32[6,256,256]{2,1,0:T(8,128)}, u32[]{:S(2)}) copy-start(f32[6,256,256]{2,1,0:T(8,128)} %weights_hbm.3) | copy-start | bytes 4718596
  36.9 6.9 %copy-start.3 = (s32[256,1]{0,1:T(1,128)S(1)}, s32[256,1]{0,1:T(1,128)}, u32[]{:S(2)}) copy-start(s32[256,1]{0,1:T(1,128)} %param.13) | copy-start | bytes 3076
  36.9 6.9 %copy-start.4 = (f32[256]{0:T(256)S(1)}, f32[256]{0:T(256)}, u32[]{:S(2)}) copy-start(f32[256]{0:T(256)} %param.17) | copy-start | bytes 3076
  36.9 6.9 %copy-start.5 = (f32[256]{0:T(256)S(1)}, f32[256]{0:T(256)}, u32[]{:S(2)}) copy-start(f32[256]{0:T(256)} %param.23) | copy-start | bytes 3076
  36.9 6.9 %copy-start.6 = (f32[256]{0:T(256)S(1)}, f32[256]{0:T(256)}, u32[]{:S(2)}) copy-start(f32[256]{0:T(256)} %param.18) | copy-start | bytes 3076
  36.9 6.9 %copy-start.7 = (f32[8,256]{1,0:T(8,128)S(1)}, f32[8,256]{1,0:T(8,128)}, u32[]{:S(2)}) copy-start(f32[8,256]{1,0:T(8,128)} %get-tuple-element.32.outputs_ref) | copy-start | bytes 24580
  57.0 1.8 %collective-permute-start.8 = (f32[384,256]{1,0:T(8,128)S(1)}, f32[384,256]{1,0:T(8,128)S(1)}, u32[]{:S(2)}, u32[]{:S(2)}) collective-permute-start(f32[384,256]{1,0:T(8,128)S(1)} %get-tuple-element.53), channel_id=1, source_target_pairs={{0,1},{1,0},{2,3},{3,2},{4,5},{5,4},{6,7},{7,6},{8,9},{9,8},{10,11... | collective-permute-start | bytes 1179656 | tf_op jit(solution)/shard_map/ppermute | solution.py:795
  57.1 2.4 %collective-permute-start.2 = (f32[392,256]{1,0:T(8,128)S(1)}, f32[392,256]{1,0:T(8,128)S(1)}, u32[]{:S(2)}, u32[]{:S(2)}) collective-permute-start(f32[392,256]{1,0:T(8,128)S(1)} %get-tuple-element.50), channel_id=1, source_target_pairs={{0,1},{1,0},{2,3},{3,2},{4,5},{5,4},{6,7},{7,6},{8,9},{9,8},{10,11... | collective-permute-start | bytes 1204232 | tf_op jit(solution)/shard_map/ppermute | solution.py:795
  58.9 5.7 %collective-permute-start.9 = (f32[192,256]{1,0:T(8,128)S(1)}, f32[192,256]{1,0:T(8,128)S(1)}, u32[]{:S(2)}, u32[]{:S(2)}) collective-permute-start(f32[192,256]{1,0:T(8,128)S(1)} %slice_select_fusion), channel_id=1, source_target_pairs={{0,2},{1,5},{2,0},{3,7},{4,6},{5,1},{6,4},{7,3},{8,10},{9,13},{10,... | collective-permute-start | bytes 589832 | tf_op jit(solution)/shard_map/ppermute | solution.py:795
  59.6 7.4 %collective-permute-start.3 = (f32[200,256]{1,0:T(8,128)S(1)}, f32[200,256]{1,0:T(8,128)S(1)}, u32[]{:S(2)}, u32[]{:S(2)}) collective-permute-start(f32[200,256]{1,0:T(8,128)S(1)} %pad_maximum_fusion.4), channel_id=1, source_target_pairs={{0,2},{1,5},{2,0},{3,7},{4,6},{5,1},{6,4},{7,3},{8,10},{9,13},{10,... | collective-permute-start | bytes 614408 | tf_op jit(solution)/shard_map/ppermute | solution.py:795
  64.7 4.7 %collective-permute-start.10 = (f32[96,256]{1,0:T(8,128)S(1)}, f32[96,256]{1,0:T(8,128)S(1)}, u32[]{:S(2)}, u32[]{:S(2)}) collective-permute-start(f32[96,256]{1,0:T(8,128)S(1)} %slice_select_fusion.2), channel_id=1, source_target_pairs={{0,4},{1,3},{2,6},{3,1},{4,0},{5,7},{6,2},{7,5},{8,12},{9,11},{10,... | collective-permute-start | bytes 294920 | tf_op jit(solution)/shard_map/ppermute | solution.py:795
  67.1 4.8 %collective-permute-start.4 = (f32[104,256]{1,0:T(8,128)S(1)}, f32[104,256]{1,0:T(8,128)S(1)}, u32[]{:S(2)}, u32[]{:S(2)}) collective-permute-start(f32[104,256]{1,0:T(8,128)S(1)} %pad_maximum_fusion.7), channel_id=1, source_target_pairs={{0,4},{1,3},{2,6},{3,1},{4,0},{5,7},{6,2},{7,5},{8,12},{9,11},{10,... | collective-permute-start | bytes 319496 | tf_op jit(solution)/shard_map/ppermute | solution.py:795
  69.4 4.2 %collective-permute-start.11 = (f32[48,256]{1,0:T(8,128)S(1)}, f32[48,256]{1,0:T(8,128)S(1)}, u32[]{:S(2)}, u32[]{:S(2)}) collective-permute-start(f32[48,256]{1,0:T(8,128)S(1)} %slice_select_fusion.4), channel_id=1, source_target_pairs={{0,8},{1,17},{2,10},{3,19},{4,12},{5,21},{6,14},{7,23},{8,0},{9,25... | collective-permute-start | bytes 147464 | tf_op jit(solution)/shard_map/ppermute | solution.py:795
  73.6 5.1 %collective-permute-start.12 = (f32[24,256]{1,0:T(8,128)S(1)}, f32[24,256]{1,0:T(8,128)S(1)}, u32[]{:S(2)}, u32[]{:S(2)}) collective-permute-start(f32[24,256]{1,0:T(8,128)S(1)} %slice_select_fusion.8), channel_id=1, source_target_pairs={{0,16},{1,9},{2,18},{3,11},{4,20},{5,13},{6,22},{7,15},{8,24},{9,1... | collective-permute-start | bytes 73736 | tf_op jit(solution)/shard_map/ppermute | solution.py:795
  74.3 5.0 %collective-permute-start.5 = (f32[56,256]{1,0:T(8,128)S(1)}, f32[56,256]{1,0:T(8,128)S(1)}, u32[]{:S(2)}, u32[]{:S(2)}) collective-permute-start(f32[56,256]{1,0:T(8,128)S(1)} %pad_maximum_fusion.10), channel_id=1, source_target_pairs={{0,8},{1,17},{2,10},{3,19},{4,12},{5,21},{6,14},{7,23},{8,0},{9,25... | collective-permute-start | bytes 172040 | tf_op jit(solution)/shard_map/ppermute | solution.py:795
  78.7 4.9 %collective-permute-start.13 = (f32[24,256]{1,0:T(8,128)S(1)}, f32[24,256]{1,0:T(8,128)S(1)}, u32[]{:S(2)}, u32[]{:S(2)}) collective-permute-start(f32[24,256]{1,0:T(8,128)S(1)} %select_add_fusion.3), channel_id=1, source_target_pairs={{0,16},{1,9},{2,18},{3,11},{4,20},{5,13},{6,22},{7,15},{8,24},{9,1... | collective-permute-start | bytes 73736 | tf_op jit(solution)/shard_map/ppermute | solution.py:795
  79.4 6.1 %collective-permute-start.6 = (f32[32,256]{1,0:T(8,128)S(1)}, f32[32,256]{1,0:T(8,128)S(1)}, u32[]{:S(2)}, u32[]{:S(2)}) collective-permute-start(f32[32,256]{1,0:T(8,128)S(1)} %pad_maximum_fusion.13), channel_id=1, source_target_pairs={{0,16},{1,9},{2,18},{3,11},{4,20},{5,13},{6,22},{7,15},{8,24},{9,1... | collective-permute-start | bytes 98312 | tf_op jit(solution)/shard_map/ppermute | solution.py:795
  85.5 4.9 %collective-permute-start.7 = (f32[32,256]{1,0:T(8,128)S(1)}, f32[32,256]{1,0:T(8,128)S(1)}, u32[]{:S(2)}, u32[]{:S(2)}) collective-permute-start(f32[32,256]{1,0:T(8,128)S(1)} %pad_maximum_fusion.14), channel_id=1, source_target_pairs={{0,16},{1,9},{2,18},{3,11},{4,20},{5,13},{6,22},{7,15},{8,24},{9,1... | collective-permute-start | bytes 98312 | tf_op jit(solution)/shard_map/ppermute | solution.py:795
  86.7 4.3 %collective-permute-start.14 = (f32[48,256]{1,0:T(8,128)S(1)}, f32[48,256]{1,0:T(8,128)S(1)}, u32[]{:S(2)}, u32[]{:S(2)}) collective-permute-start(f32[48,256]{1,0:T(8,128)S(1)} %pad_maximum_fusion.11), channel_id=1, source_target_pairs={{0,8},{1,17},{2,10},{3,19},{4,12},{5,21},{6,14},{7,23},{8,0},{9,25... | collective-permute-start | bytes 147464 | tf_op jit(solution)/shard_map/ppermute | solution.py:795
  90.4 4.2 %collective-permute-start.18 = (f32[48,256]{1,0:T(8,128)S(1)}, f32[48,256]{1,0:T(8,128)S(1)}, u32[]{:S(2)}, u32[]{:S(2)}) collective-permute-start(f32[48,256]{1,0:T(8,128)S(1)} %pad_maximum_fusion.12), channel_id=1, source_target_pairs={{0,8},{1,17},{2,10},{3,19},{4,12},{5,21},{6,14},{7,23},{8,0},{9,25... | collective-permute-start | bytes 147464 | tf_op jit(solution)/shard_map/ppermute | solution.py:795
  91.0 5.7 %collective-permute-start.15 = (f32[96,256]{1,0:T(8,128)S(1)}, f32[96,256]{1,0:T(8,128)S(1)}, u32[]{:S(2)}, u32[]{:S(2)}) collective-permute-start(f32[96,256]{1,0:T(8,128)S(1)} %pad_maximum_fusion.8), channel_id=1, source_target_pairs={{0,4},{1,3},{2,6},{3,1},{4,0},{5,7},{6,2},{7,5},{8,12},{9,11},{10,... | collective-permute-start | bytes 294920 | tf_op jit(solution)/shard_map/ppermute | solution.py:795
  94.6 4.7 %collective-permute-start.19 = (f32[96,256]{1,0:T(8,128)S(1)}, f32[96,256]{1,0:T(8,128)S(1)}, u32[]{:S(2)}, u32[]{:S(2)}) collective-permute-start(f32[96,256]{1,0:T(8,128)S(1)} %pad_maximum_fusion.9), channel_id=1, source_target_pairs={{0,4},{1,3},{2,6},{3,1},{4,0},{5,7},{6,2},{7,5},{8,12},{9,11},{10,... | collective-permute-start | bytes 294920 | tf_op jit(solution)/shard_map/ppermute | solution.py:795
  96.7 5.7 %collective-permute-start.16 = (f32[192,256]{1,0:T(8,128)S(1)}, f32[192,256]{1,0:T(8,128)S(1)}, u32[]{:S(2)}, u32[]{:S(2)}) collective-permute-start(f32[192,256]{1,0:T(8,128)S(1)} %pad_maximum_fusion.5), channel_id=1, source_target_pairs={{0,2},{1,5},{2,0},{3,7},{4,6},{5,1},{6,4},{7,3},{8,10},{9,13},{10,... | collective-permute-start | bytes 589832 | tf_op jit(solution)/shard_map/ppermute | solution.py:795
  99.4 5.7 %collective-permute-start.20 = (f32[192,256]{1,0:T(8,128)S(1)}, f32[192,256]{1,0:T(8,128)S(1)}, u32[]{:S(2)}, u32[]{:S(2)}) collective-permute-start(f32[192,256]{1,0:T(8,128)S(1)} %pad_maximum_fusion.6), channel_id=1, source_target_pairs={{0,2},{1,5},{2,0},{3,7},{4,6},{5,1},{6,4},{7,3},{8,10},{9,13},{10,... | collective-permute-start | bytes 589832 | tf_op jit(solution)/shard_map/ppermute | solution.py:795
  102.5 3.4 %collective-permute-start.17 = (f32[384,256]{1,0:T(8,128)S(1)}, f32[384,256]{1,0:T(8,128)S(1)}, u32[]{:S(2)}, u32[]{:S(2)}) collective-permute-start(f32[384,256]{1,0:T(8,128)S(1)} %pad_maximum_fusion.2), channel_id=1, source_target_pairs={{0,1},{1,0},{2,3},{3,2},{4,5},{5,4},{6,7},{7,6},{8,9},{9,8},{10,11... | collective-permute-start | bytes 1179656 | tf_op jit(solution)/shard_map/ppermute | solution.py:795
  105.2 1.8 %collective-permute-start.21 = (f32[384,256]{1,0:T(8,128)S(1)}, f32[384,256]{1,0:T(8,128)S(1)}, u32[]{:S(2)}, u32[]{:S(2)}) collective-permute-start(f32[384,256]{1,0:T(8,128)S(1)} %pad_maximum_fusion.3), channel_id=1, source_target_pairs={{0,1},{1,0},{2,3},{3,2},{4,5},{5,4},{6,7},{7,6},{8,9},{9,8},{10,11... | collective-permute-start | bytes 1179656 | tf_op jit(solution)/shard_map/ppermute | solution.py:795
